TPU v7x, 32 devices: a whole 2x2x4 slice. The times are simulated.
32 devices in a mesh: wt: 16 (over z, x, core), seq: 2 (over y).
Axes of the slice: x: 2, y: 2, z: 4, core: 2. Of those that a mesh axis runs over, the one named last changes fastest.
Arguments:
- tokens: bfloat16 [16, 1024, 1536], P('wt', 'seq'), may hold values from -6 to 6
- lengths: int32 [16], P('wt'), may hold values from 512 to 1024, as said below
- attn_gain: float32 [1536], P('wt'), may hold values from 0.5 to 1.5
- w_query: float32 [1536, 1536], P('wt'), may hold values from -0.15625 to 0.15625
- b_query: float32 [1536], P('wt'), may hold values from -3 to 3
- w_key: float32 [1536, 256], P('wt'), may hold values from -0.15625 to 0.15625
- b_key: float32 [256], P('wt'), may hold values from -3 to 3
- w_value: float32 [1536, 256], P('wt'), may hold values from -0.15625 to 0.15625
- b_value: float32 [256], P('wt'), may hold values from -0.6 to 0.6
- w_out: float32 [1536, 1536], P('wt'), may hold values from -0.625 to 0.625
- ffn_gain: float32 [1536], P('wt'), may hold values from 0.5 to 1.5
- w_gate: float32 [1536, 8960], P('wt'), may hold values from -0.15625 to 0.15625
- w_up: float32 [1536, 8960], P('wt'), may hold values from -0.15625 to 0.15625
- w_down: float32 [8960, 1536], P('wt'), may hold values from -0.0625 to 0.0625
- cotangent: bfloat16 [16, 1024, 1536], P('wt', 'seq'), may hold values from -6 to 6
Outputs:
- layer_out: bfloat16 [16, 1024, 1536], P('wt', 'seq')
- input_grad: bfloat16 [16, 1024, 1536], P('wt', 'seq')
- attn_gain_grad: float32 [1536], P('wt')
- w_query_grad: float32 [1536, 1536], P('wt')
- b_query_grad: float32 [1536], P('wt')
- w_key_grad: float32 [1536, 256], P('wt')
- b_key_grad: float32 [256], P('wt')
- w_value_grad: float32 [1536, 256], P('wt')
- b_value_grad: float32 [256], P('wt')
- w_out_grad: float32 [1536, 1536], P('wt')
- ffn_gain_grad: float32 [1536], P('wt')
- w_gate_grad: float32 [1536, 8960], P('wt')
- w_up_grad: float32 [1536, 8960], P('wt')
- w_down_grad: float32 [8960, 1536], P('wt')
Inputs may be any that keep to these rules, and one draw needn't show every extreme that they name: `lengths`: some slot has exactly 1024 valid tokens and some exactly 512.
All inputs are finite; a program needn't handle non-finite values.
Results may differ from a plain program's by a relative error of at most 0.028.
Values may be sent and summed in bfloat16 or wider, within the bound.
A program may use at most 384 MiB of HBM per device.

v0:
```python
import functools
import math

import jax
import jax.numpy as jnp
from jax import lax
from jax.experimental import pallas as pl
from jax.experimental.pallas import tpu as pltpu
from jax.sharding import PartitionSpec as P


HEADS = 12
KV_HEADS = 2
HEAD_DIM = 128
SLOT = 1024
INNER = 4
EXTRA = 8

epsilon = 1e-06
masked_score = -1e30
far_place = 1 << 30
scale = 1.0 / math.sqrt(HEAD_DIM)
low = jnp.bfloat16
full = jnp.float32


def product(left, right):
    return jnp.dot(left, right, preferred_element_type=full)


def product_left(left, right):
    return lax.dot_general(left, right, (((0,), (0,)), ((), ())), preferred_element_type=full)


def product_right(left, right):
    return lax.dot_general(left, right, (((1,), (1,)), ((), ())), preferred_element_type=full)


def norm_rows(values, gain):
    factor = lax.rsqrt(jnp.mean(values * values, axis=-1, keepdims=True) + epsilon)
    return (values * factor * gain, factor)


def norm_back(values, factor, gain, upstream):
    weighted = upstream * gain
    inner = jnp.mean(weighted * values, axis=-1, keepdims=True)
    grad_in = factor * weighted - values * (factor * factor * factor) * inner
    grad_gain = jnp.sum(upstream * values * factor, axis=0)
    return (grad_in, grad_gain)


def swap(value, hop):
    axis, bit = hop
    count = lax.axis_size(axis)
    return lax.ppermute(value, axis, [(i, i ^ bit) for i in range(count)])


def gather_hops(block, hops):
    held = block[None]
    for hop in hops:
        held = jnp.concatenate([held, swap(held, hop)], axis=0)
    return held


def reduce_hop(held, hop):
    half = held.shape[0] // 2
    other = swap(held[half:], hop)
    return (held[:half].astype(full) + other.astype(full)).astype(low)


def reduce_hops(held, hops):
    for hop in hops[:0:-1]:
        held = reduce_hop(held, hop)
    return held[0].astype(full) + swap(held[1], hops[0]).astype(full)


def bits_of(axis, count):
    found, bit = [], 1
    while bit < count:
        found.append((axis, bit))
        bit *= 2
    return found


def plane_hops(seq_count):
    inner = bits_of("wt", INNER)
    seq = bits_of("seq", seq_count)
    slow = inner[1:] + seq
    return (slow + inner[:1], slow[::-1] + inner[:1])


def rank_of(hops):
    place = jnp.int32(0)
    for k, (axis, bit) in enumerate(hops):
        here = (lax.axis_index(axis) // bit) % 2
        place = place + here * (1 << k)
    return place


def plane_order(hops, count):
    order = []
    for inner in range(INNER):
        for seq in range(count):
            place = 0
            for k, (axis, bit) in enumerate(hops):
                source = inner if axis == "wt" else seq
                place |= ((source // bit) % 2) << k
            order.append(place)
    return order


def gather_plane(block, seq_count):
    hops_a, hops_b = plane_hops(seq_count)
    half = block.shape[0] // 2
    part_a = gather_hops(block[:half], hops_a)
    part_b = gather_hops(block[half:], hops_b)
    return (part_a, part_b)


def to_place(stacked, place):
    return lax.dynamic_index_in_dim(stacked, place, 0, keepdims=False)


def flip(index, bit):
    return index + bit - 2 * bit * ((index // bit) % 2)


def flip_all(index, distance):
    bit = 1
    while bit <= distance:
        if distance & bit:
            index = flip(index, bit)
        bit *= 2
    return index


def inner_bits():
    return [bit for _, bit in bits_of("wt", INNER)]


def meet(peers):
    barrier = pltpu.get_barrier_semaphore()
    for peer in peers:
        pl.semaphore_signal(
            barrier, inc=1, device_id=peer, device_id_type=pl.DeviceIdType.MESH
        )
    pl.semaphore_wait(barrier, len(peers))


class Sender:
    def __init__(self, send_sems, recv_sems):
        self.sems = (send_sems, recv_sems)
        self.copies = []

    def start(self, source, target, peer):
        at = len(self.copies)
        copy = pltpu.make_async_remote_copy(
            src_ref=source,
            dst_ref=target,
            send_sem=self.sems[0].at[at],
            recv_sem=self.sems[1].at[at],
            device_id=peer,
            device_id_type=pl.DeviceIdType.MESH,
        )
        copy.start()
        self.copies.append(copy)
        return copy


def subsets(hops):
    found = [(0, 0)]
    for axis, bit in hops:
        more = [(a ^ bit, b) if axis == "wt" else (a, b ^ bit) for a, b in found]
        found = found + more
    return found


def plane_copies(seq_count):
    hops_a, _ = plane_hops(seq_count)
    slow = len(hops_a) - 1
    return (2 * (2**slow - 1), len(set(a for a, _ in subsets(hops_a[:-1]))))


def gather_kernel(
    outer, seq_count, x_ref, p_ref, wo_ref, s_ref, cos_ref, sin_ref,
    normed_ref, qkv_ref, vec_ref, head_ref, out_ref,
    w_scr, o_scr, s_scr, send_sems, recv_sems, local_sems,
):
    share, head_width = p_ref.shape
    width = x_ref.shape[1]
    wt, seq = lax.axis_index("wt"), lax.axis_index("seq")
    line, inner = wt // INNER, wt % INNER
    hops = plane_hops(seq_count)
    slow = len(hops[0]) - 1
    peers = [(flip_all(line, d) * INNER + inner, seq) for d in range(1, outer)]
    peers += [(wt - inner + flip(inner, bit), seq) for bit in inner_bits()]
    peers += [(wt, flip(seq, bit)) for _, bit in bits_of("seq", seq_count)]

    def own_columns(total):
        wide = total // seq_count
        return pl.ds(pl.multiple_of(seq * wide, 128), wide)

    fill = [
        pltpu.make_async_copy(
            ref.at[:, own_columns(ref.shape[1])],
            scratch.at[line, inner, :, own_columns(ref.shape[1])],
            local_sems.at[k],
        )
        for k, (ref, scratch) in enumerate(((p_ref, w_scr), (wo_ref, o_scr)))
    ] + [
        pltpu.make_async_copy(s_ref, s_scr.at[line, inner], local_sems.at[2]),
    ]
    for copy in fill:
        copy.start()
    meet(peers)
    out = Sender(send_sems, recv_sems)

    def hop_peer(hop):
        axis, bit = hop
        if axis == "wt":
            return (wt - inner + flip(inner, bit), seq)
        return (wt, flip(seq, bit))

    def columns(total, part, half):
        wide = total // seq_count
        first = -(-wide // 256) * 128
        start = part * wide + half * first
        return pl.ds(pl.multiple_of(start, 128), wide - first if half else first)

    def start_line(source, scratch, narrow):
        total = source.shape[1]
        copies = [None]
        for d in range(1, outer):
            if narrow:
                part = own_columns(total)
                pair = (source.at[:, part], scratch.at[line, inner, :, part])
            else:
                pair = (source, scratch.at[line, inner])
            copies.append(out.start(*pair, (flip_all(line, d) * INNER + inner, seq)))
        return copies

    small_line = start_line(s_ref, s_scr, False)
    head_line = start_line(p_ref, w_scr, True)
    out_line = start_line(wo_ref, o_scr, True)

    def start_stage(scratch, at, stage):
        total = scratch.shape[-1]
        copies = []
        if stage < slow:
            for half in range(2):
                hop = hops[half][stage]
                for a, b in subsets(hops[half][:stage]):
                    place = scratch.at[
                        at, flip_all(inner, a), :, columns(total, flip_all(seq, b), half)
                    ]
                    copies.append(out.start(place, place, hop_peer(hop)))
            return copies
        for a in sorted(set(a for a, _ in subsets(hops[0][:slow]))):
            place = scratch.at[at, flip_all(inner, a)]
            copies.append(out.start(place, place, hop_peer(hops[0][slow])))
        return copies

    def arrive(copies):
        for copy in copies:
            if copy is not None:
                copy.wait_recv()

    for copy in fill:
        copy.wait()
    waiting = [[copy] for copy in head_line]
    small_wait = small_line
    for step in range(outer + slow + 1):
        for stage in range(slow + 1):
            d = step - stage
            if 0 <= d < outer:
                arrive(waiting[d])
                waiting[d] = start_stage(w_scr, flip_all(line, d), stage)
        if step == 0:
            arrive(small_wait)
            small_wait = []
        if step < len(inner_bits()):
            arrive(small_wait)
            bit = inner_bits()[::-1][step]
            small_wait = []
            for a, _ in subsets([("wt", b) for b in inner_bits()[::-1][:step]]):
                place = s_scr.at[:, flip_all(inner, a)]
                small_wait.append(out.start(place, place, hop_peer(("wt", bit))))
    arrive(small_wait)
    arrive(out_line)
    out_wait = start_stage(o_scr, slice(None), 0)

    count = outer * INNER
    bias_k = share * KV_HEADS * HEAD_DIM // (HEADS * HEAD_DIM)
    query_width = HEADS * HEAD_DIM
    pair_width = KV_HEADS * HEAD_DIM
    vec_ref[...] = jnp.zeros_like(vec_ref)
    for k in range(count):
        small = s_scr[k // INNER, k % INNER].astype(full)
        at = k * share
        vec_ref[0:1, at : at + share] = small[0:1, :share]
        vec_ref[1:2, at : at + share] = small[1:2, :share]
        at = query_width + k * bias_k
        vec_ref[1:2, at : at + bias_k] = small[2:3, :bias_k]
        at = query_width + pair_width + k * bias_k
        vec_ref[1:2, at : at + bias_k] = small[3:4, :bias_k]
        at = k * share
        vec_ref[2:3, at : at + share] = small[4:5, :share]

    values = x_ref[...].astype(full)
    factor = lax.rsqrt(jnp.mean(values * values, axis=-1, keepdims=True) + epsilon)
    normed_ref[...] = (values * factor * vec_ref[0:1, :width]).astype(low)
    for d in range(outer):
        arrive(waiting[d])
    keep_head = pltpu.make_async_copy(w_scr, head_ref, local_sems.at[0])
    keep_head.start()
    wide = 2 * HEAD_DIM
    blocks = head_width // wide

    def project(at):
        weights = w_scr[:, :, :, pl.ds(at, wide)].reshape(width, wide)
        return (
            jnp.dot(normed_ref[...], weights, preferred_element_type=full)
            + vec_ref[1:2, pl.ds(at, wide)]
        )

    def turn_block(k):
        at = pl.multiple_of(k * wide, wide)
        got = project(at)
        for j in range(2):
            part = got[:, j * HEAD_DIM : (j + 1) * HEAD_DIM]
            turned = part * cos_ref[...] + pltpu.roll(part, HEAD_DIM // 2, 1) * sin_ref[...]
            where = pl.multiple_of(at + j * HEAD_DIM, HEAD_DIM)
            qkv_ref[:, pl.ds(where, HEAD_DIM)] = turned.astype(low)

    turned_blocks = blocks - pair_width // wide
    marks = [turned_blocks * (k + 1) // (slow + 1) for k in range(slow + 1)]
    begin = 0
    for stage in range(slow + 1):
        @pl.loop(begin, marks[stage])
        def _(k):
            turn_block(k)

        begin = marks[stage]
        arrive(out_wait)
        out_wait = start_stage(o_scr, slice(None), stage + 1) if stage < slow else []
    for k in range(turned_blocks, blocks):
        qkv_ref[:, k * wide : (k + 1) * wide] = project(k * wide).astype(low)
    keep_out = pltpu.make_async_copy(o_scr, out_ref, local_sems.at[1])
    keep_out.start()
    for copy in out.copies:
        copy.wait_send()
    keep_head.wait()
    keep_out.wait()


def gather_project(tokens, packed, w_out, small, cosine, sine):
    outer = lax.axis_size("wt") // INNER
    seq_count = lax.axis_size("seq")
    rows, width = tokens.shape
    share, head_width = packed.shape
    slow_copies, last_copies = plane_copies(seq_count)
    each = slow_copies + last_copies
    small_copies = 2 ** len(inner_bits()) - 1
    copies = 3 * (outer - 1) + (outer + 1) * each + small_copies
    vmem = pl.BlockSpec(memory_space=pltpu.VMEM)
    anywhere = pl.BlockSpec(memory_space=pl.ANY)
    sent = 2 * outer * INNER * share * (head_width + w_out.shape[1])
    return pl.pallas_call(
        functools.partial(gather_kernel, outer, seq_count),
        in_specs=[vmem] * 6,
        out_specs=[vmem, vmem, vmem, anywhere, anywhere],
        out_shape=[
            jax.ShapeDtypeStruct((rows, width), low),
            jax.ShapeDtypeStruct((rows, head_width), low),
            jax.ShapeDtypeStruct((8, head_width), full),
            jax.ShapeDtypeStruct((outer, INNER, share, head_width), low),
            jax.ShapeDtypeStruct((outer, INNER, share, w_out.shape[1]), low),
        ],
        scratch_shapes=[
            pltpu.VMEM((outer, INNER, share, head_width), low),
            pltpu.VMEM((outer, INNER, share, w_out.shape[1]), low),
            pltpu.VMEM((outer, INNER, small.shape[0], small.shape[1]), low),
            pltpu.SemaphoreType.DMA((copies,)),
            pltpu.SemaphoreType.DMA((copies,)),
            pltpu.SemaphoreType.DMA((3,)),
        ],
        compiler_params=pltpu.CompilerParams(
            collective_id=1, has_side_effects=True, vmem_limit_bytes=48 << 20
        ),
        cost_estimate=pl.CostEstimate(
            flops=2 * rows * width * head_width * 8, bytes_accessed=2 * sent, transcendentals=0
        ),
        name="gather_project",
    )(tokens, packed, w_out, small, cosine, sine)


def split_kernel(outer, seq_count, own, info_ref, gate_ref, up_ref, o_ref):
    inner = info_ref[1]
    width = outer * own
    padded = o_ref.shape[2] // 2
    for s in range(seq_count):
        @pl.when(info_ref[0] == s)
        def _():
            for q in range(INNER):
                place = jnp.bitwise_xor(inner, q)
                for k, ref in enumerate((gate_ref, up_ref)):
                    for o in range(outer):
                        at = ((o * INNER + q) * seq_count + s) * own
                        to = k * padded + o * own
                        o_ref[place, :, to : to + own] = ref[:, at : at + own].astype(low)
                    if padded > width:
                        blank = jnp.zeros((o_ref.shape[1], padded - width), low)
                        o_ref[place, :, k * padded + width : (k + 1) * padded] = blank


def split_units(info, gate, up, outer, seq_count, own, padded):
    vmem = pl.BlockSpec(memory_space=pltpu.VMEM)
    return pl.pallas_call(
        functools.partial(split_kernel, outer, seq_count, own),
        in_specs=[pl.BlockSpec(memory_space=pltpu.SMEM), vmem, vmem],
        out_specs=vmem,
        out_shape=jax.ShapeDtypeStruct((INNER, gate.shape[0], 2 * padded), low),
        name="split_units",
    )(info, gate, up)


def join_kernel(outer, seq_count, own, info_ref, u_ref, gate_ref, up_ref):
    seq, inner = info_ref[0], info_ref[1]
    padded = u_ref.shape[3] // 2
    for s in range(seq_count):
        for q in range(INNER):
            block = u_ref[jnp.bitwise_xor(seq, s), jnp.bitwise_xor(inner, q)].astype(full)
            for k, ref in enumerate((gate_ref, up_ref)):
                for o in range(outer):
                    at = ((o * INNER + q) * seq_count + s) * own
                    source = k * padded + o * own
                    ref[:, at : at + own] = block[:, source : source + own]


def join_units(info, units, outer, own):
    seq_count, _, rows, _ = units.shape
    vmem = pl.BlockSpec(memory_space=pltpu.VMEM)
    shape = jax.ShapeDtypeStruct((rows, outer * INNER * seq_count * own), full)
    return pl.pallas_call(
        functools.partial(join_kernel, outer, seq_count, own),
        in_specs=[pl.BlockSpec(memory_space=pltpu.SMEM), vmem],
        out_specs=[vmem, vmem],
        out_shape=[shape, shape],
        name="join_units",
    )(info, units)


def after(value, *others):
    return lax.optimization_barrier((value, *others))[0]


def shown(kpos_ref, rows, keys):
    places = lax.broadcasted_iota(jnp.int32, (rows, keys), 0)
    return kpos_ref[...] <= places


def fwd_kernel(kpos_ref, q_ref, k_ref, v_ref, o_ref):
    rows, keys = q_ref.shape[0], k_ref.shape[0]
    scores = (
        lax.dot_general(
            q_ref[...], k_ref[...], (((1,), (1,)), ((), ())), preferred_element_type=full
        )
        * scale
    )
    scores = jnp.where(shown(kpos_ref, rows, keys), scores, masked_score)
    top = jnp.max(scores, axis=-1, keepdims=True)
    weights = jnp.exp(scores - top)
    total = jnp.sum(weights, axis=-1, keepdims=True)
    probs = (weights * (1.0 / total)).astype(low)
    o_ref[...] = jnp.dot(probs, v_ref[...], preferred_element_type=full).astype(low)


def attend_forward(kpos, qkv, pairs):
    rows = qkv.shape[0]
    keys = pairs.shape[0]
    group = HEADS // KV_HEADS
    return pl.pallas_call(
        fwd_kernel,
        grid=(HEADS,),
        in_specs=[
            pl.BlockSpec((1, keys), lambda h: (0, 0)),
            pl.BlockSpec((rows, HEAD_DIM), lambda h: (0, h)),
            pl.BlockSpec((keys, HEAD_DIM), lambda h: (0, h // group)),
            pl.BlockSpec((keys, HEAD_DIM), lambda h: (0, KV_HEADS + h // group)),
        ],
        out_specs=pl.BlockSpec((rows, HEAD_DIM), lambda h: (0, h)),
        out_shape=jax.ShapeDtypeStruct((rows, HEADS * HEAD_DIM), low),
        cost_estimate=pl.CostEstimate(
            flops=4 * rows * keys * HEADS * HEAD_DIM * 3,
            bytes_accessed=4 * rows * HEADS * HEAD_DIM + 4 * keys * KV_HEADS * HEAD_DIM,
            transcendentals=rows * keys * HEADS,
        ),
        name="attend_forward",
    )(kpos, qkv, pairs, pairs)


def bwd_kernel(kpos_ref, cos_ref, sin_ref, q_ref, k_ref, v_ref, g_ref, dq_ref, dk_ref, dv_ref):
    rows, keys = q_ref.shape[0], k_ref.shape[0]
    group = HEADS // KV_HEADS
    head = pl.program_id(0)
    queries, key, value, grad = q_ref[...], k_ref[...], v_ref[...], g_ref[...]
    scores = (
        lax.dot_general(queries, key, (((1,), (1,)), ((), ())), preferred_element_type=full)
        * scale
    )
    scores = jnp.where(shown(kpos_ref, rows, keys), scores, masked_score)
    top = jnp.max(scores, axis=-1, keepdims=True)
    weights = jnp.exp(scores - top)
    total = jnp.sum(weights, axis=-1, keepdims=True)
    probs = weights * (1.0 / total)
    prob_grad = lax.dot_general(
        grad, value, (((1,), (1,)), ((), ())), preferred_element_type=full
    )
    inner = jnp.sum(probs * prob_grad, axis=-1, keepdims=True)
    score_grad = (probs * (prob_grad - inner)).astype(low)
    dv = lax.dot_general(
        probs.astype(low), grad, (((0,), (0,)), ((), ())), preferred_element_type=full
    )
    dk = (
        lax.dot_general(
            score_grad, queries, (((0,), (0,)), ((), ())), preferred_element_type=full
        )
        * scale
    )
    dq = jnp.dot(score_grad, key, preferred_element_type=full) * scale
    turned = dq * cos_ref[...] - pltpu.roll(dq, HEAD_DIM // 2, 1) * sin_ref[...]
    dq_ref[...] = turned.astype(low)

    @pl.when(head % group == 0)
    def _():
        dk_ref[...] = dk
        dv_ref[...] = dv

    @pl.when(head % group != 0)
    def _():
        dk_ref[...] += dk
        dv_ref[...] += dv


def attend_backward(kpos, cosine, sine, qkv, pairs, grad):
    rows = qkv.shape[0]
    keys = pairs.shape[0]
    group = HEADS // KV_HEADS
    width = KV_HEADS * HEAD_DIM
    return pl.pallas_call(
        bwd_kernel,
        grid=(HEADS,),
        in_specs=[
            pl.BlockSpec((1, keys), lambda h: (0, 0)),
            pl.BlockSpec((rows, HEAD_DIM), lambda h: (0, 0)),
            pl.BlockSpec((rows, HEAD_DIM), lambda h: (0, 0)),
            pl.BlockSpec((rows, HEAD_DIM), lambda h: (0, h)),
            pl.BlockSpec((keys, HEAD_DIM), lambda h: (0, h // group)),
            pl.BlockSpec((keys, HEAD_DIM), lambda h: (0, KV_HEADS + h // group)),
            pl.BlockSpec((rows, HEAD_DIM), lambda h: (0, h)),
        ],
        out_specs=[
            pl.BlockSpec((rows, HEAD_DIM), lambda h: (0, h)),
            pl.BlockSpec((keys, HEAD_DIM), lambda h: (0, h // group)),
            pl.BlockSpec((keys, HEAD_DIM), lambda h: (0, h // group)),
        ],
        out_shape=[
            jax.ShapeDtypeStruct((rows, HEADS * HEAD_DIM), low),
            jax.ShapeDtypeStruct((keys, width), full),
            jax.ShapeDtypeStruct((keys, width), full),
        ],
        cost_estimate=pl.CostEstimate(
            flops=10 * rows * keys * HEADS * HEAD_DIM * 3,
            bytes_accessed=8 * rows * HEADS * HEAD_DIM + 12 * keys * width,
            transcendentals=rows * keys * HEADS,
        ),
        name="attend_backward",
    )(kpos, cosine, sine, qkv, pairs, pairs, grad)


def body(
    tokens, lengths, attn_gain, w_query, b_query, w_key, b_key, w_value, b_value, w_out,
    ffn_gain, w_gate, w_up, w_down, cotangent,
):
    slot_count, rows, width = tokens.shape
    seq_count = lax.axis_size("seq")
    wt_count = lax.axis_size("wt")
    outer = wt_count // INNER
    seq_here = lax.axis_index("seq")
    inner_here = lax.axis_index("wt") % INNER
    line = [[o * INNER + i for o in range(outer)] for i in range(INNER)]
    hops_a, hops_b = plane_hops(seq_count)
    plane = INNER * seq_count
    share = w_query.shape[0]
    bias_q, bias_k = b_query.shape[0], b_key.shape[0]
    query_width = HEADS * HEAD_DIM
    pair_width = KV_HEADS * HEAD_DIM
    head_width = query_width + 2 * pair_width
    ff_own = w_down.shape[0] // seq_count
    ff_here = outer * ff_own
    ff_pad = -(-ff_here // 128) * 128

    flat = tokens.astype(full).reshape(rows, width)
    places = seq_here * rows + jnp.arange(rows, dtype=jnp.int32)
    keep = (places < lengths[0])[:, None]
    upstream_low = jnp.where(keep, cotangent.reshape(rows, width), jnp.zeros((), low))

    def line_gather(value):
        return lax.all_gather(value, "wt", axis=0, axis_index_groups=line, tiled=False)

    def line_reduce(value):
        return lax.psum_scatter(
            value, "wt", scatter_dimension=0, axis_index_groups=line, tiled=False
        )

    def reduce_weight(value):
        count, wide = value.shape[1:]
        half = wide // seq_count // 2
        split = value.reshape(outer, INNER, count, seq_count, 2, half)
        done = []
        for k, hops in enumerate((hops_a, hops_b)):
            piece = split[:, :, :, :, k].transpose(1, 3, 0, 2, 4)
            piece = piece.reshape(plane, outer, count, half)
            order = plane_order(hops, seq_count)
            back = [order.index(p) for p in range(plane)]
            table = jnp.asarray(back, dtype=jnp.int32)
            me = rank_of(hops)
            placed = [to_place(piece, table[me ^ p]) for p in range(plane)]
            done.append(reduce_hops(jnp.stack(placed), hops))
        lined = jnp.concatenate(done, axis=-1).astype(low)
        mine = line_reduce(lined)
        return seq_columns(mine)

    def seq_gather(value):
        stacked = gather_hops(value, bits_of("seq", seq_count))
        return jnp.stack([to_place(stacked, seq_here ^ p) for p in range(seq_count)])

    def seq_columns(value):
        got = seq_gather(value)
        return got.transpose(1, 0, 2).reshape(value.shape[0], -1)

    info = jnp.stack([seq_here, inner_here]).astype(jnp.int32)
    down_own = lax.dynamic_slice_in_dim(w_down, seq_here * ff_own, ff_own, axis=0).astype(low)
    down_w = line_gather(down_own).reshape(ff_here, width)

    def inner_swap(value, distance):
        count = lax.axis_size("wt")
        return lax.ppermute(value, "wt", [(i, i ^ distance) for i in range(count)])

    def inner_exchange(value):
        got = [value[0]] + [inner_swap(value[d], d) for d in range(1, INNER)]
        return jnp.stack(got)

    stacked = inner_exchange(split_units(info, w_gate, w_up, outer, seq_count, ff_own, ff_pad))
    block = jnp.stack([to_place(stacked, inner_here ^ p) for p in range(INNER)])
    block = block.reshape(INNER * share, 2 * ff_pad)
    units_w = line_gather(block).reshape(width, 2 * ff_pad)
    down_w = jnp.pad(down_w, ((0, ff_pad - ff_here), (0, 0)))

    bias_q, bias_k = b_query.shape[0], b_key.shape[0]
    half = HEAD_DIM // 2
    inverse = 10000.0 ** (-jnp.arange(half, dtype=full) / half)
    angle = places.astype(full)[:, None] * inverse[None, :]
    cosine = jnp.cos(angle)
    sine = jnp.sin(angle)
    cosine = jnp.concatenate([cosine, cosine], axis=1)
    sine = jnp.concatenate([-sine, sine], axis=1)

    def line_of(vector):
        return jnp.pad(vector, (0, HEAD_DIM - vector.shape[0]))

    small = jnp.stack([line_of(v) for v in (attn_gain, b_query, b_key, b_value, ffn_gain)])
    small = jnp.pad(small.astype(low), ((0, 11), (0, 0)))
    packed = jnp.concatenate([w_query, w_key, w_value], axis=1).astype(low)
    normed_low, qkv, vectors, head_all, out_all = gather_project(
        after(tokens, block, down_own).reshape(rows, width),
        packed, w_out.astype(low), small, cosine, sine,
    )
    head_w = head_all.reshape(width, head_width)
    out_w = out_all.reshape(query_width, width)
    gain_one = vectors[0, :width]
    gain_two = vectors[2, :width]

    seq_hops = bits_of("seq", seq_count)
    pairs = gather_hops(qkv[:, query_width:], seq_hops).reshape(SLOT, 2 * pair_width)
    distance = jnp.arange(SLOT, dtype=jnp.int32)
    key_place = (seq_here ^ (distance // rows)) * rows + distance % rows
    kpos = jnp.where(key_place < lengths[0], key_place - seq_here * rows, far_place)[None, :]
    mixed = attend_forward(kpos, qkv, pairs)
    resid = flat + product(mixed, out_w)
    normed_two, factor_two = norm_rows(resid, gain_two)
    normed_two_low = normed_two.astype(low)

    def spread(block):
        part_a, part_b = gather_plane(block, seq_count)
        return jnp.stack([part_a, part_b]).reshape(plane * rows, width)

    def halves(partial):
        return list(partial.astype(low).reshape(2, plane, rows // 2, width))

    def hop_halves(parts, stage):
        return [reduce_hop(part, hops[stage]) for part, hops in zip(parts, (hops_a, hops_b))]

    def last_halves(parts):
        got = [reduce_hops(part, hops[:1]) for part, hops in zip(parts, (hops_a, hops_b))]
        return jnp.concatenate(got, axis=0)

    stages = list(range(len(hops_a)))[:0:-1]
    grad_all = spread(after(upstream_low, vectors))
    hidden_grad = product_right(grad_all, down_w)
    rows_all = spread(normed_two_low)
    both = product(rows_all, units_w)
    gate, upper = both[:, :ff_pad], both[:, ff_pad:]
    sigma = jax.nn.sigmoid(gate)
    hidden = (gate * sigma * upper).astype(low)
    gate_grad = (hidden_grad * upper * sigma * (1.0 + gate * (1.0 - sigma))).astype(low)
    up_grad = (hidden_grad * gate * sigma).astype(low)
    units_grad = jnp.concatenate([gate_grad, up_grad], axis=1)
    back = halves(product_right(units_grad, units_w))
    down_grad = product_left(after(hidden, back[0]), grad_all).astype(low)[:ff_here]
    down_line = line_reduce(down_grad.reshape(outer, ff_own, width))
    back = hop_halves(back, stages[0])
    rows_late, grad_late = lax.optimization_barrier((rows_all, units_grad, back, down_grad))[:2]
    units_w_grad = product_left(rows_late, grad_late).astype(low)
    units_line = line_reduce(units_w_grad.reshape(outer, INNER * share, 2 * ff_pad))
    for stage in stages[1:]:
        back = hop_halves(back, stage)
    hidden_late = after(hidden, back, units_w_grad)
    forth = halves(product(hidden_late, down_w))
    normed_two_grad = last_halves(back)
    forth[0] = after(forth[0], normed_two_grad)
    for stage in stages:
        forth = hop_halves(forth, stage)
    result = resid + last_halves(forth)
    layer_out = jnp.where(keep, result, 0.0).astype(low).reshape(slot_count, rows, width)

    blocks = units_line.reshape(INNER, share, 2 * ff_pad)
    sent = jnp.stack([to_place(blocks, inner_here ^ d) for d in range(INNER)])
    gate_out, up_out = join_units(
        info, gather_hops(inner_exchange(sent), seq_hops), outer, ff_own
    )
    down_out = seq_gather(down_line).reshape(seq_count * ff_own, width).astype(full)

    upstream = upstream_low.astype(full)
    resid_norm_grad, gain_two_grad = norm_back(resid, factor_two, gain_two, normed_two_grad)
    resid_grad = upstream + resid_norm_grad
    attn_grad = resid_grad.astype(low)
    mixed_grad = product_right(attn_grad, out_w).astype(low)
    out_w_grad = product_left(mixed, attn_grad).astype(low)
    out_w_out = reduce_weight(out_w_grad.reshape(wt_count, -1, width)).astype(full)
    query_grad, key_part, value_part = attend_backward(
        kpos, cosine, sine, qkv, pairs, mixed_grad
    )
    pair_part = jnp.concatenate([key_part, value_part], axis=1)
    pair_sum = reduce_hops(
        pair_part.reshape(seq_count, rows, 2 * pair_width).astype(low), seq_hops
    )
    key_rot_grad = pair_sum[:, :pair_width].reshape(rows, KV_HEADS, HEAD_DIM)
    turned = jnp.concatenate([key_rot_grad[..., half:], key_rot_grad[..., :half]], axis=-1)
    key_grad = key_rot_grad * cosine[:, None, :] - turned * sine[:, None, :]
    head_grad = jnp.concatenate(
        [query_grad, key_grad.reshape(rows, pair_width).astype(low),
         pair_sum[:, pair_width:].astype(low)],
        axis=1,
    )
    head_w_grad = product_left(normed_low, head_grad).astype(low)
    head_b_grad = jnp.sum(head_grad.astype(full), axis=0)
    normed_grad = product_right(head_grad, head_w)
    factor_one = lax.rsqrt(jnp.mean(flat * flat, axis=-1, keepdims=True) + epsilon)
    input_norm_grad, gain_one_grad = norm_back(flat, factor_one, gain_one, normed_grad)
    input_grad = (resid_grad + input_norm_grad).astype(low).reshape(slot_count, rows, width)

    edges = [0, share, share + bias_q]
    edges += [edges[-1] + bias_k, edges[-1] + 2 * bias_k]

    def parts(vector):
        return vector.reshape(wt_count, -1)

    small_grad = jnp.concatenate(
        [
            parts(gain_one_grad),
            parts(head_b_grad[:query_width]),
            parts(head_b_grad[query_width : query_width + pair_width]),
            parts(head_b_grad[query_width + pair_width :]),
            parts(gain_two_grad),
        ],
        axis=1,
    ).astype(low)
    extra = jnp.pad(
        small_grad[:, None, :],
        ((0, 0), (0, EXTRA - 1), (0, head_width - small_grad.shape[1])),
    )
    head_sum = reduce_weight(
        jnp.concatenate([head_w_grad.reshape(wt_count, share, head_width), extra], axis=1)
    ).astype(full)
    heads_out = head_sum[:share]
    small_out = head_sum[share]
    return (
        layer_out,
        input_grad,
        small_out[: edges[1]],
        heads_out[:, :query_width],
        small_out[edges[1] : edges[2]],
        heads_out[:, query_width : query_width + pair_width],
        small_out[edges[2] : edges[3]],
        heads_out[:, query_width + pair_width :],
        small_out[edges[3] : edges[4]],
        out_w_out,
        small_out[edges[4] : edges[4] + ffn_gain.shape[0]],
        gate_out,
        up_out,
        down_out,
    )


def solution(mesh):
    by_wt = P("wt")
    by_row = P("wt", None)
    by_token = P("wt", "seq", None)
    return jax.shard_map(
        body,
        mesh=mesh,
        in_specs=(
            by_token, by_wt, by_wt, by_row, by_wt, by_row, by_wt, by_row, by_wt, by_row,
            by_wt, by_row, by_row, by_row, by_token,
        ),
        out_specs=(
            by_token, by_token, by_wt, by_row, by_wt, by_row, by_wt, by_row, by_wt, by_row,
            by_wt, by_row, by_row, by_row,
        ),
        check_vma=False,
    )
```

profile of v0, /device:TPU:0, one launch (start us, length us, event | category | flops | bytes accessed | tf_op | source)
XLA Modules:
  0.0 958.2 jit_solution(11017489172670383009)
XLA Ops:
  7.9 5.3 split_units.1
  30.2 9.1 collective-permute-done.9
  43.1 80.5 %gather_project.1 = (bf16[512,1536]{1,0:T(8,128)(2,1)S(1)}, bf16[512,2048]{1,0:T(8,128)(2,1)}, f32[8,2048]{1,0:T(8,128)S(1)}, bf16[4,4,96,2048]{3,2,1,0:T(8,128)(2,1)}, bf16[4,4,96,1536]{3,2,1,0:T(8,128)(2,1)}) custom-call(bf16[512,1536]{1,0:T(8,128)(2,1)S(1)} %bitcast.232, bf16[96,2048]{1,0:T(8,128)(2,1)S(1)} %pad_maximum_fusion.25.p_ref, ...), custom_call_target="tpu_custom_call" | custom-call | flops 25769803776 | bytes 22020096 | tf_op jit(solution)/shard_map/gather_project/pallas_call | solution.py:368
  132.1 6.3 collective-permute-done
  139.4 22.7 %attend_forward.1 = bf16[512,1536]{1,0:T(8,128)(2,1)} custom-call(s32[1,1024]{1,0:T(1,128)} %compare_select_fusion.kpos_ref, bf16[512,2048]{1,0:T(8,128)(2,1)} %get-tuple-element.31.q_ref, bf16[1024,512]{1,0:T(8,128)(2,1)} %bitcast.256, bf16[1024,512]{1,0:T(8,128)(2,1)} %bitcast.257), custom_call_target="tpu_custom_call" | custom-call | flops 9663676416 | bytes 4194304 | tf_op jit(solution)/shard_map/attend_forward/pallas_call | solution.py:482
  162.1 5.1 multiply_reduce_fusion.2
  175.9 29.0 %collective-permute-done.11 = bf16[2,256,1536]{2,1,0:T(8,128)(2,1)S(1)} collective-permute-done((bf16[2,256,1536]{2,1,0:T(8,128)(2,1)S(1)}, bf16[2,256,1536]{2,1,0:T(8,128)(2,1)S(1)}, u32[]{:S(2)}, u32[]{:S(2)}) %collective-permute-start.11) | collective-permute-done | bytes 1572896 | tf_op jit(solution)/shard_map/ppermute | solution.py:55
  204.9 3.9 pad_maximum_fusion.6
  208.8 4.8 collective-permute-start.12
  213.5 12.1 %collective-permute-done.1 = bf16[1,256,1536]{2,1,0:T(8,128)(2,1)S(1)} collective-permute-done((bf16[1,256,1536]{2,1,0:T(8,128)(2,1)S(1)}, bf16[1,256,1536]{2,1,0:T(8,128)(2,1)S(1)}, u32[]{:S(2)}, u32[]{:S(2)}) %collective-permute-start.1) | collective-permute-done | bytes 786464 | tf_op jit(solution)/shard_map/ppermute | solution.py:55
  225.9 3.8 pad_maximum_fusion.7
  234.6 27.7 %collective-permute-done.2 = bf16[2,256,1536]{2,1,0:T(8,128)(2,1)S(1)} collective-permute-done((bf16[2,256,1536]{2,1,0:T(8,128)(2,1)S(1)}, bf16[2,256,1536]{2,1,0:T(8,128)(2,1)S(1)}, u32[]{:S(2)}, u32[]{:S(2)}) %collective-permute-start.2) | collective-permute-done | bytes 1572896 | tf_op jit(solution)/shard_map/ppermute | solution.py:55
  265.8 3.7 collective-permute-done.5
  280.9 5.7 pad_maximum_fusion.2
  292.9 5.5 pad_maximum_fusion.1
  298.4 37.6 %fusion.45 = f32[4096,2304]{0,1:T(8,128)} fusion(bf16[4096,1536]{1,0:T(8,128)(2,1)} %bitcast.238, bf16[1536,2304]{1,0:T(8,128)(2,1)} %bitcast.262), kind=kOutput, calls=%fused_computation.245 | convolution fusion | flops 28991029248 | bytes 57409536 | tf_op jit(solution)/shard_map/dot_general | solution.py:28
  336.1 6.8 all-gather.6.cloned.1.call-done
  342.9 35.7 %multiply_convert_fusion.1 = (bf16[4096,1152]{0,1:T(8,128)(2,1)}, bf16[4096,1152]{0,1:T(8,128)(2,1)}, bf16[4096,1152]{0,1:T(8,128)(2,1)}) fusion(f32[4096,2304]{0,1:T(8,128)} %fusion.45, bf16[4096,1536]{1,0:T(8,128)(2,1)} %bitcast.240, bf16[1120,1536]{1,0:T(8,128)(2,1)} %all-gather.6.cloned.1.call-done), kind=kOutput, calls=%fused_computation.2 | convolution fusion | flops 14571012096 | bytes 82083840 | tf_op jit(solution)/shard_map/dot_general | solution.py:36
  378.6 36.3 %convolution_convert_fusion.1 = bf16[4096,1536]{1,0:T(8,128)(2,1)} fusion(bf16[1536,2304]{1,0:T(8,128)(2,1)} %bitcast.263, bf16[4096,1152]{0,1:T(8,128)(2,1)} %get-tuple-element.53, bf16[4096,1152]{0,1:T(8,128)(2,1)} %get-tuple-element.52), kind=kOutput, calls=%fused_computation.6 | convolution fusion | flops 29035069440 | bytes 38535168 | tf_op jit(solution)/shard_map/dot_general | solution.py:36
  414.9 9.2 fusion.37
  426.5 17.3 %fusion.46 = bf16[1152,1536]{1,0:T(8,128)(2,1)S(1)} fusion(bf16[4096,1152]{0,1:T(8,128)(2,1)} %get-tuple-element.37, bf16[4096,1536]{1,0:T(8,128)(2,1)S(1)} %bitcast.241), kind=kOutput, calls=%fused_computation.246 | convolution fusion | flops 14495514624 | bytes 25559040 | tf_op jit(solution)/shard_map/dot_general | solution.py:32
  445.9 15.2 %pad_maximum_fusion = bf16[4096,2304]{0,1:T(8,128)(2,1)} fusion(bf16[4096,1152]{0,1:T(8,128)(2,1)} %get-tuple-element.53, bf16[4096,1152]{0,1:T(8,128)(2,1)} %get-tuple-element.52), kind=kLoop, calls=%fused_computation | loop fusion | flops 37748736 | bytes 37748736 | tf_op jit(solution)/shard_map/concatenate | solution.py:718
  473.8 38.2 %convolution_convert_fusion.2 = bf16[1536,2304]{1,0:T(8,128)(2,1)} fusion(bf16[4096,1536]{1,0:T(8,128)(2,1)} %bitcast.239, bf16[4096,2304]{0,1:T(8,128)(2,1)} %pad_maximum_fusion), kind=kOutput, calls=%fused_computation.9 | convolution fusion | flops 28994568192 | bytes 38535168 | tf_op jit(solution)/shard_map/dot_general | solution.py:32
  517.1 23.9 %convolution_convert_fusion = bf16[4096,1536]{1,0:T(8,128)(2,1)} fusion(bf16[4096,1152]{0,1:T(8,128)(2,1)} %get-tuple-element.37, bf16[1120,1536]{1,0:T(8,128)(2,1)S(1)} %copy-done.72), kind=kOutput, calls=%fused_computation.5 | convolution fusion | flops 14501806080 | bytes 25460736 | tf_op jit(solution)/shard_map/dot_general | solution.py:28
  549.2 6.0 fusion.36
  593.5 3.7 add_convert_fusion
  603.6 3.7 fusion
  609.0 46.1 %collective-permute-done.47 = bf16[1,280,1536]{2,1,0:T(8,128)(2,1)S(1)} collective-permute-done((bf16[1,280,1536]{2,1,0:T(8,128)(2,1)}, bf16[1,280,1536]{2,1,0:T(8,128)(2,1)S(1)}, u32[]{:S(2)}, u32[]{:S(2)}) %collective-permute-start.47) | collective-permute-done | bytes 860192 | tf_op jit(solution)/shard_map/ppermute | solution.py:55
  662.2 13.8 %collective-permute-done.24 = bf16[256,1536]{1,0:T(8,128)(2,1)S(1)} collective-permute-done((bf16[256,1536]{1,0:T(8,128)(2,1)S(1)}, bf16[256,1536]{1,0:T(8,128)(2,1)S(1)}, u32[]{:S(2)}, u32[]{:S(2)}) %collective-permute-start.24) | collective-permute-done | bytes 786464 | tf_op jit(solution)/shard_map/ppermute | solution.py:55
  683.2 4.4 convolution_convert_fusion.3
  687.6 10.5 %reshape_reshape.3 = bf16[4,4,96,2,2,384]{5,4,3,2,1,0:T(2,128)(2,1)} reshape(bf16[1536,1536]{1,0:T(8,128)(2,1)} %convolution_convert_fusion.3) | data formatting | bytes 9437184 | tf_op jit(solution)/shard_map/reshape;reshape | solution.py:619
  698.1 12.4 %fusion.38 = (bf16[4,4,96,2,1,384]{5,4,3,2,1,0:T(2,128)(2,1)S(1)}, bf16[4,4,96,2,1,384]{5,4,3,2,1,0:T(2,128)(2,1)}) fusion(bf16[4,4,96,2,2,384]{5,4,3,2,1,0:T(2,128)(2,1)} %reshape_reshape.3), kind=kLoop, calls=%fused_computation.238 | loop fusion | bytes 9437184 | tf_op jit(solution)/shard_map/slice | solution.py:622
  713.2 6.2 convolution_convert_fusion.5.g_ref
  719.4 31.1 %attend_backward.1 = (bf16[512,1536]{1,0:T(8,128)(2,1)}, f32[1024,256]{1,0:T(8,128)}, f32[1024,256]{1,0:T(8,128)}) custom-call(s32[1,1024]{1,0:T(1,128)} %compare_select_fusion.kpos_ref, f32[512,128]{1,0:T(8,128)} %copy-done.4, f32[512,128]{1,0:T(8,128)} %copy-done.6, bf16[512,2048]{1,0:T(8,128)(2,1)} %get-tuple-element.31.q_ref, ...), custom_call_target="tpu_custom_call" | custom-call | flops 24159191040 | bytes 9437184 | tf_op jit(solution)/shard_map/attend_backward/pallas_call | solution.py:550
  768.8 8.8 fusion.13
  780.9 6.8 convolution_convert_fusion.4
  787.8 11.4 %concatenate.155 = bf16[4,4,96,2,2,512]{5,4,3,2,1,0:T(2,128)(2,1)} reshape(bf16[1536,2048]{1,0:T(8,128)(2,1)} %convolution_convert_fusion.4) | data formatting | bytes 12582912 | tf_op jit(solution)/shard_map/concatenate | solution.py:794
  799.2 4.6 copy_dynamic-update-slice_fusion
  815.8 9.6 %collective-permute-done.37 = bf16[2,4,96,384]{3,2,1,0:T(8,128)(2,1)S(1)} collective-permute-done((bf16[2,4,96,384]{3,2,1,0:T(8,128)(2,1)S(1)}, bf16[2,4,96,384]{3,2,1,0:T(8,128)(2,1)S(1)}, u32[]{:S(2)}, u32[]{:S(2)}) %collective-permute-start.37) | collective-permute-done | bytes 589856 | tf_op jit(solution)/shard_map/ppermute | solution.py:55
  840.3 15.0 %collective-permute-done.30 = bf16[2,4,104,512]{3,2,1,0:T(8,128)(2,1)} collective-permute-done((bf16[2,4,104,512]{3,2,1,0:T(8,128)(2,1)}, bf16[2,4,104,512]{3,2,1,0:T(8,128)(2,1)}, u32[]{:S(2)}, u32[]{:S(2)}) %collective-permute-start.30) | collective-permute-done | bytes 852000 | tf_op jit(solution)/shard_map/ppermute | solution.py:55
  860.7 6.3 collective-permute-done.31
  875.0 7.5 collective-permute-done.45
  882.6 7.7 collective-permute-done.44
  893.0 4.0 fusion.17
  897.0 4.0 reduce-scatter.5.cloned.1.call-done
  904.4 33.6 %collective-permute-done.35 = bf16[1,104,1024]{2,1,0:T(8,128)(2,1)S(1)} collective-permute-done((bf16[1,104,1024]{2,1,0:T(8,128)(2,1)}, bf16[1,104,1024]{2,1,0:T(8,128)(2,1)S(1)}, u32[]{:S(2)}, u32[]{:S(2)}) %collective-permute-start.35) | collective-permute-done | bytes 213024 | tf_op jit(solution)/shard_map/ppermute | solution.py:55
  941.0 3.8 pad_maximum_fusion.3.u_ref
  944.8 6.1 join_units.1
  (401 shorter events, 198.8 us)
Async XLA Ops:
  7.2 291.2 %all-gather.4.cloned.1.call-start = ((), (), s32[]{:S(2)}) async-start(), calls=%async_computation.4 | async-start | bytes 8847360 | tf_op jit(solution)/shard_map/all_gather | solution.py:609
  16.4 13.8 %collective-permute-start.8 = (bf16[96,2304]{1,0:T(8,128)(2,1)}, bf16[96,2304]{1,0:T(8,128)(2,1)}, u32[]{:S(2)}, u32[]{:S(2)}) collective-permute-start(bf16[96,2304]{1,0:T(8,128)(2,1)} %get-tuple-element.109), channel_id=1, source_target_pairs={{0,4},{2,6},{4,0},{6,2},{8,12},{10,14},{12,8},{14,10},{16,20},{18,... | collective-permute-start | bytes 1327112 | tf_op jit(solution)/shard_map/ppermute | solution.py:648
  18.9 20.4 %collective-permute-start.9 = (bf16[96,2304]{1,0:T(8,128)(2,1)}, bf16[96,2304]{1,0:T(8,128)(2,1)}, u32[]{:S(2)}, u32[]{:S(2)}) collective-permute-start(bf16[96,2304]{1,0:T(8,128)(2,1)} %get-tuple-element.108), channel_id=1, source_target_pairs={{0,6},{2,4},{4,2},{6,0},{8,14},{10,12},{12,10},{14,8},{16,22},{18,... | collective-permute-start | bytes 1327112 | tf_op jit(solution)/shard_map/ppermute | solution.py:648
  42.5 300.4 %all-gather.6.cloned.1.call-start = ((), (), s32[]{:S(2)}) async-start(), calls=%async_computation.9 | async-start | bytes 4300800 | tf_op jit(solution)/shard_map/all_gather | solution.py:609
  125.0 13.3 %collective-permute-start = (bf16[1,512,512]{2,1,0:T(8,128)(2,1)S(1)}, bf16[1,512,512]{2,1,0:T(8,128)(2,1)S(1)}, u32[]{:S(2)}, u32[]{:S(2)}) collective-permute-start(bf16[1,512,512]{2,1,0:T(8,128)(2,1)S(1)} %slice_bitcast_fusion.14), channel_id=1, source_target_pairs={{0,1},{1,0},{2,3},{3,2},{4,5},{5,4},{6,7},{7,6},{8,9},{9,8},{10,11... | collective-permute-start | bytes 1572872 | tf_op jit(solution)/shard_map/ppermute | solution.py:55
  128.8 39.1 %collective-permute-start.10 = (bf16[1,256,1536]{2,1,0:T(8,128)(2,1)}, bf16[1,256,1536]{2,1,0:T(8,128)(2,1)}, u32[]{:S(2)}, u32[]{:S(2)}) collective-permute-start(bf16[1,256,1536]{2,1,0:T(8,128)(2,1)} %get-tuple-element.113), channel_id=1, source_target_pairs={{0,4},{2,6},{4,0},{6,2},{8,12},{10,14},{12,8},{14,10},{16,20},{18,... | collective-permute-start | bytes 2359304 | tf_op jit(solution)/shard_map/ppermute | solution.py:55
  129.0 43.1 %collective-permute-start.13 = (bf16[1,256,1536]{2,1,0:T(8,128)(2,1)S(1)}, bf16[1,256,1536]{2,1,0:T(8,128)(2,1)}, u32[]{:S(2)}, u32[]{:S(2)}) collective-permute-start(bf16[1,256,1536]{2,1,0:T(8,128)(2,1)S(1)} %get-tuple-element.114), channel_id=1, source_target_pairs={{0,1},{1,0},{2,3},{3,2},{4,5},{5,4},{6,7},{7,6},{8,9},{9,8},{10,11... | collective-permute-start | bytes 2359304 | tf_op jit(solution)/shard_map/ppermute | solution.py:55
  169.9 35.0 %collective-permute-start.11 = (bf16[2,256,1536]{2,1,0:T(8,128)(2,1)S(1)}, bf16[2,256,1536]{2,1,0:T(8,128)(2,1)S(1)}, u32[]{:S(2)}, u32[]{:S(2)}) collective-permute-start(bf16[2,256,1536]{2,1,0:T(8,128)(2,1)S(1)} %pad_maximum_fusion.17), channel_id=1, source_target_pairs={{0,1},{1,0},{2,3},{3,2},{4,5},{5,4},{6,7},{7,6},{8,9},{9,8},{10,11... | collective-permute-start | bytes 4718600 | tf_op jit(solution)/shard_map/ppermute | solution.py:55
  173.4 52.5 %collective-permute-start.14 = (bf16[2,256,1536]{2,1,0:T(8,128)(2,1)S(1)}, bf16[2,256,1536]{2,1,0:T(8,128)(2,1)S(1)}, u32[]{:S(2)}, u32[]{:S(2)}) collective-permute-start(bf16[2,256,1536]{2,1,0:T(8,128)(2,1)S(1)} %pad_maximum_fusion.18), channel_id=1, source_target_pairs={{0,4},{2,6},{4,0},{6,2},{8,12},{10,14},{12,8},{14,10},{16,20},{18,... | collective-permute-start | bytes 4718600 | tf_op jit(solution)/shard_map/ppermute | solution.py:55
  173.8 51.9 %collective-permute-start.1 = (bf16[1,256,1536]{2,1,0:T(8,128)(2,1)S(1)}, bf16[1,256,1536]{2,1,0:T(8,128)(2,1)S(1)}, u32[]{:S(2)}, u32[]{:S(2)}) collective-permute-start(bf16[1,256,1536]{2,1,0:T(8,128)(2,1)S(1)} %get-tuple-element.115), channel_id=1, source_target_pairs={{0,4},{2,6},{4,0},{6,2},{8,12},{10,14},{12,8},{14,10},{16,20},{18,... | collective-permute-start | bytes 2359304 | tf_op jit(solution)/shard_map/ppermute | solution.py:55
  175.7 55.9 %collective-permute-start.4 = (bf16[1,256,1536]{2,1,0:T(8,128)(2,1)S(1)}, bf16[1,256,1536]{2,1,0:T(8,128)(2,1)S(1)}, u32[]{:S(2)}, u32[]{:S(2)}) collective-permute-start(bf16[1,256,1536]{2,1,0:T(8,128)(2,1)S(1)} %get-tuple-element.116), channel_id=1, source_target_pairs={{0,1},{1,0},{2,3},{3,2},{4,5},{5,4},{6,7},{7,6},{8,9},{9,8},{10,11... | collective-permute-start | bytes 2359304 | tf_op jit(solution)/shard_map/ppermute | solution.py:55
  208.8 65.3 %collective-permute-start.12 = (bf16[4,256,1536]{2,1,0:T(8,128)(2,1)}, bf16[4,256,1536]{2,1,0:T(8,128)(2,1)}, u32[]{:S(2)}, u32[]{:S(2)}) collective-permute-start(bf16[4,256,1536]{2,1,0:T(8,128)(2,1)} %pad_maximum_fusion.6), channel_id=1, source_target_pairs={{0,2},{2,0},{4,6},{6,4},{8,10},{10,8},{12,14},{14,12},{16,18},{18,... | collective-permute-start | bytes 9437192 | tf_op jit(solution)/shard_map/ppermute | solution.py:55
  225.8 36.5 %collective-permute-start.2 = (bf16[2,256,1536]{2,1,0:T(8,128)(2,1)S(1)}, bf16[2,256,1536]{2,1,0:T(8,128)(2,1)S(1)}, u32[]{:S(2)}, u32[]{:S(2)}) collective-permute-start(bf16[2,256,1536]{2,1,0:T(8,128)(2,1)S(1)} %pad_maximum_fusion.15), channel_id=1, source_target_pairs={{0,1},{1,0},{2,3},{3,2},{4,5},{5,4},{6,7},{7,6},{8,9},{9,8},{10,11... | collective-permute-start | bytes 4718600 | tf_op jit(solution)/shard_map/ppermute | solution.py:55
  229.8 48.0 %collective-permute-start.15 = (bf16[4,256,1536]{2,1,0:T(8,128)(2,1)}, bf16[4,256,1536]{2,1,0:T(8,128)(2,1)}, u32[]{:S(2)}, u32[]{:S(2)}) collective-permute-start(bf16[4,256,1536]{2,1,0:T(8,128)(2,1)} %pad_maximum_fusion.7), channel_id=1, source_target_pairs={{0,2},{2,0},{4,6},{6,4},{8,10},{10,8},{12,14},{14,12},{16,18},{18,... | collective-permute-start | bytes 9437192 | tf_op jit(solution)/shard_map/ppermute | solution.py:55
  232.9 36.6 %collective-permute-start.5 = (bf16[2,256,1536]{2,1,0:T(8,128)(2,1)}, bf16[2,256,1536]{2,1,0:T(8,128)(2,1)}, u32[]{:S(2)}, u32[]{:S(2)}) collective-permute-start(bf16[2,256,1536]{2,1,0:T(8,128)(2,1)} %pad_maximum_fusion.16), channel_id=1, source_target_pairs={{0,4},{2,6},{4,0},{6,2},{8,12},{10,14},{12,8},{14,10},{16,20},{18,... | collective-permute-start | bytes 4718600 | tf_op jit(solution)/shard_map/ppermute | solution.py:55
  264.5 22.0 %collective-permute-start.3 = (bf16[4,256,1536]{2,1,0:T(8,128)(2,1)}, bf16[4,256,1536]{2,1,0:T(8,128)(2,1)}, u32[]{:S(2)}, u32[]{:S(2)}) collective-permute-start(bf16[4,256,1536]{2,1,0:T(8,128)(2,1)} %pad_maximum_fusion.4), channel_id=1, source_target_pairs={{0,2},{2,0},{4,6},{6,4},{8,10},{10,8},{12,14},{14,12},{16,18},{18,... | collective-permute-start | bytes 9437192 | tf_op jit(solution)/shard_map/ppermute | solution.py:55
  265.6 336.2 %reduce-scatter.11.cloned.1.call-start = ((), (), s32[]{:S(2)}) async-start(), calls=%async_computation.8 | async-start | bytes 4300800 | tf_op jit(solution)/shard_map/reduce_scatter | solution.py:612
  273.1 16.5 %collective-permute-start.6 = (bf16[4,256,1536]{2,1,0:T(8,128)(2,1)}, bf16[4,256,1536]{2,1,0:T(8,128)(2,1)}, u32[]{:S(2)}, u32[]{:S(2)}) collective-permute-start(bf16[4,256,1536]{2,1,0:T(8,128)(2,1)} %pad_maximum_fusion.5), channel_id=1, source_target_pairs={{0,2},{2,0},{4,6},{6,4},{8,10},{10,8},{12,14},{14,12},{16,18},{18,... | collective-permute-start | bytes 9437192 | tf_op jit(solution)/shard_map/ppermute | solution.py:55
  424.0 37.0 %collective-permute-start.16 = (bf16[4,256,1536]{2,1,0:T(8,128)(2,1)}, bf16[4,256,1536]{2,1,0:T(8,128)(2,1)}, u32[]{:S(2)}, u32[]{:S(2)}) collective-permute-start(bf16[4,256,1536]{2,1,0:T(8,128)(2,1)} %bitcast.33), channel_id=1, source_target_pairs={{0,2},{2,0},{4,6},{6,4},{8,10},{10,8},{12,14},{14,12},{16,18},{18,... | collective-permute-start | bytes 9437192 | tf_op jit(solution)/shard_map/ppermute | solution.py:55
  424.1 41.1 %collective-permute-start.18 = (bf16[4,256,1536]{2,1,0:T(8,128)(2,1)}, bf16[4,256,1536]{2,1,0:T(8,128)(2,1)}, u32[]{:S(2)}, u32[]{:S(2)}) collective-permute-start(bf16[4,256,1536]{2,1,0:T(8,128)(2,1)} %bitcast.35), channel_id=1, source_target_pairs={{0,2},{2,0},{4,6},{6,4},{8,10},{10,8},{12,14},{14,12},{16,18},{18,... | collective-permute-start | bytes 9437192 | tf_op jit(solution)/shard_map/ppermute | solution.py:55
  445.9 421.2 %reduce-scatter.9.cloned.1.call-start = ((), (), s32[]{:S(2)}) async-start(), calls=%async_computation.7 | async-start | bytes 8847360 | tf_op jit(solution)/shard_map/reduce_scatter | solution.py:612
  470.9 41.1 %collective-permute-start.17 = (bf16[2,256,1536]{2,1,0:T(8,128)(2,1)}, bf16[2,256,1536]{2,1,0:T(8,128)(2,1)}, u32[]{:S(2)}, u32[]{:S(2)}) collective-permute-start(bf16[2,256,1536]{2,1,0:T(8,128)(2,1)} %slice.404), channel_id=1, source_target_pairs={{0,1},{1,0},{2,3},{3,2},{4,5},{5,4},{6,7},{7,6},{8,9},{9,8},{10,11... | collective-permute-start | bytes 4718600 | tf_op jit(solution)/shard_map/ppermute | solution.py:55
  472.3 41.7 %collective-permute-start.19 = (bf16[2,256,1536]{2,1,0:T(8,128)(2,1)}, bf16[2,256,1536]{2,1,0:T(8,128)(2,1)}, u32[]{:S(2)}, u32[]{:S(2)}) collective-permute-start(bf16[2,256,1536]{2,1,0:T(8,128)(2,1)} %slice.408), channel_id=1, source_target_pairs={{0,4},{2,6},{4,0},{6,2},{8,12},{10,14},{12,8},{14,10},{16,20},{18,... | collective-permute-start | bytes 4718600 | tf_op jit(solution)/shard_map/ppermute | solution.py:55
  547.7 45.8 %collective-permute-start.22 = (bf16[4,256,1536]{2,1,0:T(8,128)(2,1)}, bf16[4,256,1536]{2,1,0:T(8,128)(2,1)}, u32[]{:S(2)}, u32[]{:S(2)}) collective-permute-start(bf16[4,256,1536]{2,1,0:T(8,128)(2,1)} %slice.338), channel_id=1, source_target_pairs={{0,2},{2,0},{4,6},{6,4},{8,10},{10,8},{12,14},{14,12},{16,18},{18,... | collective-permute-start | bytes 9437192 | tf_op jit(solution)/shard_map/ppermute | solution.py:55
  548.7 39.7 %collective-permute-start.20 = (bf16[256,1536]{1,0:T(8,128)(2,1)}, bf16[256,1536]{1,0:T(8,128)(2,1)}, u32[]{:S(2)}, u32[]{:S(2)}) collective-permute-start(bf16[256,1536]{1,0:T(8,128)(2,1)} %slice_bitcast_fusion.8), channel_id=1, source_target_pairs={{0,4},{2,6},{4,0},{6,2},{8,12},{10,14},{12,8},{14,10},{16,20},{18,... | collective-permute-start | bytes 2359304 | tf_op jit(solution)/shard_map/ppermute | solution.py:55
  555.1 48.5 %collective-permute-start.25 = (bf16[4,256,1536]{2,1,0:T(8,128)(2,1)}, bf16[4,256,1536]{2,1,0:T(8,128)(2,1)}, u32[]{:S(2)}, u32[]{:S(2)}) collective-permute-start(bf16[4,256,1536]{2,1,0:T(8,128)(2,1)} %bitcast.44), channel_id=1, source_target_pairs={{0,2},{2,0},{4,6},{6,4},{8,10},{10,8},{12,14},{14,12},{16,18},{18,... | collective-permute-start | bytes 9437192 | tf_op jit(solution)/shard_map/ppermute | solution.py:55
  556.3 33.8 %collective-permute-start.21 = (bf16[256,1536]{1,0:T(8,128)(2,1)}, bf16[256,1536]{1,0:T(8,128)(2,1)}, u32[]{:S(2)}, u32[]{:S(2)}) collective-permute-start(bf16[256,1536]{1,0:T(8,128)(2,1)} %slice_bitcast_fusion.6), channel_id=1, source_target_pairs={{0,1},{1,0},{2,3},{3,2},{4,5},{5,4},{6,7},{7,6},{8,9},{9,8},{10,11... | collective-permute-start | bytes 2359304 | tf_op jit(solution)/shard_map/ppermute | solution.py:55
  588.4 285.7 %reduce-scatter.7.cloned.1.call-start = ((), (), s32[]{:S(2)}) async-start(), calls=%async_computation.6 | async-start | bytes 737280 | tf_op jit(solution)/shard_map/reduce_scatter | solution.py:612
  600.2 55.1 %collective-permute-start.23 = (bf16[2,256,1536]{2,1,0:T(8,128)(2,1)}, bf16[2,256,1536]{2,1,0:T(8,128)(2,1)}, u32[]{:S(2)}, u32[]{:S(2)}) collective-permute-start(bf16[2,256,1536]{2,1,0:T(8,128)(2,1)} %slice.415), channel_id=1, source_target_pairs={{0,1},{1,0},{2,3},{3,2},{4,5},{5,4},{6,7},{7,6},{8,9},{9,8},{10,11... | collective-permute-start | bytes 4718600 | tf_op jit(solution)/shard_map/ppermute | solution.py:55
  601.8 53.4 %collective-permute-start.47 = (bf16[1,280,1536]{2,1,0:T(8,128)(2,1)}, bf16[1,280,1536]{2,1,0:T(8,128)(2,1)S(1)}, u32[]{:S(2)}, u32[]{:S(2)}) collective-permute-start(bf16[1,280,1536]{2,1,0:T(8,128)(2,1)} %reduce-scatter.11.cloned.1.call-done), channel_id=1, source_target_pairs={{0,1},{1,0},{2,3},{3,2},{4,5},{5,4},{6,7},{7,6},{8,9},{9,8},{10,11... | collective-permute-start | bytes 2580488 | tf_op jit(solution)/shard_map/ppermute | solution.py:55
  607.5 51.3 %collective-permute-start.26 = (bf16[2,256,1536]{2,1,0:T(8,128)(2,1)S(1)}, bf16[2,256,1536]{2,1,0:T(8,128)(2,1)S(1)}, u32[]{:S(2)}, u32[]{:S(2)}) collective-permute-start(bf16[2,256,1536]{2,1,0:T(8,128)(2,1)S(1)} %slice.421), channel_id=1, source_target_pairs={{0,4},{2,6},{4,0},{6,2},{8,12},{10,14},{12,8},{14,10},{16,20},{18,... | collective-permute-start | bytes 4718600 | tf_op jit(solution)/shard_map/ppermute | solution.py:55
  657.2 18.8 %collective-permute-start.24 = (bf16[256,1536]{1,0:T(8,128)(2,1)S(1)}, bf16[256,1536]{1,0:T(8,128)(2,1)S(1)}, u32[]{:S(2)}, u32[]{:S(2)}) collective-permute-start(bf16[256,1536]{1,0:T(8,128)(2,1)S(1)} %slice_bitcast_fusion.4), channel_id=1, source_target_pairs={{0,4},{2,6},{4,0},{6,2},{8,12},{10,14},{12,8},{14,10},{16,20},{18,... | collective-permute-start | bytes 2359304 | tf_op jit(solution)/shard_map/ppermute | solution.py:55
  659.3 18.5 %collective-permute-start.27 = (bf16[256,1536]{1,0:T(8,128)(2,1)S(1)}, bf16[256,1536]{1,0:T(8,128)(2,1)S(1)}, u32[]{:S(2)}, u32[]{:S(2)}) collective-permute-start(bf16[256,1536]{1,0:T(8,128)(2,1)S(1)} %slice_bitcast_fusion.2), channel_id=1, source_target_pairs={{0,1},{1,0},{2,3},{3,2},{4,5},{5,4},{6,7},{7,6},{8,9},{9,8},{10,11... | collective-permute-start | bytes 2359304 | tf_op jit(solution)/shard_map/ppermute | solution.py:55
  757.2 50.5 %collective-permute-start.36 = (bf16[4,4,96,384]{3,2,1,0:T(8,128)(2,1)}, bf16[4,4,96,384]{3,2,1,0:T(8,128)(2,1)}, u32[]{:S(2)}, u32[]{:S(2)}) collective-permute-start(bf16[4,4,96,384]{3,2,1,0:T(8,128)(2,1)} %pad_maximum_fusion.19), channel_id=1, source_target_pairs={{0,2},{2,0},{4,6},{6,4},{8,10},{10,8},{12,14},{14,12},{16,18},{18,... | collective-permute-start | bytes 3538952 | tf_op jit(solution)/shard_map/ppermute | solution.py:55
  762.5 48.8 %collective-permute-start.39 = (bf16[4,4,96,384]{3,2,1,0:T(8,128)(2,1)}, bf16[4,4,96,384]{3,2,1,0:T(8,128)(2,1)}, u32[]{:S(2)}, u32[]{:S(2)}) collective-permute-start(bf16[4,4,96,384]{3,2,1,0:T(8,128)(2,1)} %pad_maximum_fusion.20), channel_id=1, source_target_pairs={{0,2},{2,0},{4,6},{6,4},{8,10},{10,8},{12,14},{14,12},{16,18},{18,... | collective-permute-start | bytes 3538952 | tf_op jit(solution)/shard_map/ppermute | solution.py:55
  806.1 23.2 %collective-permute-start.29 = (bf16[4,4,104,512]{3,2,1,0:T(8,128)(2,1)S(1)}, bf16[4,4,104,512]{3,2,1,0:T(8,128)(2,1)S(1)}, u32[]{:S(2)}, u32[]{:S(2)}) collective-permute-start(bf16[4,4,104,512]{3,2,1,0:T(8,128)(2,1)S(1)} %pad_maximum_fusion.13), channel_id=1, source_target_pairs={{0,2},{2,0},{4,6},{6,4},{8,10},{10,8},{12,14},{14,12},{16,18},{18,... | collective-permute-start | bytes 5111816 | tf_op jit(solution)/shard_map/ppermute | solution.py:55
  807.1 27.7 %collective-permute-start.32 = (bf16[4,4,104,512]{3,2,1,0:T(8,128)(2,1)S(1)}, bf16[4,4,104,512]{3,2,1,0:T(8,128)(2,1)S(1)}, u32[]{:S(2)}, u32[]{:S(2)}) collective-permute-start(bf16[4,4,104,512]{3,2,1,0:T(8,128)(2,1)S(1)} %pad_maximum_fusion.14), channel_id=1, source_target_pairs={{0,2},{2,0},{4,6},{6,4},{8,10},{10,8},{12,14},{14,12},{16,18},{18,... | collective-permute-start | bytes 5111816 | tf_op jit(solution)/shard_map/ppermute | solution.py:55
  809.7 15.8 %collective-permute-start.37 = (bf16[2,4,96,384]{3,2,1,0:T(8,128)(2,1)S(1)}, bf16[2,4,96,384]{3,2,1,0:T(8,128)(2,1)S(1)}, u32[]{:S(2)}, u32[]{:S(2)}) collective-permute-start(bf16[2,4,96,384]{3,2,1,0:T(8,128)(2,1)S(1)} %slice.452), channel_id=1, source_target_pairs={{0,1},{1,0},{2,3},{3,2},{4,5},{5,4},{6,7},{7,6},{8,9},{9,8},{10,11... | collective-permute-start | bytes 1769480 | tf_op jit(solution)/shard_map/ppermute | solution.py:55
  812.9 16.0 %collective-permute-start.40 = (bf16[2,4,96,384]{3,2,1,0:T(8,128)(2,1)S(1)}, bf16[2,4,96,384]{3,2,1,0:T(8,128)(2,1)S(1)}, u32[]{:S(2)}, u32[]{:S(2)}) collective-permute-start(bf16[2,4,96,384]{3,2,1,0:T(8,128)(2,1)S(1)} %slice.457), channel_id=1, source_target_pairs={{0,4},{2,6},{4,0},{6,2},{8,12},{10,14},{12,8},{14,10},{16,20},{18,... | collective-permute-start | bytes 1769480 | tf_op jit(solution)/shard_map/ppermute | solution.py:55
  830.9 24.5 %collective-permute-start.30 = (bf16[2,4,104,512]{3,2,1,0:T(8,128)(2,1)}, bf16[2,4,104,512]{3,2,1,0:T(8,128)(2,1)}, u32[]{:S(2)}, u32[]{:S(2)}) collective-permute-start(bf16[2,4,104,512]{3,2,1,0:T(8,128)(2,1)} %slice.435), channel_id=1, source_target_pairs={{0,1},{1,0},{2,3},{3,2},{4,5},{5,4},{6,7},{7,6},{8,9},{9,8},{10,11... | collective-permute-start | bytes 2555912 | tf_op jit(solution)/shard_map/ppermute | solution.py:55
  837.5 20.8 %collective-permute-start.33 = (bf16[2,4,104,512]{3,2,1,0:T(8,128)(2,1)}, bf16[2,4,104,512]{3,2,1,0:T(8,128)(2,1)}, u32[]{:S(2)}, u32[]{:S(2)}) collective-permute-start(bf16[2,4,104,512]{3,2,1,0:T(8,128)(2,1)} %slice.440), channel_id=1, source_target_pairs={{0,4},{2,6},{4,0},{6,2},{8,12},{10,14},{12,8},{14,10},{16,20},{18,... | collective-permute-start | bytes 2555912 | tf_op jit(solution)/shard_map/ppermute | solution.py:55
  840.0 61.0 %reduce-scatter.5.cloned.1.call-start = ((), (), s32[]{:S(2)}) async-start(), calls=%async_computation.5 | async-start | bytes 1064960 | tf_op jit(solution)/shard_map/reduce_scatter | solution.py:612
  869.8 12.8 %collective-permute-start.45 = (bf16[96,2304]{1,0:T(8,128)(2,1)}, bf16[96,2304]{1,0:T(8,128)(2,1)}, u32[]{:S(2)}, u32[]{:S(2)}) collective-permute-start(bf16[96,2304]{1,0:T(8,128)(2,1)} %get-tuple-element.100), channel_id=1, source_target_pairs={{0,6},{2,4},{4,2},{6,0},{8,14},{10,12},{12,10},{14,8},{16,22},{18,... | collective-permute-start | bytes 1327112 | tf_op jit(solution)/shard_map/ppermute | solution.py:648
  869.8 12.8 %collective-permute-start.43 = (bf16[96,2304]{1,0:T(8,128)(2,1)}, bf16[96,2304]{1,0:T(8,128)(2,1)}, u32[]{:S(2)}, u32[]{:S(2)}) collective-permute-start(bf16[96,2304]{1,0:T(8,128)(2,1)} %get-tuple-element.102), channel_id=1, source_target_pairs={{0,2},{2,0},{4,6},{6,4},{8,10},{10,8},{12,14},{14,12},{16,18},{18,... | collective-permute-start | bytes 1327112 | tf_op jit(solution)/shard_map/ppermute | solution.py:648
  870.5 19.8 %collective-permute-start.44 = (bf16[96,2304]{1,0:T(8,128)(2,1)}, bf16[96,2304]{1,0:T(8,128)(2,1)}, u32[]{:S(2)}, u32[]{:S(2)}) collective-permute-start(bf16[96,2304]{1,0:T(8,128)(2,1)} %get-tuple-element.101), channel_id=1, source_target_pairs={{0,4},{2,6},{4,0},{6,2},{8,12},{10,14},{12,8},{14,10},{16,20},{18,... | collective-permute-start | bytes 1327112 | tf_op jit(solution)/shard_map/ppermute | solution.py:648
  874.1 22.8 %collective-permute-start.42 = (bf16[1,96,768]{2,1,0:T(8,128)(2,1)}, bf16[1,96,768]{2,1,0:T(8,128)(2,1)S(1)}, u32[]{:S(2)}, u32[]{:S(2)}) collective-permute-start(bf16[1,96,768]{2,1,0:T(8,128)(2,1)} %reduce-scatter.7.cloned.1.call-done), channel_id=1, source_target_pairs={{0,1},{1,0},{2,3},{3,2},{4,5},{5,4},{6,7},{7,6},{8,9},{9,8},{10,11... | collective-permute-start | bytes 442376 | tf_op jit(solution)/shard_map/ppermute | solution.py:55
  892.0 49.0 %collective-permute-start.46 = (bf16[1,4,96,2304]{3,2,1,0:T(8,128)(2,1)S(1)}, bf16[1,4,96,2304]{3,2,1,0:T(8,128)(2,1)}, u32[]{:S(2)}, u32[]{:S(2)}) collective-permute-start(bf16[1,4,96,2304]{3,2,1,0:T(8,128)(2,1)S(1)} %maximum_bitcast_fusion.4), channel_id=1, source_target_pairs={{0,1},{1,0},{2,3},{3,2},{4,5},{5,4},{6,7},{7,6},{8,9},{9,8},{10,11... | collective-permute-start | bytes 5308424 | tf_op jit(solution)/shard_map/ppermute | solution.py:55
  901.0 37.1 %collective-permute-start.35 = (bf16[1,104,1024]{2,1,0:T(8,128)(2,1)}, bf16[1,104,1024]{2,1,0:T(8,128)(2,1)S(1)}, u32[]{:S(2)}, u32[]{:S(2)}) collective-permute-start(bf16[1,104,1024]{2,1,0:T(8,128)(2,1)} %reduce-scatter.5.cloned.1.call-done), channel_id=1, source_target_pairs={{0,1},{1,0},{2,3},{3,2},{4,5},{5,4},{6,7},{7,6},{8,9},{9,8},{10,11... | collective-permute-start | bytes 638984 | tf_op jit(solution)/shard_map/ppermute | solution.py:55
  (82 other events, 970.3 us)
Sparse Core Ops, SparseCore 0:
  42.6 149.8 all-gather.3
  265.7 77.1 all-gather.5
  446.0 67.1 reduce-scatter.10
  588.5 125.6 reduce-scatter.8
  840.1 24.6 reduce-scatter.6
  874.2 26.7 reduce-scatter.4
where the time goes:
time: 967 us; the launch traced here: 958 us
  waiting for transfers between devices  253 us (26%)
  matrix products  220 us (23%)
  Pallas kernels  146 us (15%)
  other arithmetic  130 us (13%)
  local copies, waits for them, and re-layouts  115 us (12%)
  starting transfers between devices  47.6 us (5%)
  between operations  46.8 us (5%)
    ppermute x42, waiting for transfers between devices, swap(): return lax.ppermute(value, axis, [(i, i ^ bit) for i in range(count)])  214 us
    dot_general x4, matrix products, product_right(): lax.dot_general(left, right, (((1,), (1,)), ((), ())), preferred_element_...  87.1 us
    pallas_call x1, Pallas kernels, gather_project(): pl.pallas_call(functools.partial(gather_kernel, outer, seq_count), in_spe...  80.5 us
    dot_general x4, matrix products, product_left(): lax.dot_general(left, right, (((0,), (0,)), ((), ())), preferred_element_...  66.7 us
    dot_general x3, matrix products, product(): return jnp.dot(left, right, preferred_element_type=full)  66.6 us
    ppermute x42, starting transfers between devices, swap(): return lax.ppermute(value, axis, [(i, i ^ bit) for i in range(count)])  41.1 us
    pallas_call x1, Pallas kernels, attend_backward(): pl.pallas_call(bwd_kernel, grid=(HEADS,), in_specs=[pl.BlockSpec((1, keys...  31.1 us
    ppermute x6, waiting for transfers between devices, inner_swap(): return lax.ppermute(value, 'wt', [(i, i ^ distance) for i in range(count)])  28 us
  transfers between devices with their start and end apart: 54, of which 23 were waited for; matrix products, arithmetic and copies ran while one was open for 38% of the time, Pallas kernels for 14%

commit v1 on v0

--- a/solution.py
+++ b/solution.py
@@ -69,8 +69,8 @@
 
 
 def reduce_hops(held, hops):
-    for hop in hops[:0:-1]:
-        held = reduce_hop(held, hop)
+    for k in range(len(hops) - 1, 0, -1):
+        held = reduce_hop(held, hops[k])
     return held[0].astype(full) + swap(held[1], hops[0]).astype(full)
 
 
@@ -107,14 +107,6 @@
                 place |= ((source // bit) % 2) << k
             order.append(place)
     return order
-
-
-def gather_plane(block, seq_count):
-    hops_a, hops_b = plane_hops(seq_count)
-    half = block.shape[0] // 2
-    part_a = gather_hops(block[:half], hops_a)
-    part_b = gather_hops(block[half:], hops_b)
-    return (part_a, part_b)
 
 
 def to_place(stacked, place):
@@ -641,7 +633,6 @@
 
     info = jnp.stack([seq_here, inner_here]).astype(jnp.int32)
     down_own = lax.dynamic_slice_in_dim(w_down, seq_here * ff_own, ff_own, axis=0).astype(low)
-    down_w = line_gather(down_own).reshape(ff_here, width)
 
     def inner_swap(value, distance):
         count = lax.axis_size("wt")
@@ -654,10 +645,6 @@
     stacked = inner_exchange(split_units(info, w_gate, w_up, outer, seq_count, ff_own, ff_pad))
     block = jnp.stack([to_place(stacked, inner_here ^ p) for p in range(INNER)])
     block = block.reshape(INNER * share, 2 * ff_pad)
-    units_w = line_gather(block).reshape(width, 2 * ff_pad)
-    down_w = jnp.pad(down_w, ((0, ff_pad - ff_here), (0, 0)))
-
-    bias_q, bias_k = b_query.shape[0], b_key.shape[0]
     half = HEAD_DIM // 2
     inverse = 10000.0 ** (-jnp.arange(half, dtype=full) / half)
     angle = places.astype(full)[:, None] * inverse[None, :]
@@ -673,13 +660,16 @@
     small = jnp.pad(small.astype(low), ((0, 11), (0, 0)))
     packed = jnp.concatenate([w_query, w_key, w_value], axis=1).astype(low)
     normed_low, qkv, vectors, head_all, out_all = gather_project(
-        after(tokens, block, down_own).reshape(rows, width),
+        tokens.reshape(rows, width),
         packed, w_out.astype(low), small, cosine, sine,
     )
     head_w = head_all.reshape(width, head_width)
     out_w = out_all.reshape(query_width, width)
     gain_one = vectors[0, :width]
     gain_two = vectors[2, :width]
+    units_w = line_gather(block).reshape(width, 2 * ff_pad)
+    down_w = line_gather(down_own).reshape(ff_here, width)
+    down_w = jnp.pad(down_w, ((0, ff_pad - ff_here), (0, 0)))
 
     seq_hops = bits_of("seq", seq_count)
     pairs = gather_hops(qkv[:, query_width:], seq_hops).reshape(SLOT, 2 * pair_width)
@@ -691,24 +681,33 @@
     normed_two, factor_two = norm_rows(resid, gain_two)
     normed_two_low = normed_two.astype(low)
 
+    core = hops_a[-1]
+    slow_a, slow_b = hops_a[:-1], hops_b[:-1]
+    near_rows = plane * rows // 2
+
     def spread(block):
-        part_a, part_b = gather_plane(block, seq_count)
-        return jnp.stack([part_a, part_b]).reshape(plane * rows, width)
-
-    def halves(partial):
-        return list(partial.astype(low).reshape(2, plane, rows // 2, width))
-
-    def hop_halves(parts, stage):
-        return [reduce_hop(part, hops[stage]) for part, hops in zip(parts, (hops_a, hops_b))]
-
-    def last_halves(parts):
-        got = [reduce_hops(part, hops[:1]) for part, hops in zip(parts, (hops_a, hops_b))]
+        part_a = gather_hops(block[: rows // 2], slow_a)
+        part_b = gather_hops(block[rows // 2 :], slow_b)
+        near = jnp.stack([part_a, part_b]).reshape(near_rows, width)
+        return jnp.concatenate([near, swap(near, core)], axis=0)
+
+    def hop_core(partial):
+        other = swap(partial[near_rows:], core)
+        near = (partial[:near_rows].astype(full) + other.astype(full)).astype(low)
+        near = near.reshape(2, plane // 2, rows // 2, width)
+        return (near[0], near[1])
+
+    def hop_slow(parts, stage):
+        return tuple(reduce_hop(part, hops[stage]) for part, hops in zip(parts, (slow_a, slow_b)))
+
+    def hop_last(parts):
+        got = [reduce_hops(part, hops[:1]) for part, hops in zip(parts, (slow_a, slow_b))]
         return jnp.concatenate(got, axis=0)
 
-    stages = list(range(len(hops_a)))[:0:-1]
-    grad_all = spread(after(upstream_low, vectors))
+    stages = list(range(1, len(slow_a)))[::-1]
+    grad_all = spread(upstream_low)
+    rows_all = spread(normed_two_low)
     hidden_grad = product_right(grad_all, down_w)
-    rows_all = spread(normed_two_low)
     both = product(rows_all, units_w)
     gate, upper = both[:, :ff_pad], both[:, ff_pad:]
     sigma = jax.nn.sigmoid(gate)
@@ -716,30 +715,19 @@
     gate_grad = (hidden_grad * upper * sigma * (1.0 + gate * (1.0 - sigma))).astype(low)
     up_grad = (hidden_grad * gate * sigma).astype(low)
     units_grad = jnp.concatenate([gate_grad, up_grad], axis=1)
-    back = halves(product_right(units_grad, units_w))
-    down_grad = product_left(after(hidden, back[0]), grad_all).astype(low)[:ff_here]
+    partial = product_right(units_grad, units_w).astype(low)
+    down_grad = product_left(after(hidden, partial), grad_all).astype(low)
+    down_grad = down_grad[:ff_here]
     down_line = line_reduce(down_grad.reshape(outer, ff_own, width))
-    back = hop_halves(back, stages[0])
+    back = hop_core(partial)
     rows_late, grad_late = lax.optimization_barrier((rows_all, units_grad, back, down_grad))[:2]
     units_w_grad = product_left(rows_late, grad_late).astype(low)
     units_line = line_reduce(units_w_grad.reshape(outer, INNER * share, 2 * ff_pad))
-    for stage in stages[1:]:
-        back = hop_halves(back, stage)
+    for stage in stages:
+        back = hop_slow(back, stage)
     hidden_late = after(hidden, back, units_w_grad)
-    forth = halves(product(hidden_late, down_w))
-    normed_two_grad = last_halves(back)
-    forth[0] = after(forth[0], normed_two_grad)
-    for stage in stages:
-        forth = hop_halves(forth, stage)
-    result = resid + last_halves(forth)
-    layer_out = jnp.where(keep, result, 0.0).astype(low).reshape(slot_count, rows, width)
-
-    blocks = units_line.reshape(INNER, share, 2 * ff_pad)
-    sent = jnp.stack([to_place(blocks, inner_here ^ d) for d in range(INNER)])
-    gate_out, up_out = join_units(
-        info, gather_hops(inner_exchange(sent), seq_hops), outer, ff_own
-    )
-    down_out = seq_gather(down_line).reshape(seq_count * ff_own, width).astype(full)
+    partial = product(hidden_late, down_w).astype(low)
+    normed_two_grad = hop_last(back)
 
     upstream = upstream_low.astype(full)
     resid_norm_grad, gain_two_grad = norm_back(resid, factor_two, gain_two, normed_two_grad)
@@ -751,6 +739,20 @@
     query_grad, key_part, value_part = attend_backward(
         kpos, cosine, sine, qkv, pairs, mixed_grad
     )
+    forth = hop_core(after(partial, normed_two_grad))
+    for stage in stages:
+        forth = hop_slow(forth, stage)
+    forth = hop_last(lax.optimization_barrier((*forth, query_grad))[:2])
+    layer_out = jnp.where(keep, resid + forth, 0.0).astype(low)
+    layer_out = layer_out.reshape(slot_count, rows, width)
+
+    blocks = units_line.reshape(INNER, share, 2 * ff_pad)
+    sent = jnp.stack([to_place(blocks, inner_here ^ d) for d in range(INNER)])
+    gate_out, up_out = join_units(
+        info, gather_hops(inner_exchange(sent), seq_hops), outer, ff_own
+    )
+    down_out = seq_gather(after(down_line, query_grad))
+    down_out = down_out.reshape(seq_count * ff_own, width).astype(full)
     pair_part = jnp.concatenate([key_part, value_part], axis=1)
     pair_sum = reduce_hops(
         pair_part.reshape(seq_count, rows, 2 * pair_width).astype(low), seq_hops

time: 967 us -> 969 us (level)
  waiting for transfers between devices: 253 us -> 307 us
  other arithmetic: 130 us -> 116 us
  Pallas kernels: 146 us -> 133 us
  starting transfers between devices: 47.6 us -> 34.7 us
  local copies, waits for them, and re-layouts: 115 us -> 104 us
    reduce_scatter x4, waiting for transfers between devices: 4 us -> 40.7 us  [line_reduce(): lax.psum_scatter(value, 'wt', scatter_dimension=0, axis_index_groups=line...]
    all_gather x2, waiting for transfers between devices: 6.78 us -> 28.6 us  [line_gather(): lax.all_gather(value, 'wt', axis=0, axis_index_groups=line, tiled=False)]
    another operation x20, other arithmetic: 32.4 us -> 11.8 us  [the longest x6 7.72 us: spread(): near = jnp.stack([part_a, part_b]).reshape(near_rows, width)]
    convert_element_type x1 -> x3, other arithmetic: 2.33 us -> 20.3 us  [the longest x2 17.9 us: hop_core(): near = (partial[:near_rows].astype(full) + other.astype(full)).astype(low)]
    concatenate x10 -> x7, other arithmetic: 23.1 us -> 5.71 us  [gather_hops(): held = jnp.concatenate([held, swap(held, hop)], axis=0)]
    pallas_call x1, Pallas kernels: 80.5 us -> 67.6 us  [gather_project(): pl.pallas_call(functools.partial(gather_kernel, outer, seq_count), in_spe...]
    ppermute x42 -> x38, starting transfers between devices: 41.1 us -> 28.7 us  [swap(): return lax.ppermute(value, axis, [(i, i ^ bit) for i in range(count)])]
    convert_element_type x16 -> x12, other arithmetic: 27 us -> 15.5 us  [reduce_hop(): return (held[:half].astype(full) + other.astype(full)).astype(low)]
  transfers between devices with their start and end apart: 54 -> 50, of which waited for: 23 -> 26; matrix products, arithmetic and copies ran while one was open for 38% -> 35% of each run, Pallas kernels for 14% -> 13%
where the time goes in v1:
time: 969 us; the launch traced here: 961 us
  waiting for transfers between devices  307 us (32%)
  matrix products  221 us (23%)
  Pallas kernels  133 us (14%)
  other arithmetic  116 us (12%)
  local copies, waits for them, and re-layouts  104 us (11%)
  between operations  47 us (5%)
  starting transfers between devices  34.7 us (4%)
    ppermute x38, waiting for transfers between devices, swap(): return lax.ppermute(value, axis, [(i, i ^ bit) for i in range(count)])  219 us
    dot_general x4, matrix products, product_right(): lax.dot_general(left, right, (((1,), (1,)), ((), ())), preferred_element_...  85.8 us
    dot_general x4, matrix products, product_left(): lax.dot_general(left, right, (((0,), (0,)), ((), ())), preferred_element_...  69.9 us
    pallas_call x1, Pallas kernels, gather_project(): pl.pallas_call(functools.partial(gather_kernel, outer, seq_count), in_spe...  67.6 us
    dot_general x3, matrix products, product(): return jnp.dot(left, right, preferred_element_type=full)  65.1 us
    reduce_scatter x4, waiting for transfers between devices, line_reduce(): lax.psum_scatter(value, 'wt', scatter_dimension=0, axis_index_groups=line...  40.7 us
    pallas_call x1, Pallas kernels, attend_backward(): pl.pallas_call(bwd_kernel, grid=(HEADS,), in_specs=[pl.BlockSpec((1, keys...  30.9 us
    ppermute x38, starting transfers between devices, swap(): return lax.ppermute(value, axis, [(i, i ^ bit) for i in range(count)])  28.7 us
  transfers between devices with their start and end apart: 50, of which 26 were waited for; matrix products, arithmetic and copies ran while one was open for 35% of the time, Pallas kernels for 13%

profile of v1, /device:TPU:0, one launch (start us, length us, event | category | flops | bytes accessed | tf_op | source)
XLA Modules:
  0.0 961.4 jit_solution(6185910192275955771)
XLA Ops:
  7.8 5.3 split_units.1
  33.0 67.6 %gather_project.1 = (bf16[512,1536]{1,0:T(8,128)(2,1)S(1)}, bf16[512,2048]{1,0:T(8,128)(2,1)}, f32[8,2048]{1,0:T(8,128)S(1)}, bf16[4,4,96,2048]{3,2,1,0:T(8,128)(2,1)}, bf16[4,4,96,1536]{3,2,1,0:T(8,128)(2,1)}) custom-call(bf16[512,1536]{1,0:T(8,128)(2,1)S(1)} %bitcast.227, bf16[96,2048]{1,0:T(8,128)(2,1)S(1)} %pad_maximum_fusion.25.p_ref, ...), custom_call_target="tpu_custom_call" | custom-call | flops 25769803776 | bytes 22020096 | tf_op jit(solution)/shard_map/gather_project/pallas_call | solution.py:360
  109.9 7.5 collective-permute-done
  119.8 22.8 %attend_forward.1 = bf16[512,1536]{1,0:T(8,128)(2,1)} custom-call(s32[1,1024]{1,0:T(1,128)} %compare_select_fusion.kpos_ref, bf16[512,2048]{1,0:T(8,128)(2,1)} %get-tuple-element.32.q_ref, bf16[1024,512]{1,0:T(8,128)(2,1)} %bitcast.246, bf16[1024,512]{1,0:T(8,128)(2,1)} %bitcast.247), custom_call_target="tpu_custom_call" | custom-call | flops 9663676416 | bytes 4194304 | tf_op jit(solution)/shard_map/attend_forward/pallas_call | solution.py:474
  142.6 6.0 multiply_reduce_fusion.2
  152.3 18.2 %collective-permute-done.1 = bf16[1,256,1536]{2,1,0:T(8,128)(2,1)S(1)} collective-permute-done((bf16[1,256,1536]{2,1,0:T(8,128)(2,1)S(1)}, bf16[1,256,1536]{2,1,0:T(8,128)(2,1)S(1)}, u32[]{:S(2)}, u32[]{:S(2)}) %collective-permute-start.1) | collective-permute-done | bytes 786464 | tf_op jit(solution)/shard_map/ppermute | solution.py:55
  172.9 34.5 %collective-permute-done.2 = bf16[2,256,1536]{2,1,0:T(8,128)(2,1)S(1)} collective-permute-done((bf16[2,256,1536]{2,1,0:T(8,128)(2,1)S(1)}, bf16[2,256,1536]{2,1,0:T(8,128)(2,1)S(1)}, u32[]{:S(2)}, u32[]{:S(2)}) %collective-permute-start.2) | collective-permute-done | bytes 1572896 | tf_op jit(solution)/shard_map/ppermute | solution.py:55
  208.5 3.3 pad_maximum_fusion.5
  214.4 17.9 %collective-permute-done.9 = bf16[1,256,1536]{2,1,0:T(8,128)(2,1)S(1)} collective-permute-done((bf16[1,256,1536]{2,1,0:T(8,128)(2,1)S(1)}, bf16[1,256,1536]{2,1,0:T(8,128)(2,1)S(1)}, u32[]{:S(2)}, u32[]{:S(2)}) %collective-permute-start.9) | collective-permute-done | bytes 786464 | tf_op jit(solution)/shard_map/ppermute | solution.py:55
  234.8 33.8 %collective-permute-done.10 = bf16[2,256,1536]{2,1,0:T(8,128)(2,1)S(1)} collective-permute-done((bf16[2,256,1536]{2,1,0:T(8,128)(2,1)S(1)}, bf16[2,256,1536]{2,1,0:T(8,128)(2,1)S(1)}, u32[]{:S(2)}, u32[]{:S(2)}) %collective-permute-start.10) | collective-permute-done | bytes 1572896 | tf_op jit(solution)/shard_map/ppermute | solution.py:55
  270.1 3.2 pad_maximum_fusion.6
  274.6 38.2 %fusion.42 = f32[4096,2304]{0,1:T(8,128)} fusion(bf16[1536,2304]{1,0:T(8,128)(2,1)} %bitcast.255, bf16[2048,1536]{1,0:T(8,128)(2,1)} %collective-permute-done.5, bf16[2048,1536]{1,0:T(8,128)(2,1)} %bitcast.14), kind=kOutput, calls=%fused_computation.236 | convolution fusion | flops 29016195072 | bytes 57409536 | tf_op jit(solution)/shard_map/dot_general | solution.py:28
  312.8 28.6 %all-gather.6.cloned.1.call-done = bf16[1120,1536]{1,0:T(8,128)(2,1)} async-done(((bf16[280,1536]{1,0:T(8,128)(2,1)}), bf16[1120,1536]{1,0:T(8,128)(2,1)}) %all-gather.6.cloned.1.call-update) | async-done | bytes 3440656 | tf_op jit(solution)/shard_map/all_gather | solution.py:601
  341.4 36.5 %multiply_convert_fusion.1 = (bf16[4096,1152]{0,1:T(8,128)(2,1)}, bf16[4096,1152]{0,1:T(8,128)(2,1)}, bf16[4096,1152]{0,1:T(8,128)(2,1)}) fusion(f32[4096,2304]{0,1:T(8,128)} %fusion.42, bf16[1120,1536]{1,0:T(8,128)(2,1)} %all-gather.6.cloned.1.call-done, bf16[2048,1536]{1,0:T(8,128)(2,1)} %collective-permute-done.13, bf16[2048,1536]{1,0:T(8,128)(2,1)} %bitcast.30), kind=kOutput, calls=%fused_computation.2 | convolution fusion | flops 14596177920 | bytes 82083840 | tf_op jit(solution)/shard_map/dot_general | solution.py:36
  377.9 36.7 %convolution_convert_fusion.1 = bf16[4096,1536]{1,0:T(8,128)(2,1)} fusion(bf16[1536,2304]{1,0:T(8,128)(2,1)} %bitcast.256, bf16[4096,1152]{0,1:T(8,128)(2,1)} %get-tuple-element.57, bf16[4096,1152]{0,1:T(8,128)(2,1)} %get-tuple-element.56), kind=kOutput, calls=%fused_computation.6 | convolution fusion | flops 29035069440 | bytes 38535168 | tf_op jit(solution)/shard_map/dot_general | solution.py:36
  414.6 3.2 slice.399
  417.8 10.3 %collective-permute-done.14 = bf16[2048,1536]{1,0:T(8,128)(2,1)} collective-permute-done((bf16[2048,1536]{1,0:T(8,128)(2,1)S(1)}, bf16[2048,1536]{1,0:T(8,128)(2,1)}, u32[]{:S(2)}, u32[]{:S(2)}) %collective-permute-start.14) | collective-permute-done | bytes 6291488 | tf_op jit(solution)/shard_map/ppermute | solution.py:55
  428.1 8.9 add_convert_fusion.1
  437.0 5.2 fusion.44
  488.4 20.2 %fusion = bf16[1152,1536]{1,0:T(8,128)(2,1)S(1)} fusion(bf16[4096,1152]{0,1:T(8,128)(2,1)} %get-tuple-element.38, bf16[2048,1536]{1,0:T(8,128)(2,1)} %collective-permute-done.13, bf16[2048,1536]{1,0:T(8,128)(2,1)} %bitcast.30), kind=kOutput, calls=%fused_computation.12 | convolution fusion | flops 14520680448 | bytes 25559040 | tf_op jit(solution)/shard_map/dot_general | solution.py:32
  517.7 3.8 convolution_convert_fusion.5.g_ref
  521.5 4.4 convolution_convert_fusion.3
  525.9 30.9 %attend_backward.1 = (bf16[512,1536]{1,0:T(8,128)(2,1)}, f32[1024,256]{1,0:T(8,128)}, f32[1024,256]{1,0:T(8,128)}) custom-call(s32[1,1024]{1,0:T(1,128)} %compare_select_fusion.kpos_ref, f32[512,128]{1,0:T(8,128)} %copy-done.4, f32[512,128]{1,0:T(8,128)} %copy-done.6, bf16[512,2048]{1,0:T(8,128)(2,1)} %get-tuple-element.32.q_ref, ...), custom_call_target="tpu_custom_call" | custom-call | flops 24159191040 | bytes 9437184 | tf_op jit(solution)/shard_map/attend_backward/pallas_call | solution.py:542
  556.8 10.5 %reshape_reshape.3 = bf16[4,4,96,2,2,384]{5,4,3,2,1,0:T(2,128)(2,1)} reshape(bf16[1536,1536]{1,0:T(8,128)(2,1)} %convolution_convert_fusion.3) | data formatting | bytes 9437184 | tf_op jit(solution)/shard_map/reshape;reshape | solution.py:611
  567.3 11.7 %fusion.45 = (bf16[4,4,96,2,1,384]{5,4,3,2,1,0:T(2,128)(2,1)S(1)}, bf16[4,4,96,2,1,384]{5,4,3,2,1,0:T(2,128)(2,1)S(1)}) fusion(bf16[4,4,96,2,2,384]{5,4,3,2,1,0:T(2,128)(2,1)} %reshape_reshape.3), kind=kLoop, calls=%fused_computation.239 | loop fusion | bytes 9437184 | tf_op jit(solution)/shard_map/slice | solution.py:614
  588.1 6.3 collective-permute-done.24
  603.1 8.9 fusion.11
  615.2 6.9 convolution_convert_fusion.4
  622.0 11.3 %concatenate.143 = bf16[4,4,96,2,2,512]{5,4,3,2,1,0:T(2,128)(2,1)} reshape(bf16[1536,2048]{1,0:T(8,128)(2,1)} %convolution_convert_fusion.4) | data formatting | bytes 12582912 | tf_op jit(solution)/shard_map/concatenate | solution.py:796
  633.3 4.6 copy_dynamic-update-slice_fusion
  646.3 10.4 %pad_maximum_fusion.1 = bf16[4096,1536]{1,0:T(8,128)(2,1)} fusion(bf16[2048,1536]{1,0:T(8,128)(2,1)} %collective-permute-done.5, bf16[2048,1536]{1,0:T(8,128)(2,1)} %bitcast.14), kind=kLoop, calls=%fused_computation.7 | loop fusion | flops 25165824 | bytes 25165824 | tf_op jit(solution)/shard_map/concatenate | solution.py:692
  672.9 15.3 %collective-permute-done.26 = bf16[2,4,104,512]{3,2,1,0:T(8,128)(2,1)} collective-permute-done((bf16[2,4,104,512]{3,2,1,0:T(8,128)(2,1)}, bf16[2,4,104,512]{3,2,1,0:T(8,128)(2,1)}, u32[]{:S(2)}, u32[]{:S(2)}) %collective-permute-start.26) | collective-permute-done | bytes 852000 | tf_op jit(solution)/shard_map/ppermute | solution.py:55
  695.1 14.9 %pad_maximum_fusion = bf16[4096,2304]{0,1:T(8,128)(2,1)} fusion(bf16[4096,1152]{0,1:T(8,128)(2,1)} %get-tuple-element.57, bf16[4096,1152]{0,1:T(8,128)(2,1)} %get-tuple-element.56), kind=kLoop, calls=%fused_computation | loop fusion | flops 37748736 | bytes 37748736 | tf_op jit(solution)/shard_map/concatenate | solution.py:717
  711.3 38.5 %convolution_convert_fusion.2 = bf16[1536,2304]{1,0:T(8,128)(2,1)} fusion(bf16[4096,1536]{1,0:T(8,128)(2,1)} %pad_maximum_fusion.1, bf16[4096,2304]{0,1:T(8,128)(2,1)} %pad_maximum_fusion), kind=kOutput, calls=%fused_computation.11 | convolution fusion | flops 28994568192 | bytes 38535168 | tf_op jit(solution)/shard_map/dot_general | solution.py:32
  749.8 20.9 %convolution_convert_fusion = bf16[4096,1536]{1,0:T(8,128)(2,1)S(1)} fusion(bf16[4096,1152]{0,1:T(8,128)(2,1)} %get-tuple-element.38, bf16[1120,1536]{1,0:T(8,128)(2,1)} %all-gather.6.cloned.1.call-done), kind=kOutput, calls=%fused_computation.5 | convolution fusion | flops 14501806080 | bytes 25460736 | tf_op jit(solution)/shard_map/dot_general | solution.py:28
  770.7 3.4 slice.334
  777.2 4.9 fusion.19
  782.1 16.8 %collective-permute-done.43 = bf16[1,280,1536]{2,1,0:T(8,128)(2,1)S(1)} collective-permute-done((bf16[1,280,1536]{2,1,0:T(8,128)(2,1)}, bf16[1,280,1536]{2,1,0:T(8,128)(2,1)S(1)}, u32[]{:S(2)}, u32[]{:S(2)}) %collective-permute-start.43) | collective-permute-done | bytes 860192 | tf_op jit(solution)/shard_map/ppermute | solution.py:55
  802.4 3.1 collective-permute-done.38
  808.1 3.9 collective-permute-done.31
  812.1 9.0 add_convert_fusion
  821.1 5.1 fusion.43
  828.7 40.7 %reduce-scatter.9.cloned.1.call-done = bf16[1,384,2304]{2,1,0:T(8,128)(2,1)} async-done(((bf16[4,384,2304]{2,1,0:T(8,128)(2,1)}), bf16[1,384,2304]{2,1,0:T(8,128)(2,1)}) %reduce-scatter.9.cloned.1.call-update) | async-done | bytes 1769488 | tf_op jit(solution)/shard_map/reduce_scatter | solution.py:604
  874.5 9.0 collective-permute-done.41
  883.5 9.5 collective-permute-done.40
  901.2 33.6 %collective-permute-done.42 = bf16[1,4,96,2304]{3,2,1,0:T(8,128)(2,1)S(1)} collective-permute-done((bf16[1,4,96,2304]{3,2,1,0:T(8,128)(2,1)S(1)}, bf16[1,4,96,2304]{3,2,1,0:T(8,128)(2,1)S(1)}, u32[]{:S(2)}, u32[]{:S(2)}) %collective-permute-start.42) | collective-permute-done | bytes 1769504 | tf_op jit(solution)/shard_map/ppermute | solution.py:55
  936.9 6.2 join_units.1
  944.6 6.3 collective-permute-done.23
  (358 shorter events, 155.8 us)
Async XLA Ops:
  7.2 267.4 %all-gather.4.cloned.1.call-start = ((), (), s32[]{:S(2)}) async-start(), calls=%async_computation.4 | async-start | bytes 8847360 | tf_op jit(solution)/shard_map/all_gather | solution.py:601
  15.9 90.6 %collective-permute-start.6 = (bf16[96,2304]{1,0:T(8,128)(2,1)}, bf16[96,2304]{1,0:T(8,128)(2,1)}, u32[]{:S(2)}, u32[]{:S(2)}) collective-permute-start(bf16[96,2304]{1,0:T(8,128)(2,1)} %get-tuple-element.114), channel_id=1, source_target_pairs={{0,2},{2,0},{4,6},{6,4},{8,10},{10,8},{12,14},{14,12},{16,18},{18,... | collective-permute-start | bytes 1327112 | tf_op jit(solution)/shard_map/ppermute | solution.py:639
  16.4 90.1 %collective-permute-start.7 = (bf16[96,2304]{1,0:T(8,128)(2,1)}, bf16[96,2304]{1,0:T(8,128)(2,1)}, u32[]{:S(2)}, u32[]{:S(2)}) collective-permute-start(bf16[96,2304]{1,0:T(8,128)(2,1)} %get-tuple-element.113), channel_id=1, source_target_pairs={{0,4},{2,6},{4,0},{6,2},{8,12},{10,14},{12,8},{14,10},{16,20},{18,... | collective-permute-start | bytes 1327112 | tf_op jit(solution)/shard_map/ppermute | solution.py:639
  18.8 87.6 %collective-permute-start.8 = (bf16[96,2304]{1,0:T(8,128)(2,1)}, bf16[96,2304]{1,0:T(8,128)(2,1)}, u32[]{:S(2)}, u32[]{:S(2)}) collective-permute-start(bf16[96,2304]{1,0:T(8,128)(2,1)} %get-tuple-element.112), channel_id=1, source_target_pairs={{0,6},{2,4},{4,2},{6,0},{8,14},{10,12},{12,10},{14,8},{16,22},{18,... | collective-permute-start | bytes 1327112 | tf_op jit(solution)/shard_map/ppermute | solution.py:639
  103.6 13.8 %collective-permute-start = (bf16[1,512,512]{2,1,0:T(8,128)(2,1)}, bf16[1,512,512]{2,1,0:T(8,128)(2,1)}, u32[]{:S(2)}, u32[]{:S(2)}) collective-permute-start(bf16[1,512,512]{2,1,0:T(8,128)(2,1)} %slice_bitcast_fusion.12), channel_id=1, source_target_pairs={{0,1},{1,0},{2,3},{3,2},{4,5},{5,4},{6,7},{7,6},{8,9},{9,8},{10,11... | collective-permute-start | bytes 1572872 | tf_op jit(solution)/shard_map/ppermute | solution.py:55
  109.7 231.7 %all-gather.6.cloned.1.call-start = ((), (), s32[]{:S(2)}) async-start(), calls=%async_computation.9 | async-start | bytes 4300800 | tf_op jit(solution)/shard_map/all_gather | solution.py:601
  150.3 20.2 %collective-permute-start.1 = (bf16[1,256,1536]{2,1,0:T(8,128)(2,1)S(1)}, bf16[1,256,1536]{2,1,0:T(8,128)(2,1)S(1)}, u32[]{:S(2)}, u32[]{:S(2)}) collective-permute-start(bf16[1,256,1536]{2,1,0:T(8,128)(2,1)S(1)} %get-tuple-element.119), channel_id=1, source_target_pairs={{0,4},{2,6},{4,0},{6,2},{8,12},{10,14},{12,8},{14,10},{16,20},{18,... | collective-permute-start | bytes 2359304 | tf_op jit(solution)/shard_map/ppermute | solution.py:55
  151.1 20.3 %collective-permute-start.3 = (bf16[1,256,1536]{2,1,0:T(8,128)(2,1)S(1)}, bf16[1,256,1536]{2,1,0:T(8,128)(2,1)S(1)}, u32[]{:S(2)}, u32[]{:S(2)}) collective-permute-start(bf16[1,256,1536]{2,1,0:T(8,128)(2,1)S(1)} %get-tuple-element.120), channel_id=1, source_target_pairs={{0,1},{1,0},{2,3},{3,2},{4,5},{5,4},{6,7},{7,6},{8,9},{9,8},{10,11... | collective-permute-start | bytes 2359304 | tf_op jit(solution)/shard_map/ppermute | solution.py:55
  170.6 36.8 %collective-permute-start.2 = (bf16[2,256,1536]{2,1,0:T(8,128)(2,1)S(1)}, bf16[2,256,1536]{2,1,0:T(8,128)(2,1)S(1)}, u32[]{:S(2)}, u32[]{:S(2)}) collective-permute-start(bf16[2,256,1536]{2,1,0:T(8,128)(2,1)S(1)} %pad_maximum_fusion.15), channel_id=1, source_target_pairs={{0,1},{1,0},{2,3},{3,2},{4,5},{5,4},{6,7},{7,6},{8,9},{9,8},{10,11... | collective-permute-start | bytes 4718600 | tf_op jit(solution)/shard_map/ppermute | solution.py:55
  171.5 36.7 %collective-permute-start.4 = (bf16[2,256,1536]{2,1,0:T(8,128)(2,1)S(1)}, bf16[2,256,1536]{2,1,0:T(8,128)(2,1)S(1)}, u32[]{:S(2)}, u32[]{:S(2)}) collective-permute-start(bf16[2,256,1536]{2,1,0:T(8,128)(2,1)S(1)} %pad_maximum_fusion.16), channel_id=1, source_target_pairs={{0,4},{2,6},{4,0},{6,2},{8,12},{10,14},{12,8},{14,10},{16,20},{18,... | collective-permute-start | bytes 4718600 | tf_op jit(solution)/shard_map/ppermute | solution.py:55
  211.8 62.8 %collective-permute-start.5 = (bf16[2048,1536]{1,0:T(8,128)(2,1)}, bf16[2048,1536]{1,0:T(8,128)(2,1)}, u32[]{:S(2)}, u32[]{:S(2)}) collective-permute-start(bf16[2048,1536]{1,0:T(8,128)(2,1)} %bitcast.14), channel_id=1, source_target_pairs={{0,2},{2,0},{4,6},{6,4},{8,10},{10,8},{12,14},{14,12},{16,18},{18,... | collective-permute-start | bytes 18874376 | tf_op jit(solution)/shard_map/ppermute | solution.py:55
  212.4 20.0 %collective-permute-start.9 = (bf16[1,256,1536]{2,1,0:T(8,128)(2,1)S(1)}, bf16[1,256,1536]{2,1,0:T(8,128)(2,1)S(1)}, u32[]{:S(2)}, u32[]{:S(2)}) collective-permute-start(bf16[1,256,1536]{2,1,0:T(8,128)(2,1)S(1)} %get-tuple-element.117), channel_id=1, source_target_pairs={{0,4},{2,6},{4,0},{6,2},{8,12},{10,14},{12,8},{14,10},{16,20},{18,... | collective-permute-start | bytes 2359304 | tf_op jit(solution)/shard_map/ppermute | solution.py:55
  213.5 20.2 %collective-permute-start.11 = (bf16[1,256,1536]{2,1,0:T(8,128)(2,1)S(1)}, bf16[1,256,1536]{2,1,0:T(8,128)(2,1)S(1)}, u32[]{:S(2)}, u32[]{:S(2)}) collective-permute-start(bf16[1,256,1536]{2,1,0:T(8,128)(2,1)S(1)} %get-tuple-element.118), channel_id=1, source_target_pairs={{0,1},{1,0},{2,3},{3,2},{4,5},{5,4},{6,7},{7,6},{8,9},{9,8},{10,11... | collective-permute-start | bytes 2359304 | tf_op jit(solution)/shard_map/ppermute | solution.py:55
  232.5 36.1 %collective-permute-start.10 = (bf16[2,256,1536]{2,1,0:T(8,128)(2,1)S(1)}, bf16[2,256,1536]{2,1,0:T(8,128)(2,1)S(1)}, u32[]{:S(2)}, u32[]{:S(2)}) collective-permute-start(bf16[2,256,1536]{2,1,0:T(8,128)(2,1)S(1)} %pad_maximum_fusion.17), channel_id=1, source_target_pairs={{0,1},{1,0},{2,3},{3,2},{4,5},{5,4},{6,7},{7,6},{8,9},{9,8},{10,11... | collective-permute-start | bytes 4718600 | tf_op jit(solution)/shard_map/ppermute | solution.py:55
  233.9 35.9 %collective-permute-start.12 = (bf16[2,256,1536]{2,1,0:T(8,128)(2,1)S(1)}, bf16[2,256,1536]{2,1,0:T(8,128)(2,1)S(1)}, u32[]{:S(2)}, u32[]{:S(2)}) collective-permute-start(bf16[2,256,1536]{2,1,0:T(8,128)(2,1)S(1)} %pad_maximum_fusion.18), channel_id=1, source_target_pairs={{0,4},{2,6},{4,0},{6,2},{8,12},{10,14},{12,8},{14,10},{16,20},{18,... | collective-permute-start | bytes 4718600 | tf_op jit(solution)/shard_map/ppermute | solution.py:55
  273.3 68.1 %collective-permute-start.13 = (bf16[2048,1536]{1,0:T(8,128)(2,1)}, bf16[2048,1536]{1,0:T(8,128)(2,1)}, u32[]{:S(2)}, u32[]{:S(2)}) collective-permute-start(bf16[2048,1536]{1,0:T(8,128)(2,1)} %bitcast.30), channel_id=1, source_target_pairs={{0,2},{2,0},{4,6},{6,4},{8,10},{10,8},{12,14},{14,12},{16,18},{18,... | collective-permute-start | bytes 18874376 | tf_op jit(solution)/shard_map/ppermute | solution.py:55
  274.3 502.9 %reduce-scatter.11.cloned.1.call-start = ((), (), s32[]{:S(2)}) async-start(), calls=%async_computation.8 | async-start | bytes 4300800 | tf_op jit(solution)/shard_map/reduce_scatter | solution.py:604
  417.8 10.4 %collective-permute-start.14 = (bf16[2048,1536]{1,0:T(8,128)(2,1)S(1)}, bf16[2048,1536]{1,0:T(8,128)(2,1)}, u32[]{:S(2)}, u32[]{:S(2)}) collective-permute-start(bf16[2048,1536]{1,0:T(8,128)(2,1)S(1)} %slice.399), channel_id=1, source_target_pairs={{0,2},{2,0},{4,6},{6,4},{8,10},{10,8},{12,14},{14,12},{16,18},{18,... | collective-permute-start | bytes 18874376 | tf_op jit(solution)/shard_map/ppermute | solution.py:55
  442.3 36.8 %collective-permute-start.15 = (bf16[2,256,1536]{2,1,0:T(8,128)(2,1)}, bf16[2,256,1536]{2,1,0:T(8,128)(2,1)}, u32[]{:S(2)}, u32[]{:S(2)}) collective-permute-start(bf16[2,256,1536]{2,1,0:T(8,128)(2,1)} %bitcast.32), channel_id=1, source_target_pairs={{0,1},{1,0},{2,3},{3,2},{4,5},{5,4},{6,7},{7,6},{8,9},{9,8},{10,11... | collective-permute-start | bytes 4718600 | tf_op jit(solution)/shard_map/ppermute | solution.py:55
  443.7 40.0 %collective-permute-start.16 = (bf16[2,256,1536]{2,1,0:T(8,128)(2,1)}, bf16[2,256,1536]{2,1,0:T(8,128)(2,1)}, u32[]{:S(2)}, u32[]{:S(2)}) collective-permute-start(bf16[2,256,1536]{2,1,0:T(8,128)(2,1)} %bitcast.34), channel_id=1, source_target_pairs={{0,4},{2,6},{4,0},{6,2},{8,12},{10,14},{12,8},{14,10},{16,20},{18,... | collective-permute-start | bytes 4718600 | tf_op jit(solution)/shard_map/ppermute | solution.py:55
  482.3 28.5 %collective-permute-start.17 = (bf16[256,1536]{1,0:T(8,128)(2,1)}, bf16[256,1536]{1,0:T(8,128)(2,1)}, u32[]{:S(2)}, u32[]{:S(2)}) collective-permute-start(bf16[256,1536]{1,0:T(8,128)(2,1)} %slice_bitcast_fusion.4), channel_id=1, source_target_pairs={{0,4},{2,6},{4,0},{6,2},{8,12},{10,14},{12,8},{14,10},{16,20},{18,... | collective-permute-start | bytes 2359304 | tf_op jit(solution)/shard_map/ppermute | solution.py:55
  487.0 25.5 %collective-permute-start.18 = (bf16[256,1536]{1,0:T(8,128)(2,1)}, bf16[256,1536]{1,0:T(8,128)(2,1)}, u32[]{:S(2)}, u32[]{:S(2)}) collective-permute-start(bf16[256,1536]{1,0:T(8,128)(2,1)} %slice_bitcast_fusion.2), channel_id=1, source_target_pairs={{0,1},{1,0},{2,3},{3,2},{4,5},{5,4},{6,7},{7,6},{8,9},{9,8},{10,11... | collective-permute-start | bytes 2359304 | tf_op jit(solution)/shard_map/ppermute | solution.py:55
  510.7 289.0 %reduce-scatter.7.cloned.1.call-start = ((), (), s32[]{:S(2)}) async-start(), calls=%async_computation.6 | async-start | bytes 737280 | tf_op jit(solution)/shard_map/reduce_scatter | solution.py:604
  581.5 12.9 %collective-permute-start.24 = (bf16[512,512]{1,0:T(8,128)(2,1)}, bf16[512,512]{1,0:T(8,128)(2,1)}, u32[]{:S(2)}, u32[]{:S(2)}) collective-permute-start(bf16[512,512]{1,0:T(8,128)(2,1)} %pad_maximum_fusion.24), channel_id=1, source_target_pairs={{0,1},{1,0},{2,3},{3,2},{4,5},{5,4},{6,7},{7,6},{8,9},{9,8},{10,11... | collective-permute-start | bytes 1572872 | tf_op jit(solution)/shard_map/ppermute | solution.py:55
  584.5 57.3 %collective-permute-start.32 = (bf16[4,4,96,384]{3,2,1,0:T(8,128)(2,1)}, bf16[4,4,96,384]{3,2,1,0:T(8,128)(2,1)}, u32[]{:S(2)}, u32[]{:S(2)}) collective-permute-start(bf16[4,4,96,384]{3,2,1,0:T(8,128)(2,1)} %pad_maximum_fusion.19), channel_id=1, source_target_pairs={{0,2},{2,0},{4,6},{6,4},{8,10},{10,8},{12,14},{14,12},{16,18},{18,... | collective-permute-start | bytes 3538952 | tf_op jit(solution)/shard_map/ppermute | solution.py:55
  587.5 56.7 %collective-permute-start.35 = (bf16[4,4,96,384]{3,2,1,0:T(8,128)(2,1)}, bf16[4,4,96,384]{3,2,1,0:T(8,128)(2,1)}, u32[]{:S(2)}, u32[]{:S(2)}) collective-permute-start(bf16[4,4,96,384]{3,2,1,0:T(8,128)(2,1)} %pad_maximum_fusion.20), channel_id=1, source_target_pairs={{0,2},{2,0},{4,6},{6,4},{8,10},{10,8},{12,14},{14,12},{16,18},{18,... | collective-permute-start | bytes 3538952 | tf_op jit(solution)/shard_map/ppermute | solution.py:55
  640.2 23.9 %collective-permute-start.25 = (bf16[4,4,104,512]{3,2,1,0:T(8,128)(2,1)S(1)}, bf16[4,4,104,512]{3,2,1,0:T(8,128)(2,1)S(1)}, u32[]{:S(2)}, u32[]{:S(2)}) collective-permute-start(bf16[4,4,104,512]{3,2,1,0:T(8,128)(2,1)S(1)} %pad_maximum_fusion.13), channel_id=1, source_target_pairs={{0,2},{2,0},{4,6},{6,4},{8,10},{10,8},{12,14},{14,12},{16,18},{18,... | collective-permute-start | bytes 5111816 | tf_op jit(solution)/shard_map/ppermute | solution.py:55
  641.3 27.3 %collective-permute-start.28 = (bf16[4,4,104,512]{3,2,1,0:T(8,128)(2,1)S(1)}, bf16[4,4,104,512]{3,2,1,0:T(8,128)(2,1)S(1)}, u32[]{:S(2)}, u32[]{:S(2)}) collective-permute-start(bf16[4,4,104,512]{3,2,1,0:T(8,128)(2,1)S(1)} %pad_maximum_fusion.14), channel_id=1, source_target_pairs={{0,2},{2,0},{4,6},{6,4},{8,10},{10,8},{12,14},{14,12},{16,18},{18,... | collective-permute-start | bytes 5111816 | tf_op jit(solution)/shard_map/ppermute | solution.py:55
  643.8 15.8 %collective-permute-start.33 = (bf16[2,4,96,384]{3,2,1,0:T(8,128)(2,1)S(1)}, bf16[2,4,96,384]{3,2,1,0:T(8,128)(2,1)S(1)}, u32[]{:S(2)}, u32[]{:S(2)}) collective-permute-start(bf16[2,4,96,384]{3,2,1,0:T(8,128)(2,1)S(1)} %slice.441), channel_id=1, source_target_pairs={{0,1},{1,0},{2,3},{3,2},{4,5},{5,4},{6,7},{7,6},{8,9},{9,8},{10,11... | collective-permute-start | bytes 1769480 | tf_op jit(solution)/shard_map/ppermute | solution.py:55
  645.9 15.5 %collective-permute-start.36 = (bf16[2,4,96,384]{3,2,1,0:T(8,128)(2,1)S(1)}, bf16[2,4,96,384]{3,2,1,0:T(8,128)(2,1)S(1)}, u32[]{:S(2)}, u32[]{:S(2)}) collective-permute-start(bf16[2,4,96,384]{3,2,1,0:T(8,128)(2,1)S(1)} %slice.446), channel_id=1, source_target_pairs={{0,4},{2,6},{4,0},{6,2},{8,12},{10,14},{12,8},{14,10},{16,20},{18,... | collective-permute-start | bytes 1769480 | tf_op jit(solution)/shard_map/ppermute | solution.py:55
  659.8 8.6 collective-permute-start.34
  661.6 10.3 %collective-permute-start.37 = (bf16[4,96,384]{2,1,0:T(8,128)(2,1)S(1)}, bf16[4,96,384]{2,1,0:T(8,128)(2,1)S(1)}, u32[]{:S(2)}, u32[]{:S(2)}) collective-permute-start(bf16[4,96,384]{2,1,0:T(8,128)(2,1)S(1)} %slice_bitcast_fusion.20), channel_id=1, source_target_pairs={{0,1},{1,0},{2,3},{3,2},{4,5},{5,4},{6,7},{7,6},{8,9},{9,8},{10,11... | collective-permute-start | bytes 884744 | tf_op jit(solution)/shard_map/ppermute | solution.py:55
  665.6 22.7 %collective-permute-start.26 = (bf16[2,4,104,512]{3,2,1,0:T(8,128)(2,1)}, bf16[2,4,104,512]{3,2,1,0:T(8,128)(2,1)}, u32[]{:S(2)}, u32[]{:S(2)}) collective-permute-start(bf16[2,4,104,512]{3,2,1,0:T(8,128)(2,1)} %slice.424), channel_id=1, source_target_pairs={{0,1},{1,0},{2,3},{3,2},{4,5},{5,4},{6,7},{7,6},{8,9},{9,8},{10,11... | collective-permute-start | bytes 2555912 | tf_op jit(solution)/shard_map/ppermute | solution.py:55
  671.2 20.5 %collective-permute-start.29 = (bf16[2,4,104,512]{3,2,1,0:T(8,128)(2,1)}, bf16[2,4,104,512]{3,2,1,0:T(8,128)(2,1)}, u32[]{:S(2)}, u32[]{:S(2)}) collective-permute-start(bf16[2,4,104,512]{3,2,1,0:T(8,128)(2,1)} %slice.429), channel_id=1, source_target_pairs={{0,4},{2,6},{4,0},{6,2},{8,12},{10,14},{12,8},{14,10},{16,20},{18,... | collective-permute-start | bytes 2555912 | tf_op jit(solution)/shard_map/ppermute | solution.py:55
  672.9 132.7 %reduce-scatter.5.cloned.1.call-start = ((), (), s32[]{:S(2)}) async-start(), calls=%async_computation.5 | async-start | bytes 1064960 | tf_op jit(solution)/shard_map/reduce_scatter | solution.py:604
  689.7 20.2 %collective-permute-start.27 = (bf16[4,104,512]{2,1,0:T(8,128)(2,1)S(1)}, bf16[4,104,512]{2,1,0:T(8,128)(2,1)S(1)}, u32[]{:S(2)}, u32[]{:S(2)}) collective-permute-start(bf16[4,104,512]{2,1,0:T(8,128)(2,1)S(1)} %slice_bitcast_fusion.18), channel_id=1, source_target_pairs={{0,4},{2,6},{4,0},{6,2},{8,12},{10,14},{12,8},{14,10},{16,20},{18,... | collective-permute-start | bytes 1277960 | tf_op jit(solution)/shard_map/ppermute | solution.py:55
  693.1 16.9 %collective-permute-start.30 = (bf16[4,104,512]{2,1,0:T(8,128)(2,1)S(1)}, bf16[4,104,512]{2,1,0:T(8,128)(2,1)S(1)}, u32[]{:S(2)}, u32[]{:S(2)}) collective-permute-start(bf16[4,104,512]{2,1,0:T(8,128)(2,1)S(1)} %slice_bitcast_fusion.16), channel_id=1, source_target_pairs={{0,1},{1,0},{2,3},{3,2},{4,5},{5,4},{6,7},{7,6},{8,9},{9,8},{10,11... | collective-permute-start | bytes 1277960 | tf_op jit(solution)/shard_map/ppermute | solution.py:55
  711.2 158.1 %reduce-scatter.9.cloned.1.call-start = ((), (), s32[]{:S(2)}) async-start(), calls=%async_computation.7 | async-start | bytes 8847360 | tf_op jit(solution)/shard_map/reduce_scatter | solution.py:604
  777.2 34.9 %collective-permute-start.19 = (bf16[2048,1536]{1,0:T(8,128)(2,1)}, bf16[2048,1536]{1,0:T(8,128)(2,1)}, u32[]{:S(2)}, u32[]{:S(2)}) collective-permute-start(bf16[2048,1536]{1,0:T(8,128)(2,1)} %slice.334), channel_id=1, source_target_pairs={{0,2},{2,0},{4,6},{6,4},{8,10},{10,8},{12,14},{14,12},{16,18},{18,... | collective-permute-start | bytes 18874376 | tf_op jit(solution)/shard_map/ppermute | solution.py:55
  777.2 21.7 %collective-permute-start.43 = (bf16[1,280,1536]{2,1,0:T(8,128)(2,1)}, bf16[1,280,1536]{2,1,0:T(8,128)(2,1)S(1)}, u32[]{:S(2)}, u32[]{:S(2)}) collective-permute-start(bf16[1,280,1536]{2,1,0:T(8,128)(2,1)} %reduce-scatter.11.cloned.1.call-done), channel_id=1, source_target_pairs={{0,1},{1,0},{2,3},{3,2},{4,5},{5,4},{6,7},{7,6},{8,9},{9,8},{10,11... | collective-permute-start | bytes 2580488 | tf_op jit(solution)/shard_map/ppermute | solution.py:55
  826.2 68.6 %collective-permute-start.21 = (bf16[2,256,1536]{2,1,0:T(8,128)(2,1)}, bf16[2,256,1536]{2,1,0:T(8,128)(2,1)}, u32[]{:S(2)}, u32[]{:S(2)}) collective-permute-start(bf16[2,256,1536]{2,1,0:T(8,128)(2,1)} %bitcast.42), channel_id=1, source_target_pairs={{0,4},{2,6},{4,0},{6,2},{8,12},{10,14},{12,8},{14,10},{16,20},{18,... | collective-permute-start | bytes 4718600 | tf_op jit(solution)/shard_map/ppermute | solution.py:55
  827.8 68.8 %collective-permute-start.20 = (bf16[2,256,1536]{2,1,0:T(8,128)(2,1)}, bf16[2,256,1536]{2,1,0:T(8,128)(2,1)}, u32[]{:S(2)}, u32[]{:S(2)}) collective-permute-start(bf16[2,256,1536]{2,1,0:T(8,128)(2,1)} %bitcast.40), channel_id=1, source_target_pairs={{0,1},{1,0},{2,3},{3,2},{4,5},{5,4},{6,7},{7,6},{8,9},{9,8},{10,11... | collective-permute-start | bytes 4718600 | tf_op jit(solution)/shard_map/ppermute | solution.py:55
  871.0 12.5 %collective-permute-start.41 = (bf16[96,2304]{1,0:T(8,128)(2,1)S(1)}, bf16[96,2304]{1,0:T(8,128)(2,1)S(1)}, u32[]{:S(2)}, u32[]{:S(2)}) collective-permute-start(bf16[96,2304]{1,0:T(8,128)(2,1)S(1)} %get-tuple-element.104), channel_id=1, source_target_pairs={{0,6},{2,4},{4,2},{6,0},{8,14},{10,12},{12,10},{14,8},{16,22},{18,... | collective-permute-start | bytes 1327112 | tf_op jit(solution)/shard_map/ppermute | solution.py:639
  871.9 11.6 %collective-permute-start.39 = (bf16[96,2304]{1,0:T(8,128)(2,1)S(1)}, bf16[96,2304]{1,0:T(8,128)(2,1)S(1)}, u32[]{:S(2)}, u32[]{:S(2)}) collective-permute-start(bf16[96,2304]{1,0:T(8,128)(2,1)S(1)} %get-tuple-element.106), channel_id=1, source_target_pairs={{0,2},{2,0},{4,6},{6,4},{8,10},{10,8},{12,14},{14,12},{16,18},{18,... | collective-permute-start | bytes 1327112 | tf_op jit(solution)/shard_map/ppermute | solution.py:639
  872.7 20.4 %collective-permute-start.40 = (bf16[96,2304]{1,0:T(8,128)(2,1)S(1)}, bf16[96,2304]{1,0:T(8,128)(2,1)S(1)}, u32[]{:S(2)}, u32[]{:S(2)}) collective-permute-start(bf16[96,2304]{1,0:T(8,128)(2,1)S(1)} %get-tuple-element.105), channel_id=1, source_target_pairs={{0,4},{2,6},{4,0},{6,2},{8,12},{10,14},{12,8},{14,10},{16,20},{18,... | collective-permute-start | bytes 1327112 | tf_op jit(solution)/shard_map/ppermute | solution.py:639
  893.3 41.5 %collective-permute-start.42 = (bf16[1,4,96,2304]{3,2,1,0:T(8,128)(2,1)S(1)}, bf16[1,4,96,2304]{3,2,1,0:T(8,128)(2,1)S(1)}, u32[]{:S(2)}, u32[]{:S(2)}) collective-permute-start(bf16[1,4,96,2304]{3,2,1,0:T(8,128)(2,1)S(1)} %maximum_bitcast_fusion.4), channel_id=1, source_target_pairs={{0,1},{1,0},{2,3},{3,2},{4,5},{5,4},{6,7},{7,6},{8,9},{9,8},{10,11... | collective-permute-start | bytes 5308424 | tf_op jit(solution)/shard_map/ppermute | solution.py:55
  899.1 44.0 %collective-permute-start.22 = (bf16[256,1536]{1,0:T(8,128)(2,1)S(1)}, bf16[256,1536]{1,0:T(8,128)(2,1)}, u32[]{:S(2)}, u32[]{:S(2)}) collective-permute-start(bf16[256,1536]{1,0:T(8,128)(2,1)S(1)} %slice_bitcast_fusion.11), channel_id=1, source_target_pairs={{0,4},{2,6},{4,0},{6,2},{8,12},{10,14},{12,8},{14,10},{16,20},{18,... | collective-permute-start | bytes 2359304 | tf_op jit(solution)/shard_map/ppermute | solution.py:55
  900.6 50.3 %collective-permute-start.23 = (bf16[256,1536]{1,0:T(8,128)(2,1)S(1)}, bf16[256,1536]{1,0:T(8,128)(2,1)}, u32[]{:S(2)}, u32[]{:S(2)}) collective-permute-start(bf16[256,1536]{1,0:T(8,128)(2,1)S(1)} %slice_bitcast_fusion.10), channel_id=1, source_target_pairs={{0,1},{1,0},{2,3},{3,2},{4,5},{5,4},{6,7},{7,6},{8,9},{9,8},{10,11... | collective-permute-start | bytes 2359304 | tf_op jit(solution)/shard_map/ppermute | solution.py:55
  (65 other events, 789.3 us)
Sparse Core Ops, SparseCore 0:
  109.8 128.2 all-gather.3
  274.4 66.9 all-gather.5
  510.8 61.7 reduce-scatter.10
  673.0 19.9 reduce-scatter.6
  711.3 20.1 reduce-scatter.4
  749.9 119.4 reduce-scatter.8

commit v2 on v1

--- a/solution.py
+++ b/solution.py
@@ -14,7 +14,6 @@
 HEAD_DIM = 128
 SLOT = 1024
 INNER = 4
-EXTRA = 8
 
 epsilon = 1e-06
 masked_score = -1e30
@@ -87,26 +86,6 @@
     seq = bits_of("seq", seq_count)
     slow = inner[1:] + seq
     return (slow + inner[:1], slow[::-1] + inner[:1])
-
-
-def rank_of(hops):
-    place = jnp.int32(0)
-    for k, (axis, bit) in enumerate(hops):
-        here = (lax.axis_index(axis) // bit) % 2
-        place = place + here * (1 << k)
-    return place
-
-
-def plane_order(hops, count):
-    order = []
-    for inner in range(INNER):
-        for seq in range(count):
-            place = 0
-            for k, (axis, bit) in enumerate(hops):
-                source = inner if axis == "wt" else seq
-                place |= ((source // bit) % 2) << k
-            order.append(place)
-    return order
 
 
 def to_place(stacked, place):
@@ -386,6 +365,156 @@
     )(tokens, packed, w_out, small, cosine, sine)
 
 
+def near_inner(seq_count):
+    hops = plane_hops(seq_count)[0]
+    return sorted(set(a for a, _ in subsets(hops[:-1])))
+
+
+def reduce_kernel(outer, seq_count, count, *refs):
+    given, results = refs[:count], refs[count : 2 * count]
+    slow = len(plane_hops(seq_count)[0]) - 1
+    held = refs[2 * count : 3 * count]
+    lines = refs[3 * count : 4 * count]
+    joined = refs[4 * count : 5 * count]
+    landed = refs[5 * count : (6 + slow) * count]
+    send_sems, recv_sems = refs[(6 + slow) * count :]
+    wt, seq = lax.axis_index("wt"), lax.axis_index("seq")
+    line, inner = wt // INNER, wt % INNER
+    hops = plane_hops(seq_count)
+    nears = near_inner(seq_count)
+    peers = [(flip_all(line, d) * INNER + inner, seq) for d in range(1, outer)]
+    peers += [(wt - inner + flip(inner, bit), seq) for bit in inner_bits()]
+    peers += [(wt, flip_all(seq, d)) for d in range(1, seq_count)]
+    meet(peers)
+    out = Sender(send_sems, recv_sems)
+
+    def hop_peer(hop):
+        axis, bit = hop
+        if axis == "wt":
+            return (wt - inner + flip(inner, bit), seq)
+        return (wt, flip(seq, bit))
+
+    def columns(total, part, half):
+        wide = total // seq_count
+        first = -(-wide // 256) * 128
+        start = part * wide + half * first
+        return pl.ds(pl.multiple_of(start, 128), wide - first if half else first)
+
+    def arrive(copies):
+        for copy in copies:
+            copy.wait_recv()
+
+    def steps(k):
+        source, total = given[k], given[k].shape[3]
+        sums, wide = held[k], given[k].shape[3] // seq_count
+        own = pl.ds(pl.multiple_of(seq * wide, 128), wide)
+        core = hops[0][slow]
+        copies = [
+            out.start(
+                source.at[:, flip_all(inner, a ^ core[1])],
+                landed[k].at[:, at],
+                hop_peer(core),
+            )
+            for at, a in enumerate(nears)
+        ]
+        yield
+        arrive(copies)
+        for at, a in enumerate(nears):
+            place = flip_all(inner, a)
+
+            @pl.loop(0, outer)
+            def _(o):
+                both = source[o, place].astype(full) + landed[k][o, at].astype(full)
+                sums[o, at] = both.astype(low)
+
+        for stage in range(slow - 1, -1, -1):
+            target = landed[(1 + stage) * count + k]
+            copies, blocks = [], []
+            for half in range(2):
+                axis, bit = hops[half][stage]
+                for a, b in subsets(hops[half][:stage]):
+                    from_a = a ^ bit if axis == "wt" else a
+                    from_b = b ^ bit if axis == "seq" else b
+                    sent = columns(total, flip_all(seq, from_b), half)
+                    copies.append(
+                        out.start(
+                            sums.at[:, nears.index(from_a), :, sent],
+                            target.at[:, nears.index(a), :, sent],
+                            hop_peer((axis, bit)),
+                        )
+                    )
+                    blocks.append((nears.index(a), columns(total, flip_all(seq, b), half)))
+            yield
+            arrive(copies)
+            for at, part in blocks:
+
+                @pl.loop(0, outer)
+                def _(o):
+                    both = sums[o, at, :, part].astype(full) + target[o, at, :, part].astype(full)
+                    sums[o, at, :, part] = both.astype(low)
+
+        copies = [
+            out.start(
+                sums.at[flip_all(line, d), 0, :, own],
+                lines[k].at[d],
+                (flip_all(line, d) * INNER + inner, seq),
+            )
+            for d in range(1, outer)
+        ]
+        yield
+        arrive(copies)
+        both = sums[line, 0, :, own].astype(full)
+        for d in range(1, outer):
+            both = both + lines[k][d].astype(full)
+        joined[k][:, own] = both.astype(low)
+        copies = [
+            out.start(joined[k].at[:, own], joined[k].at[:, own], (wt, flip_all(seq, d)))
+            for d in range(1, seq_count)
+        ]
+        yield
+        arrive(copies)
+        results[k][...] = joined[k][...].astype(full)
+
+    running = [steps(k) for k in range(count)]
+    while running:
+        for one in list(running):
+            if next(one, "done") == "done":
+                running.remove(one)
+    for copy in out.copies:
+        copy.wait_send()
+
+
+def reduce_shares(*partials):
+    outer = lax.axis_size("wt") // INNER
+    seq_count = lax.axis_size("seq")
+    count = len(partials)
+    slow = len(plane_hops(seq_count)[0]) - 1
+    nears = len(near_inner(seq_count))
+    vmem = pl.BlockSpec(memory_space=pltpu.VMEM)
+    near = [
+        pltpu.VMEM((outer, nears) + p.shape[2:], low) for p in partials
+    ]
+    shapes = [p.shape[2:] for p in partials]
+    copies = count * (nears + 2 * (2**slow - 1) + outer - 1 + seq_count - 1)
+    sent = sum(2 * p.size for p in partials)
+    return pl.pallas_call(
+        functools.partial(reduce_kernel, outer, seq_count, count),
+        in_specs=[vmem] * count,
+        out_specs=[vmem] * count,
+        out_shape=[jax.ShapeDtypeStruct(shape, full) for shape in shapes],
+        scratch_shapes=near
+        + [pltpu.VMEM((outer, r, c // seq_count), low) for r, c in shapes]
+        + [pltpu.VMEM(shape, low) for shape in shapes]
+        + near * (1 + slow)
+        + [pltpu.SemaphoreType.DMA((copies,)), pltpu.SemaphoreType.DMA((copies,))],
+        compiler_params=pltpu.CompilerParams(
+            collective_id=2, has_side_effects=True, vmem_limit_bytes=60 << 20
+        ),
+        cost_estimate=pl.CostEstimate(flops=0, bytes_accessed=8 * sent, transcendentals=0),
+        name="reduce_shares",
+    )(*partials)
+
+
 def split_kernel(outer, seq_count, own, info_ref, gate_ref, up_ref, o_ref):
     inner = info_ref[1]
     width = outer * own
@@ -605,31 +734,9 @@
             value, "wt", scatter_dimension=0, axis_index_groups=line, tiled=False
         )
 
-    def reduce_weight(value):
-        count, wide = value.shape[1:]
-        half = wide // seq_count // 2
-        split = value.reshape(outer, INNER, count, seq_count, 2, half)
-        done = []
-        for k, hops in enumerate((hops_a, hops_b)):
-            piece = split[:, :, :, :, k].transpose(1, 3, 0, 2, 4)
-            piece = piece.reshape(plane, outer, count, half)
-            order = plane_order(hops, seq_count)
-            back = [order.index(p) for p in range(plane)]
-            table = jnp.asarray(back, dtype=jnp.int32)
-            me = rank_of(hops)
-            placed = [to_place(piece, table[me ^ p]) for p in range(plane)]
-            done.append(reduce_hops(jnp.stack(placed), hops))
-        lined = jnp.concatenate(done, axis=-1).astype(low)
-        mine = line_reduce(lined)
-        return seq_columns(mine)
-
     def seq_gather(value):
         stacked = gather_hops(value, bits_of("seq", seq_count))
         return jnp.stack([to_place(stacked, seq_here ^ p) for p in range(seq_count)])
-
-    def seq_columns(value):
-        got = seq_gather(value)
-        return got.transpose(1, 0, 2).reshape(value.shape[0], -1)
 
     info = jnp.stack([seq_here, inner_here]).astype(jnp.int32)
     down_own = lax.dynamic_slice_in_dim(w_down, seq_here * ff_own, ff_own, axis=0).astype(low)
@@ -705,7 +812,7 @@
         return jnp.concatenate(got, axis=0)
 
     stages = list(range(1, len(slow_a)))[::-1]
-    grad_all = spread(upstream_low)
+    grad_all = spread(after(upstream_low, pairs))
     rows_all = spread(normed_two_low)
     hidden_grad = product_right(grad_all, down_w)
     both = product(rows_all, units_w)
@@ -735,7 +842,6 @@
     attn_grad = resid_grad.astype(low)
     mixed_grad = product_right(attn_grad, out_w).astype(low)
     out_w_grad = product_left(mixed, attn_grad).astype(low)
-    out_w_out = reduce_weight(out_w_grad.reshape(wt_count, -1, width)).astype(full)
     query_grad, key_part, value_part = attend_backward(
         kpos, cosine, sine, qkv, pairs, mixed_grad
     )
@@ -751,7 +857,7 @@
     gate_out, up_out = join_units(
         info, gather_hops(inner_exchange(sent), seq_hops), outer, ff_own
     )
-    down_out = seq_gather(after(down_line, query_grad))
+    down_out = seq_gather(down_line)
     down_out = down_out.reshape(seq_count * ff_own, width).astype(full)
     pair_part = jnp.concatenate([key_part, value_part], axis=1)
     pair_sum = reduce_hops(
@@ -788,15 +894,16 @@
         ],
         axis=1,
     ).astype(low)
-    extra = jnp.pad(
-        small_grad[:, None, :],
-        ((0, 0), (0, EXTRA - 1), (0, head_width - small_grad.shape[1])),
-    )
-    head_sum = reduce_weight(
-        jnp.concatenate([head_w_grad.reshape(wt_count, share, head_width), extra], axis=1)
-    ).astype(full)
-    heads_out = head_sum[:share]
-    small_out = head_sum[share]
+    small_grad = jnp.pad(small_grad, ((0, 0), (0, 256 * seq_count - small_grad.shape[1])))
+    small_grad = jnp.pad(small_grad[:, None, :], ((0, 0), (0, 15), (0, 0)))
+
+    def by_owner(partial):
+        return partial.reshape(outer, INNER, -1, partial.shape[-1])
+
+    heads_out, out_w_out, small_out = reduce_shares(
+        by_owner(head_w_grad), by_owner(out_w_grad), by_owner(small_grad)
+    )
+    small_out = small_out[0]
     return (
         layer_out,
         input_grad,

time: 969 us -> 903 us (0.932)
  Pallas kernels: 133 us -> 243 us
  waiting for transfers between devices: 307 us -> 225 us
  local copies, waits for them, and re-layouts: 104 us -> 54.7 us
  between operations: 47 us -> 15.8 us
  other arithmetic: 116 us -> 105 us
    pallas_call x0 -> x1, Pallas kernels: none -> 109 us  [reduce_shares(): pl.pallas_call(functools.partial(reduce_kernel, outer, seq_count, count),...]
    reduce_scatter x4 -> x2, waiting for transfers between devices: 40.7 us -> 0.31 us  [line_reduce(): lax.psum_scatter(value, 'wt', scatter_dimension=0, axis_index_groups=line...]
    all_gather x2, waiting for transfers between devices: 28.6 us -> 0.01 us  [line_gather(): lax.all_gather(value, 'wt', axis=0, axis_index_groups=line, tiled=False)]
    concatenate x3 -> x0, local copies, waits for them, and re-layouts: 13.9 us -> none  [body(): jnp.concatenate([head_w_grad.reshape(wt_count, share, head_width), extra]...]
    slice x1, local copies, waits for them, and re-layouts: 11.7 us -> 0.09 us  [body(): head_b_grad[query_width:query_width + pair_width]]
    convert_element_type x12 -> x4, other arithmetic: 15.5 us -> 4.36 us  [reduce_hop(): return (held[:half].astype(full) + other.astype(full)).astype(low)]
    ppermute x38 -> x24, waiting for transfers between devices: 219 us -> 208 us  [swap(): return lax.ppermute(value, axis, [(i, i ^ bit) for i in range(count)])]
    another operation x1 -> x0, local copies, waits for them, and re-layouts: 10.5 us -> none  [reduce_weight(): split = value.reshape(outer, INNER, count, seq_count, 2, half)]
  transfers between devices with their start and end apart: 50 -> 34, of which waited for: 26 -> 17; matrix products, arithmetic and copies ran while one was open for 35% -> 29% of each run, Pallas kernels for 13% -> 26%
where the time goes in v2:
time: 903 us; the launch traced here: 896 us
  Pallas kernels  243 us (27%)
  matrix products  226 us (25%)
  waiting for transfers between devices  225 us (25%)
  other arithmetic  105 us (12%)
  local copies, waits for them, and re-layouts  54.7 us (6%)
  starting transfers between devices  27 us (3%)
  between operations  15.8 us (2%)
    ppermute x24, waiting for transfers between devices, swap(): return lax.ppermute(value, axis, [(i, i ^ bit) for i in range(count)])  208 us
    pallas_call x1, Pallas kernels, reduce_shares(): pl.pallas_call(functools.partial(reduce_kernel, outer, seq_count, count),...  109 us
    dot_general x4, matrix products, product_right(): lax.dot_general(left, right, (((1,), (1,)), ((), ())), preferred_element_...  94.5 us
    pallas_call x1, Pallas kernels, gather_project(): pl.pallas_call(functools.partial(gather_kernel, outer, seq_count), in_spe...  67.7 us
    dot_general x4, matrix products, product_left(): lax.dot_general(left, right, (((0,), (0,)), ((), ())), preferred_element_...  67.7 us
    dot_general x3, matrix products, product(): return jnp.dot(left, right, preferred_element_type=full)  63.8 us
    pallas_call x1, Pallas kernels, attend_backward(): pl.pallas_call(bwd_kernel, grid=(HEADS,), in_specs=[pl.BlockSpec((1, keys...  31.1 us
    pallas_call x1, Pallas kernels, attend_forward(): pl.pallas_call(fwd_kernel, grid=(HEADS,), in_specs=[pl.BlockSpec((1, keys...  22.8 us
  transfers between devices with their start and end apart: 34, of which 17 were waited for; matrix products, arithmetic and copies ran while one was open for 29% of the time, Pallas kernels for 26%

profile of v2, /device:TPU:0, one launch (start us, length us, event | category | flops | bytes accessed | tf_op | source)
XLA Modules:
  0.0 896.2 jit_solution(6624144390945144108)
XLA Ops:
  7.9 5.3 split_units.1
  13.3 2.7 fusion.39
  16.4 2.5 collective-permute-start.7
  33.1 67.7 %gather_project.1 = (bf16[512,1536]{1,0:T(8,128)(2,1)S(1)}, bf16[512,2048]{1,0:T(8,128)(2,1)}, f32[8,2048]{1,0:T(8,128)S(1)}, bf16[4,4,96,2048]{3,2,1,0:T(8,128)(2,1)}, bf16[4,4,96,1536]{3,2,1,0:T(8,128)(2,1)}) custom-call(bf16[512,1536]{1,0:T(8,128)(2,1)S(1)} %bitcast.154, bf16[96,2048]{1,0:T(8,128)(2,1)S(1)} %pad_maximum_fusion.19.p_ref, ...), custom_call_target="tpu_custom_call" | custom-call | flops 25769803776 | bytes 22020096 | tf_op jit(solution)/shard_map/gather_project/pallas_call | solution.py:339
  110.1 7.5 collective-permute-done
  117.6 2.4 pad_maximum_fusion.17
  120.0 22.8 %attend_forward.1 = bf16[512,1536]{1,0:T(8,128)(2,1)} custom-call(s32[1,1024]{1,0:T(1,128)} %compare_select_fusion.kpos_ref, bf16[512,2048]{1,0:T(8,128)(2,1)} %get-tuple-element.35.q_ref, bf16[1024,512]{1,0:T(8,128)(2,1)} %bitcast.170, bf16[1024,512]{1,0:T(8,128)(2,1)} %bitcast.171), custom_call_target="tpu_custom_call" | custom-call | flops 9663676416 | bytes 4194304 | tf_op jit(solution)/shard_map/attend_forward/pallas_call | solution.py:603
  142.8 6.0 multiply_reduce_fusion.2
  152.4 18.2 %collective-permute-done.1 = bf16[1,256,1536]{2,1,0:T(8,128)(2,1)S(1)} collective-permute-done((bf16[1,256,1536]{2,1,0:T(8,128)(2,1)S(1)}, bf16[1,256,1536]{2,1,0:T(8,128)(2,1)S(1)}, u32[]{:S(2)}, u32[]{:S(2)}) %collective-permute-start.1) | collective-permute-done | bytes 786464 | tf_op jit(solution)/shard_map/ppermute | solution.py:54
  173.1 34.5 %collective-permute-done.2 = bf16[2,256,1536]{2,1,0:T(8,128)(2,1)S(1)} collective-permute-done((bf16[2,256,1536]{2,1,0:T(8,128)(2,1)S(1)}, bf16[2,256,1536]{2,1,0:T(8,128)(2,1)S(1)}, u32[]{:S(2)}, u32[]{:S(2)}) %collective-permute-start.2) | collective-permute-done | bytes 1572896 | tf_op jit(solution)/shard_map/ppermute | solution.py:54
  208.7 3.1 pad_maximum_fusion.5
  214.4 17.9 %collective-permute-done.9 = bf16[1,256,1536]{2,1,0:T(8,128)(2,1)S(1)} collective-permute-done((bf16[1,256,1536]{2,1,0:T(8,128)(2,1)S(1)}, bf16[1,256,1536]{2,1,0:T(8,128)(2,1)S(1)}, u32[]{:S(2)}, u32[]{:S(2)}) %collective-permute-start.9) | collective-permute-done | bytes 786464 | tf_op jit(solution)/shard_map/ppermute | solution.py:54
  241.8 28.3 %collective-permute-done.10 = bf16[2,256,1536]{2,1,0:T(8,128)(2,1)} collective-permute-done((bf16[2,256,1536]{2,1,0:T(8,128)(2,1)}, bf16[2,256,1536]{2,1,0:T(8,128)(2,1)}, u32[]{:S(2)}, u32[]{:S(2)}) %collective-permute-start.10) | collective-permute-done | bytes 1572896 | tf_op jit(solution)/shard_map/ppermute | solution.py:54
  270.1 2.2 maximum_bitcast_fusion.2
  275.0 3.3 pad_maximum_fusion.6
  278.3 10.6 %pad_maximum_fusion.1 = bf16[4096,1536]{1,0:T(8,128)(2,1)} fusion(bf16[2048,1536]{1,0:T(8,128)(2,1)} %collective-permute-done.5, bf16[2048,1536]{1,0:T(8,128)(2,1)} %bitcast.14), kind=kLoop, calls=%fused_computation.7 | loop fusion | flops 25165824 | bytes 25165824 | tf_op jit(solution)/shard_map/concatenate | solution.py:799
  288.8 38.5 %fusion.36 = f32[4096,2304]{0,1:T(8,128)} fusion(bf16[1536,2304]{1,0:T(8,128)(2,1)} %bitcast.178, bf16[2048,1536]{1,0:T(8,128)(2,1)} %collective-permute-done.5, bf16[2048,1536]{1,0:T(8,128)(2,1)} %bitcast.14), kind=kOutput, calls=%fused_computation.159 | convolution fusion | flops 29016195072 | bytes 57409536 | tf_op jit(solution)/shard_map/dot_general | solution.py:27
  327.3 47.7 %multiply_convert_fusion.1 = (bf16[4096,1152]{0,1:T(8,128)(2,1)}, bf16[4096,1152]{0,1:T(8,128)(2,1)}, bf16[4096,1152]{0,1:T(8,128)(2,1)}) fusion(f32[4096,2304]{0,1:T(8,128)} %fusion.36, bf16[1120,1536]{1,0:T(8,128)(2,1)} %all-gather.6.cloned.1.call-done, bf16[2048,1536]{1,0:T(8,128)(2,1)} %collective-permute-done.13, bf16[2048,1536]{1,0:T(8,128)(2,1)} %bitcast.30), kind=kOutput, calls=%fused_computation.2 | convolution fusion | flops 14596177920 | bytes 82083840 | tf_op jit(solution)/shard_map/dot_general | solution.py:35
  375.0 36.2 %convolution_convert_fusion.1 = bf16[4096,1536]{1,0:T(8,128)(2,1)} fusion(bf16[1536,2304]{1,0:T(8,128)(2,1)} %bitcast.179, bf16[4096,1152]{0,1:T(8,128)(2,1)} %get-tuple-element.63, bf16[4096,1152]{0,1:T(8,128)(2,1)} %get-tuple-element.62), kind=kOutput, calls=%fused_computation.6 | convolution fusion | flops 29035069440 | bytes 38535168 | tf_op jit(solution)/shard_map/dot_general | solution.py:35
  411.2 6.5 slice.303
  419.0 17.6 %fusion = bf16[1152,1536]{1,0:T(8,128)(2,1)S(1)} fusion(bf16[4096,1152]{0,1:T(8,128)(2,1)S(1)} %copy-done.54, bf16[2048,1536]{1,0:T(8,128)(2,1)} %collective-permute-done.13, bf16[2048,1536]{1,0:T(8,128)(2,1)} %bitcast.30), kind=kOutput, calls=%fused_computation.12 | convolution fusion | flops 14520680448 | bytes 25559040 | tf_op jit(solution)/shard_map/dot_general | solution.py:31
  439.3 15.4 %pad_maximum_fusion = bf16[4096,2304]{0,1:T(8,128)(2,1)} fusion(bf16[4096,1152]{0,1:T(8,128)(2,1)} %get-tuple-element.63, bf16[4096,1152]{0,1:T(8,128)(2,1)} %get-tuple-element.62), kind=kLoop, calls=%fused_computation | loop fusion | flops 37748736 | bytes 37748736 | tf_op jit(solution)/shard_map/concatenate | solution.py:824
  454.6 38.3 %convolution_convert_fusion.2 = bf16[1536,2304]{1,0:T(8,128)(2,1)} fusion(bf16[4096,1536]{1,0:T(8,128)(2,1)} %pad_maximum_fusion.1, bf16[4096,2304]{0,1:T(8,128)(2,1)} %pad_maximum_fusion), kind=kOutput, calls=%fused_computation.11 | convolution fusion | flops 28994568192 | bytes 38535168 | tf_op jit(solution)/shard_map/dot_general | solution.py:31
  493.0 9.1 %add_convert_fusion.1 = bf16[2048,1536]{1,0:T(8,128)(2,1)} fusion(bf16[2048,1536]{1,0:T(8,128)(2,1)} %collective-permute-done.14, bf16[4096,1536]{1,0:T(8,128)(2,1)} %convolution_convert_fusion.1), kind=kLoop, calls=%fused_computation.10 | loop fusion | flops 12582912 | bytes 18874368 | tf_op jit(solution)/shard_map/convert_element_type | solution.py:803
  503.9 3.2 fusion.38
  509.3 15.3 %collective-permute-done.29 = bf16[1,280,1536]{2,1,0:T(8,128)(2,1)S(1)} collective-permute-done((bf16[1,280,1536]{2,1,0:T(8,128)(2,1)}, bf16[1,280,1536]{2,1,0:T(8,128)(2,1)S(1)}, u32[]{:S(2)}, u32[]{:S(2)}) %collective-permute-start.29) | collective-permute-done | bytes 860192 | tf_op jit(solution)/shard_map/ppermute | solution.py:54
  525.0 2.3 bitcast_convert_fusion
  527.3 29.9 %collective-permute-done.15 = bf16[2,256,1536]{2,1,0:T(8,128)(2,1)S(1)} collective-permute-done((bf16[2,256,1536]{2,1,0:T(8,128)(2,1)S(1)}, bf16[2,256,1536]{2,1,0:T(8,128)(2,1)S(1)}, u32[]{:S(2)}, u32[]{:S(2)}) %collective-permute-start.15) | collective-permute-done | bytes 1572896 | tf_op jit(solution)/shard_map/ppermute | solution.py:54
  562.4 19.2 %convolution_convert_fusion = bf16[4096,1536]{1,0:T(8,128)(2,1)S(1)} fusion(bf16[4096,1152]{0,1:T(8,128)(2,1)} %get-tuple-element.42, bf16[1120,1536]{1,0:T(8,128)(2,1)S(1)} %copy-done.48), kind=kOutput, calls=%fused_computation.5 | convolution fusion | flops 14501806080 | bytes 25460736 | tf_op jit(solution)/shard_map/dot_general | solution.py:27
  581.7 3.4 slice.258
  585.1 3.1 copy-done.14
  595.7 3.7 convolution_convert_fusion.5.g_ref
  599.5 31.1 %attend_backward.1 = (bf16[512,1536]{1,0:T(8,128)(2,1)}, f32[1024,256]{1,0:T(8,128)}, f32[1024,256]{1,0:T(8,128)}) custom-call(s32[1,1024]{1,0:T(1,128)} %compare_select_fusion.kpos_ref, f32[512,128]{1,0:T(8,128)} %copy-done.4, f32[512,128]{1,0:T(8,128)} %copy-done.6, bf16[512,2048]{1,0:T(8,128)(2,1)} %get-tuple-element.35.q_ref, ...), custom_call_target="tpu_custom_call" | custom-call | flops 24159191040 | bytes 9437184 | tf_op jit(solution)/shard_map/attend_backward/pallas_call | solution.py:671
  635.2 5.9 convolution_convert_fusion.3
  641.0 7.9 collective-permute-done.24
  653.4 6.8 fusion.11
  660.3 5.8 convolution_convert_fusion.4
  666.1 2.0 fusion.19
  668.2 9.0 %add_convert_fusion = bf16[2048,1536]{1,0:T(8,128)(2,1)} fusion(bf16[2048,1536]{1,0:T(8,128)(2,1)} %collective-permute-done.19, bf16[4096,1536]{1,0:T(8,128)(2,1)} %copy-done.14), kind=kLoop, calls=%fused_computation.9 | loop fusion | flops 12582912 | bytes 18874368 | tf_op jit(solution)/shard_map/convert_element_type | solution.py:803
  677.2 5.1 fusion.37
  684.1 109.4 %reduce_shares.1 = (f32[96,2048]{1,0:T(8,128)}, f32[96,1536]{1,0:T(8,128)}, f32[16,512]{1,0:T(8,128)}) custom-call(bf16[4,4,96,2048]{3,2,1,0:T(8,128)(2,1)} %bitcast.162, bf16[4,4,96,1536]{3,2,1,0:T(8,128)(2,1)} %bitcast.163, bf16[4,4,16,512]{3,2,1,0:T(8,128)(2,1)} %bitcast.169), custom_call_target="tpu_custom_call" | custom-call | bytes 90177536 | tf_op jit(solution)/shard_map/reduce_shares/pallas_call | solution.py:500
  804.9 8.3 collective-permute-done.26
  813.2 8.4 collective-permute-done.27
  824.2 10.2 %collective-permute-done.20 = bf16[2,256,1536]{2,1,0:T(8,128)(2,1)} collective-permute-done((bf16[2,256,1536]{2,1,0:T(8,128)(2,1)}, bf16[2,256,1536]{2,1,0:T(8,128)(2,1)}, u32[]{:S(2)}, u32[]{:S(2)}) %collective-permute-start.20) | collective-permute-done | bytes 1572896 | tf_op jit(solution)/shard_map/ppermute | solution.py:54
  838.9 33.3 %collective-permute-done.28 = bf16[1,4,96,2304]{3,2,1,0:T(8,128)(2,1)S(1)} collective-permute-done((bf16[1,4,96,2304]{3,2,1,0:T(8,128)(2,1)S(1)}, bf16[1,4,96,2304]{3,2,1,0:T(8,128)(2,1)S(1)}, u32[]{:S(2)}, u32[]{:S(2)}) %collective-permute-start.28) | collective-permute-done | bytes 1769504 | tf_op jit(solution)/shard_map/ppermute | solution.py:54
  872.2 2.1 pad_maximum_fusion.7.u_ref
  874.3 6.2 join_units.1
  882.0 3.2 collective-permute-done.23
  (265 shorter events, 101.0 us)
Async XLA Ops:
  7.2 230.8 %copy-start = (f32[560,1536]{1,0:T(8,128)S(1)}, f32[560,1536]{1,0:T(8,128)}, u32[]{:S(2)}) copy-start(f32[560,1536]{1,0:T(8,128)} %param.28) | copy-start | bytes 10321924
  7.2 281.6 %all-gather.4.cloned.1.call-start = ((), (), s32[]{:S(2)}) async-start(), calls=%async_computation.2 | async-start | bytes 8847360 | tf_op jit(solution)/shard_map/all_gather | solution.py:730
  15.9 90.7 %collective-permute-start.6 = (bf16[96,2304]{1,0:T(8,128)(2,1)}, bf16[96,2304]{1,0:T(8,128)(2,1)}, u32[]{:S(2)}, u32[]{:S(2)}) collective-permute-start(bf16[96,2304]{1,0:T(8,128)(2,1)} %get-tuple-element.84), channel_id=1, source_target_pairs={{0,2},{2,0},{4,6},{6,4},{8,10},{10,8},{12,14},{14,12},{16,18},{18,... | collective-permute-start | bytes 1327112 | tf_op jit(solution)/shard_map/ppermute | solution.py:746
  16.4 90.2 %collective-permute-start.7 = (bf16[96,2304]{1,0:T(8,128)(2,1)}, bf16[96,2304]{1,0:T(8,128)(2,1)}, u32[]{:S(2)}, u32[]{:S(2)}) collective-permute-start(bf16[96,2304]{1,0:T(8,128)(2,1)} %get-tuple-element.83), channel_id=1, source_target_pairs={{0,4},{2,6},{4,0},{6,2},{8,12},{10,14},{12,8},{14,10},{16,20},{18,... | collective-permute-start | bytes 1327112 | tf_op jit(solution)/shard_map/ppermute | solution.py:746
  18.9 87.7 %collective-permute-start.8 = (bf16[96,2304]{1,0:T(8,128)(2,1)}, bf16[96,2304]{1,0:T(8,128)(2,1)}, u32[]{:S(2)}, u32[]{:S(2)}) collective-permute-start(bf16[96,2304]{1,0:T(8,128)(2,1)} %get-tuple-element.82), channel_id=1, source_target_pairs={{0,6},{2,4},{4,2},{6,0},{8,14},{10,12},{12,10},{14,8},{16,22},{18,... | collective-permute-start | bytes 1327112 | tf_op jit(solution)/shard_map/ppermute | solution.py:746
  29.5 71.3 %copy-start.4 = (f32[512,128]{1,0:T(8,128)}, f32[512,128]{1,0:T(8,128)S(1)}, u32[]{:S(2)}) copy-start(f32[512,128]{1,0:T(8,128)S(1)} %get-tuple-element.116.cos_ref) | copy-start | bytes 786436
  29.5 71.3 %copy-start.6 = (f32[512,128]{1,0:T(8,128)}, f32[512,128]{1,0:T(8,128)S(1)}, u32[]{:S(2)}) copy-start(f32[512,128]{1,0:T(8,128)S(1)} %get-tuple-element.117.sin_ref) | copy-start | bytes 786436
  103.8 13.8 %collective-permute-start = (bf16[1,512,512]{2,1,0:T(8,128)(2,1)}, bf16[1,512,512]{2,1,0:T(8,128)(2,1)}, u32[]{:S(2)}, u32[]{:S(2)}) collective-permute-start(bf16[1,512,512]{2,1,0:T(8,128)(2,1)} %slice_bitcast_fusion.10), channel_id=1, source_target_pairs={{0,1},{1,0},{2,3},{3,2},{4,5},{5,4},{6,7},{7,6},{8,9},{9,8},{10,11... | collective-permute-start | bytes 1572872 | tf_op jit(solution)/shard_map/ppermute | solution.py:54
  106.6 42.8 %copy-start.38 = (f32[1536]{0:T(1024)}, f32[1536]{0:T(1024)S(1)}, u32[]{:S(2)}) copy-start(f32[1536]{0:T(1024)S(1)} %get-tuple-element.61) | copy-start | bytes 18436
  109.9 217.4 %all-gather.6.cloned.1.call-start = ((), (), s32[]{:S(2)}) async-start(), calls=%async_computation.5 | async-start | bytes 4300800 | tf_op jit(solution)/shard_map/all_gather | solution.py:730
  150.5 20.2 %collective-permute-start.1 = (bf16[1,256,1536]{2,1,0:T(8,128)(2,1)S(1)}, bf16[1,256,1536]{2,1,0:T(8,128)(2,1)S(1)}, u32[]{:S(2)}, u32[]{:S(2)}) collective-permute-start(bf16[1,256,1536]{2,1,0:T(8,128)(2,1)S(1)} %get-tuple-element.89), channel_id=1, source_target_pairs={{0,4},{2,6},{4,0},{6,2},{8,12},{10,14},{12,8},{14,10},{16,20},{18,... | collective-permute-start | bytes 2359304 | tf_op jit(solution)/shard_map/ppermute | solution.py:54
  151.2 20.3 %collective-permute-start.3 = (bf16[1,256,1536]{2,1,0:T(8,128)(2,1)S(1)}, bf16[1,256,1536]{2,1,0:T(8,128)(2,1)S(1)}, u32[]{:S(2)}, u32[]{:S(2)}) collective-permute-start(bf16[1,256,1536]{2,1,0:T(8,128)(2,1)S(1)} %get-tuple-element.90), channel_id=1, source_target_pairs={{0,1},{1,0},{2,3},{3,2},{4,5},{5,4},{6,7},{7,6},{8,9},{9,8},{10,11... | collective-permute-start | bytes 2359304 | tf_op jit(solution)/shard_map/ppermute | solution.py:54
  170.8 36.8 %collective-permute-start.2 = (bf16[2,256,1536]{2,1,0:T(8,128)(2,1)S(1)}, bf16[2,256,1536]{2,1,0:T(8,128)(2,1)S(1)}, u32[]{:S(2)}, u32[]{:S(2)}) collective-permute-start(bf16[2,256,1536]{2,1,0:T(8,128)(2,1)S(1)} %pad_maximum_fusion.13), channel_id=1, source_target_pairs={{0,1},{1,0},{2,3},{3,2},{4,5},{5,4},{6,7},{7,6},{8,9},{9,8},{10,11... | collective-permute-start | bytes 4718600 | tf_op jit(solution)/shard_map/ppermute | solution.py:54
  171.7 36.7 %collective-permute-start.4 = (bf16[2,256,1536]{2,1,0:T(8,128)(2,1)S(1)}, bf16[2,256,1536]{2,1,0:T(8,128)(2,1)S(1)}, u32[]{:S(2)}, u32[]{:S(2)}) collective-permute-start(bf16[2,256,1536]{2,1,0:T(8,128)(2,1)S(1)} %pad_maximum_fusion.14), channel_id=1, source_target_pairs={{0,4},{2,6},{4,0},{6,2},{8,12},{10,14},{12,8},{14,10},{16,20},{18,... | collective-permute-start | bytes 4718600 | tf_op jit(solution)/shard_map/ppermute | solution.py:54
  211.8 66.4 %collective-permute-start.5 = (bf16[2048,1536]{1,0:T(8,128)(2,1)}, bf16[2048,1536]{1,0:T(8,128)(2,1)}, u32[]{:S(2)}, u32[]{:S(2)}) collective-permute-start(bf16[2048,1536]{1,0:T(8,128)(2,1)} %bitcast.14), channel_id=1, source_target_pairs={{0,2},{2,0},{4,6},{6,4},{8,10},{10,8},{12,14},{14,12},{16,18},{18,... | collective-permute-start | bytes 18874376 | tf_op jit(solution)/shard_map/ppermute | solution.py:54
  212.4 24.7 %copy-start.18 = (bf16[1,256,1536]{2,1,0:T(8,128)(2,1)}, bf16[1,256,1536]{2,1,0:T(8,128)(2,1)S(1)}, u32[]{:S(2)}) copy-start(bf16[1,256,1536]{2,1,0:T(8,128)(2,1)S(1)} %get-tuple-element.88) | copy-start | bytes 2359300
  212.4 24.7 %copy-start.20 = (bf16[1,256,1536]{2,1,0:T(8,128)(2,1)}, bf16[1,256,1536]{2,1,0:T(8,128)(2,1)S(1)}, u32[]{:S(2)}) copy-start(bf16[1,256,1536]{2,1,0:T(8,128)(2,1)S(1)} %get-tuple-element.87) | copy-start | bytes 2359300
  212.4 19.9 %collective-permute-start.9 = (bf16[1,256,1536]{2,1,0:T(8,128)(2,1)S(1)}, bf16[1,256,1536]{2,1,0:T(8,128)(2,1)S(1)}, u32[]{:S(2)}, u32[]{:S(2)}) collective-permute-start(bf16[1,256,1536]{2,1,0:T(8,128)(2,1)S(1)} %get-tuple-element.87), channel_id=1, source_target_pairs={{0,4},{2,6},{4,0},{6,2},{8,12},{10,14},{12,8},{14,10},{16,20},{18,... | collective-permute-start | bytes 2359304 | tf_op jit(solution)/shard_map/ppermute | solution.py:54
  213.5 21.4 %collective-permute-start.11 = (bf16[1,256,1536]{2,1,0:T(8,128)(2,1)S(1)}, bf16[1,256,1536]{2,1,0:T(8,128)(2,1)S(1)}, u32[]{:S(2)}, u32[]{:S(2)}) collective-permute-start(bf16[1,256,1536]{2,1,0:T(8,128)(2,1)S(1)} %get-tuple-element.88), channel_id=1, source_target_pairs={{0,1},{1,0},{2,3},{3,2},{4,5},{5,4},{6,7},{7,6},{8,9},{9,8},{10,11... | collective-permute-start | bytes 2359304 | tf_op jit(solution)/shard_map/ppermute | solution.py:54
  233.7 36.4 %collective-permute-start.10 = (bf16[2,256,1536]{2,1,0:T(8,128)(2,1)}, bf16[2,256,1536]{2,1,0:T(8,128)(2,1)}, u32[]{:S(2)}, u32[]{:S(2)}) collective-permute-start(bf16[2,256,1536]{2,1,0:T(8,128)(2,1)} %pad_maximum_fusion.15), channel_id=1, source_target_pairs={{0,1},{1,0},{2,3},{3,2},{4,5},{5,4},{6,7},{7,6},{8,9},{9,8},{10,11... | collective-permute-start | bytes 4718600 | tf_op jit(solution)/shard_map/ppermute | solution.py:54
  237.1 36.1 %collective-permute-start.12 = (bf16[2,256,1536]{2,1,0:T(8,128)(2,1)}, bf16[2,256,1536]{2,1,0:T(8,128)(2,1)}, u32[]{:S(2)}, u32[]{:S(2)}) collective-permute-start(bf16[2,256,1536]{2,1,0:T(8,128)(2,1)} %pad_maximum_fusion.16), channel_id=1, source_target_pairs={{0,4},{2,6},{4,0},{6,2},{8,12},{10,14},{12,8},{14,10},{16,20},{18,... | collective-permute-start | bytes 4718600 | tf_op jit(solution)/shard_map/ppermute | solution.py:54
  239.0 263.4 %reduce-scatter.5.cloned.1.call-start = ((), (), s32[]{:S(2)}) async-start(), calls=%async_computation.4 | async-start | bytes 4300800 | tf_op jit(solution)/shard_map/reduce_scatter | solution.py:733
  241.8 31.5 %copy-start.19 = (bf16[1,256,1536]{2,1,0:T(8,128)(2,1)S(1)}, bf16[1,256,1536]{2,1,0:T(8,128)(2,1)}, u32[]{:S(2)}) copy-start(bf16[1,256,1536]{2,1,0:T(8,128)(2,1)} %copy-done.18) | copy-start | bytes 2359300
  241.8 31.5 %copy-start.32 = (bf16[1,256,1536]{2,1,0:T(8,128)(2,1)S(1)}, bf16[1,256,1536]{2,1,0:T(8,128)(2,1)}, u32[]{:S(2)}) copy-start(bf16[1,256,1536]{2,1,0:T(8,128)(2,1)} %copy-done.31) | copy-start | bytes 2359300
  278.3 49.1 %collective-permute-start.13 = (bf16[2048,1536]{1,0:T(8,128)(2,1)}, bf16[2048,1536]{1,0:T(8,128)(2,1)}, u32[]{:S(2)}, u32[]{:S(2)}) collective-permute-start(bf16[2048,1536]{1,0:T(8,128)(2,1)} %bitcast.30), channel_id=1, source_target_pairs={{0,2},{2,0},{4,6},{6,4},{8,10},{10,8},{12,14},{14,12},{16,18},{18,... | collective-permute-start | bytes 18874376 | tf_op jit(solution)/shard_map/ppermute | solution.py:54
  411.2 7.8 copy-start.54
  438.6 359.7 %reduce-scatter.3.cloned.1.call-start = ((), (), s32[]{:S(2)}) async-start(), calls=%async_computation.3 | async-start | bytes 8847360 | tf_op jit(solution)/shard_map/reduce_scatter | solution.py:733
  438.7 54.3 %collective-permute-start.14 = (bf16[2048,1536]{1,0:T(8,128)(2,1)}, bf16[2048,1536]{1,0:T(8,128)(2,1)}, u32[]{:S(2)}, u32[]{:S(2)}) collective-permute-start(bf16[2048,1536]{1,0:T(8,128)(2,1)} %slice.303), channel_id=1, source_target_pairs={{0,2},{2,0},{4,6},{6,4},{8,10},{10,8},{12,14},{14,12},{16,18},{18,... | collective-permute-start | bytes 18874376 | tf_op jit(solution)/shard_map/ppermute | solution.py:54
  502.4 22.2 %collective-permute-start.29 = (bf16[1,280,1536]{2,1,0:T(8,128)(2,1)}, bf16[1,280,1536]{2,1,0:T(8,128)(2,1)S(1)}, u32[]{:S(2)}, u32[]{:S(2)}) collective-permute-start(bf16[1,280,1536]{2,1,0:T(8,128)(2,1)} %reduce-scatter.5.cloned.1.call-done), channel_id=1, source_target_pairs={{0,1},{1,0},{2,3},{3,2},{4,5},{5,4},{6,7},{7,6},{8,9},{9,8},{10,11... | collective-permute-start | bytes 2580488 | tf_op jit(solution)/shard_map/ppermute | solution.py:54
  507.1 50.1 %collective-permute-start.15 = (bf16[2,256,1536]{2,1,0:T(8,128)(2,1)S(1)}, bf16[2,256,1536]{2,1,0:T(8,128)(2,1)S(1)}, u32[]{:S(2)}, u32[]{:S(2)}) collective-permute-start(bf16[2,256,1536]{2,1,0:T(8,128)(2,1)S(1)} %bitcast.168), channel_id=1, source_target_pairs={{0,1},{1,0},{2,3},{3,2},{4,5},{5,4},{6,7},{7,6},{8,9},{9,8},{10,11... | collective-permute-start | bytes 4718600 | tf_op jit(solution)/shard_map/ppermute | solution.py:54
  507.8 50.7 %collective-permute-start.16 = (bf16[2,256,1536]{2,1,0:T(8,128)(2,1)S(1)}, bf16[2,256,1536]{2,1,0:T(8,128)(2,1)S(1)}, u32[]{:S(2)}, u32[]{:S(2)}) collective-permute-start(bf16[2,256,1536]{2,1,0:T(8,128)(2,1)S(1)} %bitcast.167), channel_id=1, source_target_pairs={{0,4},{2,6},{4,0},{6,2},{8,12},{10,14},{12,8},{14,10},{16,20},{18,... | collective-permute-start | bytes 4718600 | tf_op jit(solution)/shard_map/ppermute | solution.py:54
  559.9 28.3 %collective-permute-start.17 = (bf16[256,1536]{1,0:T(8,128)(2,1)}, bf16[256,1536]{1,0:T(8,128)(2,1)}, u32[]{:S(2)}, u32[]{:S(2)}) collective-permute-start(bf16[256,1536]{1,0:T(8,128)(2,1)} %slice_bitcast_fusion.2), channel_id=1, source_target_pairs={{0,4},{2,6},{4,0},{6,2},{8,12},{10,14},{12,8},{14,10},{16,20},{18,... | collective-permute-start | bytes 2359304 | tf_op jit(solution)/shard_map/ppermute | solution.py:54
  560.9 28.8 %collective-permute-start.18 = (bf16[256,1536]{1,0:T(8,128)(2,1)}, bf16[256,1536]{1,0:T(8,128)(2,1)}, u32[]{:S(2)}, u32[]{:S(2)}) collective-permute-start(bf16[256,1536]{1,0:T(8,128)(2,1)} %slice_bitcast_fusion), channel_id=1, source_target_pairs={{0,1},{1,0},{2,3},{3,2},{4,5},{5,4},{6,7},{7,6},{8,9},{9,8},{10,11... | collective-permute-start | bytes 2359304 | tf_op jit(solution)/shard_map/ppermute | solution.py:54
  588.2 80.0 %collective-permute-start.19 = (bf16[2048,1536]{1,0:T(8,128)(2,1)}, bf16[2048,1536]{1,0:T(8,128)(2,1)}, u32[]{:S(2)}, u32[]{:S(2)}) collective-permute-start(bf16[2048,1536]{1,0:T(8,128)(2,1)} %slice.258), channel_id=1, source_target_pairs={{0,2},{2,0},{4,6},{6,4},{8,10},{10,8},{12,14},{14,12},{16,18},{18,... | collective-permute-start | bytes 18874376 | tf_op jit(solution)/shard_map/ppermute | solution.py:54
  634.5 14.5 %collective-permute-start.24 = (bf16[512,512]{1,0:T(8,128)(2,1)}, bf16[512,512]{1,0:T(8,128)(2,1)}, u32[]{:S(2)}, u32[]{:S(2)}) collective-permute-start(bf16[512,512]{1,0:T(8,128)(2,1)} %pad_maximum_fusion.18), channel_id=1, source_target_pairs={{0,1},{1,0},{2,3},{3,2},{4,5},{5,4},{6,7},{7,6},{8,9},{9,8},{10,11... | collective-permute-start | bytes 1572872 | tf_op jit(solution)/shard_map/ppermute | solution.py:54
  635.2 13.8 %copy-start.28 = (bf16[1024,256]{1,0:T(8,128)(2,1)S(1)}, bf16[1024,256]{1,0:T(8,128)(2,1)}, u32[]{:S(2)}) copy-start(bf16[1024,256]{1,0:T(8,128)(2,1)} %copy-done.27) | copy-start | bytes 1572868
  635.2 13.8 %copy-start.30 = (bf16[1024,256]{1,0:T(8,128)(2,1)S(1)}, bf16[1024,256]{1,0:T(8,128)(2,1)}, u32[]{:S(2)}) copy-start(bf16[1024,256]{1,0:T(8,128)(2,1)} %copy-done.29) | copy-start | bytes 1572868
  641.0 10.8 %copy-start.7 = (f32[512,128]{1,0:T(8,128)S(1)}, f32[512,128]{1,0:T(8,128)}, u32[]{:S(2)}) copy-start(f32[512,128]{1,0:T(8,128)} %copy-done.6) | copy-start | bytes 786436
  682.3 140.1 %collective-permute-start.21 = (bf16[2,256,1536]{2,1,0:T(8,128)(2,1)}, bf16[2,256,1536]{2,1,0:T(8,128)(2,1)}, u32[]{:S(2)}, u32[]{:S(2)}) collective-permute-start(bf16[2,256,1536]{2,1,0:T(8,128)(2,1)} %bitcast.42), channel_id=1, source_target_pairs={{0,4},{2,6},{4,0},{6,2},{8,12},{10,14},{12,8},{14,10},{16,20},{18,... | collective-permute-start | bytes 4718600 | tf_op jit(solution)/shard_map/ppermute | solution.py:54
  796.8 37.6 %collective-permute-start.20 = (bf16[2,256,1536]{2,1,0:T(8,128)(2,1)}, bf16[2,256,1536]{2,1,0:T(8,128)(2,1)}, u32[]{:S(2)}, u32[]{:S(2)}) collective-permute-start(bf16[2,256,1536]{2,1,0:T(8,128)(2,1)} %bitcast.40), channel_id=1, source_target_pairs={{0,1},{1,0},{2,3},{3,2},{4,5},{5,4},{6,7},{7,6},{8,9},{9,8},{10,11... | collective-permute-start | bytes 4718600 | tf_op jit(solution)/shard_map/ppermute | solution.py:54
  798.3 24.1 %copy-start.23 = (bf16[512,1536]{1,0:T(8,128)(2,1)S(1)}, bf16[512,1536]{1,0:T(8,128)(2,1)}, u32[]{:S(2)}) copy-start(bf16[512,1536]{1,0:T(8,128)(2,1)} %get-tuple-element.66) | copy-start | bytes 4718596
  800.0 4.9 collective-permute-start.25
  800.1 13.1 %collective-permute-start.26 = (bf16[96,2304]{1,0:T(8,128)(2,1)S(1)}, bf16[96,2304]{1,0:T(8,128)(2,1)S(1)}, u32[]{:S(2)}, u32[]{:S(2)}) collective-permute-start(bf16[96,2304]{1,0:T(8,128)(2,1)S(1)} %get-tuple-element.75), channel_id=1, source_target_pairs={{0,4},{2,6},{4,0},{6,2},{8,12},{10,14},{12,8},{14,10},{16,20},{18,... | collective-permute-start | bytes 1327112 | tf_op jit(solution)/shard_map/ppermute | solution.py:746
  800.6 20.9 %collective-permute-start.27 = (bf16[96,2304]{1,0:T(8,128)(2,1)S(1)}, bf16[96,2304]{1,0:T(8,128)(2,1)S(1)}, u32[]{:S(2)}, u32[]{:S(2)}) collective-permute-start(bf16[96,2304]{1,0:T(8,128)(2,1)S(1)} %get-tuple-element.74), channel_id=1, source_target_pairs={{0,6},{2,4},{4,2},{6,0},{8,14},{10,12},{12,10},{14,8},{16,22},{18,... | collective-permute-start | bytes 1327112 | tf_op jit(solution)/shard_map/ppermute | solution.py:746
  821.8 50.4 %collective-permute-start.28 = (bf16[1,4,96,2304]{3,2,1,0:T(8,128)(2,1)S(1)}, bf16[1,4,96,2304]{3,2,1,0:T(8,128)(2,1)S(1)}, u32[]{:S(2)}, u32[]{:S(2)}) collective-permute-start(bf16[1,4,96,2304]{3,2,1,0:T(8,128)(2,1)S(1)} %maximum_bitcast_fusion.4), channel_id=1, source_target_pairs={{0,1},{1,0},{2,3},{3,2},{4,5},{5,4},{6,7},{7,6},{8,9},{9,8},{10,11... | collective-permute-start | bytes 5308424 | tf_op jit(solution)/shard_map/ppermute | solution.py:54
  824.2 12.9 %copy-start.24 = (bf16[2,256,1536]{2,1,0:T(8,128)(2,1)}, bf16[2,256,1536]{2,1,0:T(8,128)(2,1)S(1)}, u32[]{:S(2)}) copy-start(bf16[2,256,1536]{2,1,0:T(8,128)(2,1)S(1)} %fusion.14) | copy-start | bytes 4718596
  836.3 44.2 %collective-permute-start.22 = (bf16[256,1536]{1,0:T(8,128)(2,1)S(1)}, bf16[256,1536]{1,0:T(8,128)(2,1)}, u32[]{:S(2)}, u32[]{:S(2)}) collective-permute-start(bf16[256,1536]{1,0:T(8,128)(2,1)S(1)} %slice_bitcast_fusion.7), channel_id=1, source_target_pairs={{0,4},{2,6},{4,0},{6,2},{8,12},{10,14},{12,8},{14,10},{16,20},{18,... | collective-permute-start | bytes 2359304 | tf_op jit(solution)/shard_map/ppermute | solution.py:54
  837.4 47.8 %collective-permute-start.23 = (bf16[256,1536]{1,0:T(8,128)(2,1)S(1)}, bf16[256,1536]{1,0:T(8,128)(2,1)}, u32[]{:S(2)}, u32[]{:S(2)}) collective-permute-start(bf16[256,1536]{1,0:T(8,128)(2,1)S(1)} %slice_bitcast_fusion.6), channel_id=1, source_target_pairs={{0,1},{1,0},{2,3},{3,2},{4,5},{5,4},{6,7},{7,6},{8,9},{9,8},{10,11... | collective-permute-start | bytes 2359304 | tf_op jit(solution)/shard_map/ppermute | solution.py:54
  (43 other events, 139.7 us)
Sparse Core Ops, SparseCore 0:
  110.0 128.2 all-gather.3
  240.4 66.4 all-gather.5
  438.8 63.6 reduce-scatter.4
  504.6 123.5 reduce-scatter.2

commit v3 on v2

--- a/solution.py
+++ b/solution.py
@@ -152,35 +152,95 @@
     return (2 * (2**slow - 1), len(set(a for a, _ in subsets(hops_a[:-1]))))
 
 
+def line_kernel(outer, seq_count, p_ref, wo_ref, s_ref, head_ref, out_ref, small_ref, *sems):
+    send_sems, recv_sems, local_sems = sems
+    wt, seq = lax.axis_index("wt"), lax.axis_index("seq")
+    line, inner = wt // INNER, wt % INNER
+
+    def own_columns(total):
+        wide = total // seq_count
+        return pl.ds(pl.multiple_of(seq * wide, 128), wide)
+
+    pairs = [
+        (s_ref, small_ref),
+        (p_ref.at[:, own_columns(p_ref.shape[1])], head_ref),
+        (wo_ref.at[:, own_columns(wo_ref.shape[1])], out_ref),
+    ]
+    own = [
+        pltpu.make_async_copy(source, target.at[0], local_sems.at[k])
+        for k, (source, target) in enumerate(pairs)
+    ]
+    for copy in own:
+        copy.start()
+    peers = [(flip_all(line, d) * INNER + inner, seq) for d in range(1, outer)]
+    meet(peers)
+    out = Sender(send_sems, recv_sems)
+    for source, target in pairs:
+        for d in range(1, outer):
+            out.start(source, target.at[d], peers[d - 1])
+    for copy in own:
+        copy.wait()
+    for copy in out.copies:
+        copy.wait()
+
+
+def gather_line(packed, w_out, small):
+    outer = lax.axis_size("wt") // INNER
+    seq_count = lax.axis_size("seq")
+    share, head_width = packed.shape
+    vmem = pl.BlockSpec(memory_space=pltpu.VMEM)
+    copies = 3 * (outer - 1)
+    sent = 2 * outer * share * (head_width + w_out.shape[1])
+    return pl.pallas_call(
+        functools.partial(line_kernel, outer, seq_count),
+        in_specs=[vmem] * 3,
+        out_specs=[vmem] * 3,
+        out_shape=[
+            jax.ShapeDtypeStruct((outer, share, head_width // seq_count), low),
+            jax.ShapeDtypeStruct((outer, share, w_out.shape[1] // seq_count), low),
+            jax.ShapeDtypeStruct((outer,) + small.shape, low),
+        ],
+        scratch_shapes=[
+            pltpu.SemaphoreType.DMA((copies,)),
+            pltpu.SemaphoreType.DMA((copies,)),
+            pltpu.SemaphoreType.DMA((3,)),
+        ],
+        compiler_params=pltpu.CompilerParams(collective_id=3, has_side_effects=True),
+        cost_estimate=pl.CostEstimate(flops=0, bytes_accessed=8 * sent, transcendentals=0),
+        name="gather_line",
+    )(packed, w_out, small)
+
+
 def gather_kernel(
     outer, seq_count, x_ref, p_ref, wo_ref, s_ref, cos_ref, sin_ref,
     normed_ref, qkv_ref, vec_ref, head_ref, out_ref,
     w_scr, o_scr, s_scr, send_sems, recv_sems, local_sems,
 ):
-    share, head_width = p_ref.shape
+    share, head_width = p_ref.shape[1], w_scr.shape[3]
     width = x_ref.shape[1]
     wt, seq = lax.axis_index("wt"), lax.axis_index("seq")
     line, inner = wt // INNER, wt % INNER
     hops = plane_hops(seq_count)
     slow = len(hops[0]) - 1
-    peers = [(flip_all(line, d) * INNER + inner, seq) for d in range(1, outer)]
-    peers += [(wt - inner + flip(inner, bit), seq) for bit in inner_bits()]
+    peers = [(wt - inner + flip(inner, bit), seq) for bit in inner_bits()]
     peers += [(wt, flip(seq, bit)) for _, bit in bits_of("seq", seq_count)]
 
     def own_columns(total):
         wide = total // seq_count
         return pl.ds(pl.multiple_of(seq * wide, 128), wide)
 
-    fill = [
-        pltpu.make_async_copy(
-            ref.at[:, own_columns(ref.shape[1])],
-            scratch.at[line, inner, :, own_columns(ref.shape[1])],
-            local_sems.at[k],
-        )
-        for k, (ref, scratch) in enumerate(((p_ref, w_scr), (wo_ref, o_scr)))
-    ] + [
-        pltpu.make_async_copy(s_ref, s_scr.at[line, inner], local_sems.at[2]),
-    ]
+    fill = []
+    for d in range(outer):
+        at = flip_all(line, d)
+        pairs = [
+            (s_ref.at[d], s_scr.at[at, inner]),
+            (p_ref.at[d], w_scr.at[at, inner, :, own_columns(head_width)]),
+            (wo_ref.at[d], o_scr.at[at, inner, :, own_columns(o_scr.shape[3])]),
+        ]
+        fill += [
+            pltpu.make_async_copy(source, target, local_sems.at[3 * d + k])
+            for k, (source, target) in enumerate(pairs)
+        ]
     for copy in fill:
         copy.start()
     meet(peers)
@@ -197,22 +257,6 @@
         first = -(-wide // 256) * 128
         start = part * wide + half * first
         return pl.ds(pl.multiple_of(start, 128), wide - first if half else first)
-
-    def start_line(source, scratch, narrow):
-        total = source.shape[1]
-        copies = [None]
-        for d in range(1, outer):
-            if narrow:
-                part = own_columns(total)
-                pair = (source.at[:, part], scratch.at[line, inner, :, part])
-            else:
-                pair = (source, scratch.at[line, inner])
-            copies.append(out.start(*pair, (flip_all(line, d) * INNER + inner, seq)))
-        return copies
-
-    small_line = start_line(s_ref, s_scr, False)
-    head_line = start_line(p_ref, w_scr, True)
-    out_line = start_line(wo_ref, o_scr, True)
 
     def start_stage(scratch, at, stage):
         total = scratch.shape[-1]
@@ -238,17 +282,14 @@
 
     for copy in fill:
         copy.wait()
-    waiting = [[copy] for copy in head_line]
-    small_wait = small_line
+    waiting = [[] for _ in range(outer)]
+    small_wait = []
     for step in range(outer + slow + 1):
         for stage in range(slow + 1):
             d = step - stage
             if 0 <= d < outer:
                 arrive(waiting[d])
                 waiting[d] = start_stage(w_scr, flip_all(line, d), stage)
-        if step == 0:
-            arrive(small_wait)
-            small_wait = []
         if step < len(inner_bits()):
             arrive(small_wait)
             bit = inner_bits()[::-1][step]
@@ -257,7 +298,6 @@
                 place = s_scr.at[:, flip_all(inner, a)]
                 small_wait.append(out.start(place, place, hop_peer(("wt", bit))))
     arrive(small_wait)
-    arrive(out_line)
     out_wait = start_stage(o_scr, slice(None), 0)
 
     count = outer * INNER
@@ -328,14 +368,15 @@
     outer = lax.axis_size("wt") // INNER
     seq_count = lax.axis_size("seq")
     rows, width = tokens.shape
-    share, head_width = packed.shape
+    share, head_width = packed.shape[1], packed.shape[2] * seq_count
+    out_width = w_out.shape[2] * seq_count
     slow_copies, last_copies = plane_copies(seq_count)
     each = slow_copies + last_copies
     small_copies = 2 ** len(inner_bits()) - 1
-    copies = 3 * (outer - 1) + (outer + 1) * each + small_copies
+    copies = (outer + 1) * each + small_copies
     vmem = pl.BlockSpec(memory_space=pltpu.VMEM)
     anywhere = pl.BlockSpec(memory_space=pl.ANY)
-    sent = 2 * outer * INNER * share * (head_width + w_out.shape[1])
+    sent = 2 * outer * INNER * share * (head_width + out_width)
     return pl.pallas_call(
         functools.partial(gather_kernel, outer, seq_count),
         in_specs=[vmem] * 6,
@@ -345,15 +386,15 @@
             jax.ShapeDtypeStruct((rows, head_width), low),
             jax.ShapeDtypeStruct((8, head_width), full),
             jax.ShapeDtypeStruct((outer, INNER, share, head_width), low),
-            jax.ShapeDtypeStruct((outer, INNER, share, w_out.shape[1]), low),
+            jax.ShapeDtypeStruct((outer, INNER, share, out_width), low),
         ],
         scratch_shapes=[
             pltpu.VMEM((outer, INNER, share, head_width), low),
-            pltpu.VMEM((outer, INNER, share, w_out.shape[1]), low),
-            pltpu.VMEM((outer, INNER, small.shape[0], small.shape[1]), low),
+            pltpu.VMEM((outer, INNER, share, out_width), low),
+            pltpu.VMEM((outer, INNER) + small.shape[1:], low),
             pltpu.SemaphoreType.DMA((copies,)),
             pltpu.SemaphoreType.DMA((copies,)),
-            pltpu.SemaphoreType.DMA((3,)),
+            pltpu.SemaphoreType.DMA((3 * outer,)),
         ],
         compiler_params=pltpu.CompilerParams(
             collective_id=1, has_side_effects=True, vmem_limit_bytes=48 << 20
@@ -370,7 +411,10 @@
     return sorted(set(a for a, _ in subsets(hops[:-1])))
 
 
-def reduce_kernel(outer, seq_count, count, *refs):
+def reduce_kernel(outer, seq_count, count, u_ref, *refs):
+    refs = list(refs)
+    units_ref = refs.pop(2 * count)
+    own_sem = refs.pop()
     given, results = refs[:count], refs[count : 2 * count]
     slow = len(plane_hops(seq_count)[0]) - 1
     held = refs[2 * count : 3 * count]
@@ -383,8 +427,14 @@
     hops = plane_hops(seq_count)
     nears = near_inner(seq_count)
     peers = [(flip_all(line, d) * INNER + inner, seq) for d in range(1, outer)]
-    peers += [(wt - inner + flip(inner, bit), seq) for bit in inner_bits()]
-    peers += [(wt, flip_all(seq, d)) for d in range(1, seq_count)]
+    peers += [
+        (wt - inner + flip_all(inner, a), flip_all(seq, b))
+        for b in range(seq_count)
+        for a in range(INNER)
+        if a or b
+    ]
+    keep = pltpu.make_async_copy(u_ref.at[inner], units_ref.at[0, 0], own_sem.at[0])
+    keep.start()
     meet(peers)
     out = Sender(send_sems, recv_sems)
 
@@ -475,16 +525,35 @@
         arrive(copies)
         results[k][...] = joined[k][...].astype(full)
 
-    running = [steps(k) for k in range(count)]
+    def exchange():
+        copies = []
+        for b in range(seq_count):
+            copies += [
+                out.start(
+                    u_ref.at[flip_all(inner, a)],
+                    units_ref.at[b, a],
+                    (wt - inner + flip_all(inner, a), flip_all(seq, b)),
+                )
+                for a in range(INNER)
+                if a or b
+            ]
+            if b == 0:
+                for _ in range(slow + 1):
+                    yield
+        yield
+        arrive(copies)
+
+    running = [steps(k) for k in range(count)] + [exchange()]
     while running:
         for one in list(running):
             if next(one, "done") == "done":
                 running.remove(one)
     for copy in out.copies:
         copy.wait_send()
-
-
-def reduce_shares(*partials):
+    keep.wait()
+
+
+def reduce_shares(units, *partials):
     outer = lax.axis_size("wt") // INNER
     seq_count = lax.axis_size("seq")
     count = len(partials)
@@ -496,23 +565,25 @@
     ]
     shapes = [p.shape[2:] for p in partials]
     copies = count * (nears + 2 * (2**slow - 1) + outer - 1 + seq_count - 1)
+    copies += INNER * seq_count - 1
     sent = sum(2 * p.size for p in partials)
     return pl.pallas_call(
         functools.partial(reduce_kernel, outer, seq_count, count),
-        in_specs=[vmem] * count,
-        out_specs=[vmem] * count,
-        out_shape=[jax.ShapeDtypeStruct(shape, full) for shape in shapes],
+        in_specs=[vmem] * (count + 1),
+        out_specs=[vmem] * (count + 1),
+        out_shape=[jax.ShapeDtypeStruct(shape, full) for shape in shapes]
+        + [jax.ShapeDtypeStruct((seq_count,) + units.shape, low)],
         scratch_shapes=near
         + [pltpu.VMEM((outer, r, c // seq_count), low) for r, c in shapes]
         + [pltpu.VMEM(shape, low) for shape in shapes]
         + near * (1 + slow)
-        + [pltpu.SemaphoreType.DMA((copies,)), pltpu.SemaphoreType.DMA((copies,))],
+        + [pltpu.SemaphoreType.DMA((n,)) for n in (copies, copies, 1)],
         compiler_params=pltpu.CompilerParams(
             collective_id=2, has_side_effects=True, vmem_limit_bytes=60 << 20
         ),
         cost_estimate=pl.CostEstimate(flops=0, bytes_accessed=8 * sent, transcendentals=0),
         name="reduce_shares",
-    )(*partials)
+    )(units, *partials)
 
 
 def split_kernel(outer, seq_count, own, info_ref, gate_ref, up_ref, o_ref):
@@ -569,6 +640,50 @@
         out_shape=[shape, shape],
         name="join_units",
     )(info, units)
+
+
+def hidden_kernel(both_ref, grad_ref, down_ref, hidden_ref, units_ref):
+    wide = hidden_ref.shape[1]
+    hidden_grad = lax.dot_general(
+        grad_ref[...], down_ref[...], (((1,), (1,)), ((), ())), preferred_element_type=full
+    )
+    gate, upper = both_ref[:, :wide], both_ref[:, wide:]
+    sigma = 1.0 / (1.0 + jnp.exp(-gate))
+    taken = gate * sigma
+    hidden_ref[...] = (taken * upper).astype(low)
+    slope = sigma * (1.0 + gate * (1.0 - sigma))
+    units_ref[:, :wide] = (hidden_grad * upper * slope).astype(low)
+    units_ref[:, wide:] = (hidden_grad * taken).astype(low)
+
+
+def hidden_units(both, grad, down_w):
+    total, width = grad.shape
+    wide = down_w.shape[0]
+    block = min(512, total)
+    return pl.pallas_call(
+        hidden_kernel,
+        grid=(total // block,),
+        in_specs=[
+            pl.BlockSpec((block, 2 * wide), lambda i: (i, 0)),
+            pl.BlockSpec((block, width), lambda i: (i, 0)),
+            pl.BlockSpec((wide, width), lambda i: (0, 0)),
+        ],
+        out_specs=[
+            pl.BlockSpec((block, wide), lambda i: (i, 0)),
+            pl.BlockSpec((block, 2 * wide), lambda i: (i, 0)),
+        ],
+        out_shape=[
+            jax.ShapeDtypeStruct((total, wide), low),
+            jax.ShapeDtypeStruct((total, 2 * wide), low),
+        ],
+        compiler_params=pltpu.CompilerParams(vmem_limit_bytes=56 << 20),
+        cost_estimate=pl.CostEstimate(
+            flops=2 * total * width * wide,
+            bytes_accessed=2 * total * (width + 7 * wide) + 2 * wide * width,
+            transcendentals=total * wide,
+        ),
+        name="hidden_units",
+    )(both, grad, down_w)
 
 
 def after(value, *others):
@@ -768,7 +883,7 @@
     packed = jnp.concatenate([w_query, w_key, w_value], axis=1).astype(low)
     normed_low, qkv, vectors, head_all, out_all = gather_project(
         tokens.reshape(rows, width),
-        packed, w_out.astype(low), small, cosine, sine,
+        *gather_line(packed, w_out.astype(low), small), cosine, sine,
     )
     head_w = head_all.reshape(width, head_width)
     out_w = out_all.reshape(query_width, width)
@@ -814,14 +929,8 @@
     stages = list(range(1, len(slow_a)))[::-1]
     grad_all = spread(after(upstream_low, pairs))
     rows_all = spread(normed_two_low)
-    hidden_grad = product_right(grad_all, down_w)
     both = product(rows_all, units_w)
-    gate, upper = both[:, :ff_pad], both[:, ff_pad:]
-    sigma = jax.nn.sigmoid(gate)
-    hidden = (gate * sigma * upper).astype(low)
-    gate_grad = (hidden_grad * upper * sigma * (1.0 + gate * (1.0 - sigma))).astype(low)
-    up_grad = (hidden_grad * gate * sigma).astype(low)
-    units_grad = jnp.concatenate([gate_grad, up_grad], axis=1)
+    hidden, units_grad = hidden_units(both, grad_all, down_w)
     partial = product_right(units_grad, units_w).astype(low)
     down_grad = product_left(after(hidden, partial), grad_all).astype(low)
     down_grad = down_grad[:ff_here]
@@ -852,11 +961,6 @@
     layer_out = jnp.where(keep, resid + forth, 0.0).astype(low)
     layer_out = layer_out.reshape(slot_count, rows, width)
 
-    blocks = units_line.reshape(INNER, share, 2 * ff_pad)
-    sent = jnp.stack([to_place(blocks, inner_here ^ d) for d in range(INNER)])
-    gate_out, up_out = join_units(
-        info, gather_hops(inner_exchange(sent), seq_hops), outer, ff_own
-    )
     down_out = seq_gather(down_line)
     down_out = down_out.reshape(seq_count * ff_own, width).astype(full)
     pair_part = jnp.concatenate([key_part, value_part], axis=1)
@@ -900,10 +1004,11 @@
     def by_owner(partial):
         return partial.reshape(outer, INNER, -1, partial.shape[-1])
 
-    heads_out, out_w_out, small_out = reduce_shares(
-        by_owner(head_w_grad), by_owner(out_w_grad), by_owner(small_grad)
+    heads_out, out_w_out, small_out, units_got = reduce_shares(
+        units_line.reshape(INNER, share, 2 * ff_pad), by_owner(head_w_grad), by_owner(out_w_grad), by_owner(small_grad)
     )
     small_out = small_out[0]
+    gate_out, up_out = join_units(info, units_got, outer, ff_own)
     return (
         layer_out,
         input_grad,

time: 903 us -> 907 us (level)
  Pallas kernels: 243 us -> 361 us
  waiting for transfers between devices: 225 us -> 168 us
  matrix products: 226 us -> 180 us
  other arithmetic: 105 us -> 90.8 us
    pallas_call x0 -> x2, Pallas kernels: none -> 100 us  [the longest x1 64.4 us: gather_line(): pl.pallas_call(functools.partial(line_kernel, outer, seq_count), in_specs...]
    ppermute x24 -> x23, waiting for transfers between devices: 208 us -> 135 us  [swap(): return lax.ppermute(value, axis, [(i, i ^ bit) for i in range(count)])]
    dot_general x4 -> x3, matrix products: 94.5 us -> 48.7 us  [product_right(): lax.dot_general(left, right, (((1,), (1,)), ((), ())), preferred_element_...]
    pallas_call x1, Pallas kernels: 109 us -> 140 us  [reduce_shares(): pl.pallas_call(functools.partial(reduce_kernel, outer, seq_count, count),...]
    reduce_scatter x2, waiting for transfers between devices: 0.31 us -> 17.1 us  [line_reduce(): lax.psum_scatter(value, 'wt', scatter_dimension=0, axis_index_groups=line...]
    concatenate x1 -> x0, other arithmetic: 15.4 us -> none  [body(): units_grad = jnp.concatenate([gate_grad, up_grad], axis=1)]
    pallas_call x1, Pallas kernels: 67.7 us -> 56.4 us  [gather_project(): pl.pallas_call(functools.partial(gather_kernel, outer, seq_count), in_spe...]
    ppermute x24 -> x23, starting transfers between devices: 21.3 us -> 20.8 us  [swap(): return lax.ppermute(value, axis, [(i, i ^ bit) for i in range(count)])]
  transfers between devices with their start and end apart: 34 -> 30, of which waited for: 17 -> 11; matrix products, arithmetic and copies ran while one was open for 29% -> 24% of each run, Pallas kernels for 26% -> 36%
where the time goes in v3:
time: 907 us; the launch traced here: 899 us
  Pallas kernels  361 us (40%)
  matrix products  180 us (20%)
  waiting for transfers between devices  168 us (19%)
  other arithmetic  90.8 us (10%)
  local copies, waits for them, and re-layouts  58.6 us (6%)
  starting transfers between devices  24.6 us (3%)
  between operations  15.8 us (2%)
    pallas_call x1, Pallas kernels, reduce_shares(): pl.pallas_call(functools.partial(reduce_kernel, outer, seq_count, count),...  140 us
    ppermute x23, waiting for transfers between devices, swap(): return lax.ppermute(value, axis, [(i, i ^ bit) for i in range(count)])  135 us
    dot_general x4, matrix products, product_left(): lax.dot_general(left, right, (((0,), (0,)), ((), ())), preferred_element_...  67.7 us
    pallas_call x1, Pallas kernels, gather_line(): pl.pallas_call(functools.partial(line_kernel, outer, seq_count), in_specs...  64.4 us
    dot_general x3, matrix products, product(): return jnp.dot(left, right, preferred_element_type=full)  63.5 us
    pallas_call x1, Pallas kernels, gather_project(): pl.pallas_call(functools.partial(gather_kernel, outer, seq_count), in_spe...  56.4 us
    dot_general x3, matrix products, product_right(): lax.dot_general(left, right, (((1,), (1,)), ((), ())), preferred_element_...  48.7 us
    pallas_call x1, Pallas kernels, hidden_units(): pl.pallas_call(hidden_kernel, grid=(total // block,), in_specs=[pl.BlockS...  35.8 us
  transfers between devices with their start and end apart: 30, of which 11 were waited for; matrix products, arithmetic and copies ran while one was open for 24% of the time, Pallas kernels for 36%

profile of v3, /device:TPU:0, one launch (start us, length us, event | category | flops | bytes accessed | tf_op | source)
XLA Modules:
  0.0 899.2 jit_solution(11956020572653300446)
XLA Ops:
  20.2 64.4 %gather_line.1 = (bf16[4,96,1024]{2,1,0:T(8,128)(2,1)}, bf16[4,96,768]{2,1,0:T(8,128)(2,1)}, bf16[4,16,128]{2,1,0:T(8,128)(2,1)}) custom-call(bf16[96,2048]{1,0:T(8,128)(2,1)} %pad_maximum_fusion.15.p_ref, bf16[96,1536]{1,0:T(8,128)(2,1)} %convert_element_type.193.wo_ref, bf16[16,128]{1,0:T(8,128)(2,1)} %pad.43.s_ref), custom_call_target="tpu_custom_call" | custom-call | bytes 22020096 | tf_op jit(solution)/shard_map/gather_line/pallas_call | solution.py:194
  87.5 56.4 %gather_project.1 = (bf16[512,1536]{1,0:T(8,128)(2,1)S(1)}, bf16[512,2048]{1,0:T(8,128)(2,1)}, f32[8,2048]{1,0:T(8,128)S(1)}, bf16[4,4,96,2048]{3,2,1,0:T(8,128)(2,1)}, bf16[4,4,96,1536]{3,2,1,0:T(8,128)(2,1)}) custom-call(bf16[512,1536]{1,0:T(8,128)(2,1)S(1)} %bitcast.144, bf16[4,96,1024]{2,1,0:T(8,128)(2,1)S(1)} %copy-done.8, ...), custom_call_target="tpu_custom_call" | custom-call | flops 25769803776 | bytes 22020096 | tf_op jit(solution)/shard_map/gather_project/pallas_call | solution.py:380
  148.8 5.0 split_units.1
  153.8 2.8 fusion.33
  156.6 2.2 collective-permute-start.6
  163.4 8.7 collective-permute-done.7
  172.1 7.5 collective-permute-done.8
  183.0 2.3 pad_maximum_fusion.13
  189.0 22.7 %attend_forward.1 = bf16[512,1536]{1,0:T(8,128)(2,1)} custom-call(s32[1,1024]{1,0:T(1,128)} %compare_select_fusion.kpos_ref, bf16[512,2048]{1,0:T(8,128)(2,1)} %get-tuple-element.44.q_ref, bf16[1024,512]{1,0:T(8,128)(2,1)} %bitcast.160, bf16[1024,512]{1,0:T(8,128)(2,1)} %bitcast.161), custom_call_target="tpu_custom_call" | custom-call | flops 9663676416 | bytes 4194304 | tf_op jit(solution)/shard_map/attend_forward/pallas_call | solution.py:718
  211.7 5.1 multiply_reduce_fusion.2
  224.8 15.4 %collective-permute-done.1 = bf16[1,256,1536]{2,1,0:T(8,128)(2,1)S(1)} collective-permute-done((bf16[1,256,1536]{2,1,0:T(8,128)(2,1)S(1)}, bf16[1,256,1536]{2,1,0:T(8,128)(2,1)S(1)}, u32[]{:S(2)}, u32[]{:S(2)}) %collective-permute-start.1) | collective-permute-done | bytes 786464 | tf_op jit(solution)/shard_map/ppermute | solution.py:54
  242.1 31.3 %collective-permute-done.3 = bf16[1,256,1536]{2,1,0:T(8,128)(2,1)S(1)} collective-permute-done((bf16[1,256,1536]{2,1,0:T(8,128)(2,1)S(1)}, bf16[1,256,1536]{2,1,0:T(8,128)(2,1)S(1)}, u32[]{:S(2)}, u32[]{:S(2)}) %collective-permute-start.3) | collective-permute-done | bytes 786464 | tf_op jit(solution)/shard_map/ppermute | solution.py:54
  277.0 3.2 pad_maximum_fusion.3
  280.2 26.1 %collective-permute-done.2 = bf16[2,256,1536]{2,1,0:T(8,128)(2,1)S(1)} collective-permute-done((bf16[2,256,1536]{2,1,0:T(8,128)(2,1)S(1)}, bf16[2,256,1536]{2,1,0:T(8,128)(2,1)S(1)}, u32[]{:S(2)}, u32[]{:S(2)}) %collective-permute-start.2) | collective-permute-done | bytes 1572896 | tf_op jit(solution)/shard_map/ppermute | solution.py:54
  306.6 2.0 collective-permute-done.4
  309.0 3.3 pad_maximum_fusion.2
  312.2 4.0 pad.44.down_ref
  316.2 10.5 %pad_maximum_fusion.1.grad_ref = bf16[4096,1536]{1,0:T(8,128)(2,1)} fusion(bf16[2048,1536]{1,0:T(8,128)(2,1)} %collective-permute-done.13, bf16[2048,1536]{1,0:T(8,128)(2,1)} %bitcast.30), kind=kLoop, calls=%fused_computation.3 | loop fusion | flops 25165824 | bytes 25165824 | tf_op jit(solution)/shard_map/concatenate | solution.py:914
  326.7 39.3 %fusion.30.both_ref = f32[4096,2304]{1,0:T(8,128)} fusion(bf16[1536,2304]{1,0:T(8,128)(2,1)} %bitcast.165, bf16[2048,1536]{1,0:T(8,128)(2,1)} %collective-permute-done.5, bf16[2048,1536]{1,0:T(8,128)(2,1)} %bitcast.14), kind=kOutput, calls=%fused_computation.142 | convolution fusion | flops 29016195072 | bytes 57409536 | tf_op jit(solution)/shard_map/dot_general | solution.py:27
  366.1 35.8 %hidden_units.1 = (bf16[4096,1152]{1,0:T(8,128)(2,1)}, bf16[4096,2304]{1,0:T(8,128)(2,1)}) custom-call(f32[4096,2304]{1,0:T(8,128)} %fusion.30.both_ref, bf16[4096,1536]{1,0:T(8,128)(2,1)} %pad_maximum_fusion.1.grad_ref, bf16[1152,1536]{1,0:T(8,128)(2,1)} %pad.44.down_ref), custom_call_target="tpu_custom_call" | custom-call | flops 14495514624 | bytes 82182144 | tf_op jit(solution)/shard_map/hidden_units/pallas_call | solution.py:663
  401.9 36.3 %convolution_convert_fusion.1 = bf16[4096,1536]{1,0:T(8,128)(2,1)} fusion(bf16[4096,2304]{1,0:T(8,128)(2,1)} %get-tuple-element.52, bf16[1536,2304]{1,0:T(8,128)(2,1)} %bitcast.166), kind=kOutput, calls=%fused_computation.1 | convolution fusion | flops 28997320704 | bytes 38535168 | tf_op jit(solution)/shard_map/dot_general | solution.py:35
  438.2 18.1 %fusion.29 = bf16[1152,1536]{1,0:T(8,128)(2,1)S(1)} fusion(bf16[4096,1152]{1,0:T(8,128)(2,1)S(1)} %copy-done.52, bf16[2048,1536]{1,0:T(8,128)(2,1)} %collective-permute-done.13, bf16[2048,1536]{1,0:T(8,128)(2,1)} %bitcast.30), kind=kOutput, calls=%fused_computation.141 | convolution fusion | flops 14520680448 | bytes 25559040 | tf_op jit(solution)/shard_map/dot_general | solution.py:31
  458.5 5.9 slice.293
  465.8 6.1 pad_maximum_fusion
  471.9 36.4 %convolution_convert_fusion.2 = bf16[1536,2304]{1,0:T(8,128)(2,1)} fusion(bf16[4096,1536]{1,0:T(8,128)(2,1)S(1)} %pad_maximum_fusion, bf16[4096,2304]{1,0:T(8,128)(2,1)} %get-tuple-element.52), kind=kOutput, calls=%fused_computation.6 | convolution fusion | flops 28994568192 | bytes 38535168 | tf_op jit(solution)/shard_map/dot_general | solution.py:31
  508.3 9.0 add_convert_fusion.1
  517.3 17.1 %reduce-scatter.5.cloned.1.call-done = bf16[1,280,1536]{2,1,0:T(8,128)(2,1)} async-done(((bf16[4,280,1536]{2,1,0:T(8,128)(2,1)}), bf16[1,280,1536]{2,1,0:T(8,128)(2,1)}) %reduce-scatter.5.cloned.1.call-update) | async-done | bytes 860176 | tf_op jit(solution)/shard_map/reduce_scatter | solution.py:848
  535.9 3.2 fusion.32
  541.3 15.3 %collective-permute-done.25 = bf16[1,280,1536]{2,1,0:T(8,128)(2,1)S(1)} collective-permute-done((bf16[1,280,1536]{2,1,0:T(8,128)(2,1)}, bf16[1,280,1536]{2,1,0:T(8,128)(2,1)S(1)}, u32[]{:S(2)}, u32[]{:S(2)}) %collective-permute-start.25) | collective-permute-done | bytes 860192 | tf_op jit(solution)/shard_map/ppermute | solution.py:54
  556.9 2.3 bitcast_convert_fusion
  559.3 29.5 %collective-permute-done.15 = bf16[2,256,1536]{2,1,0:T(8,128)(2,1)S(1)} collective-permute-done((bf16[2,256,1536]{2,1,0:T(8,128)(2,1)S(1)}, bf16[2,256,1536]{2,1,0:T(8,128)(2,1)S(1)}, u32[]{:S(2)}, u32[]{:S(2)}) %collective-permute-start.15) | collective-permute-done | bytes 1572896 | tf_op jit(solution)/shard_map/ppermute | solution.py:54
  593.6 19.0 %convolution_convert_fusion = bf16[4096,1536]{1,0:T(8,128)(2,1)S(1)} fusion(bf16[4096,1152]{1,0:T(8,128)(2,1)} %get-tuple-element.53, bf16[1120,1536]{1,0:T(8,128)(2,1)S(1)} %copy-done.31), kind=kOutput, calls=%fused_computation | convolution fusion | flops 14501806080 | bytes 25460736 | tf_op jit(solution)/shard_map/dot_general | solution.py:27
  612.6 3.3 slice.250
  615.9 3.2 copy-done.16
  626.7 3.7 convolution_convert_fusion.5.g_ref
  630.4 31.1 %attend_backward.1 = (bf16[512,1536]{1,0:T(8,128)(2,1)}, f32[1024,256]{1,0:T(8,128)}, f32[1024,256]{1,0:T(8,128)}) custom-call(s32[1,1024]{1,0:T(1,128)} %compare_select_fusion.kpos_ref, f32[512,128]{1,0:T(8,128)} %copy-done.4, f32[512,128]{1,0:T(8,128)} %copy-done.6, bf16[512,2048]{1,0:T(8,128)(2,1)} %get-tuple-element.44.q_ref, ...), custom_call_target="tpu_custom_call" | custom-call | flops 24159191040 | bytes 9437184 | tf_op jit(solution)/shard_map/attend_backward/pallas_call | solution.py:786
  665.0 7.3 convolution_convert_fusion.3
  672.4 6.3 collective-permute-done.24
  681.6 2.1 reshape.299
  687.4 8.7 fusion.7
  697.0 8.9 add_convert_fusion
  706.0 5.8 fusion.31
  712.3 5.8 convolution_convert_fusion.4
  718.7 2.0 fusion.15
  720.8 139.9 %reduce_shares.1 = (f32[96,2048]{1,0:T(8,128)}, f32[96,1536]{1,0:T(8,128)}, f32[16,512]{1,0:T(8,128)}, bf16[2,4,96,2304]{3,2,1,0:T(8,128)(2,1)}) custom-call(bf16[4,96,2304]{2,1,0:T(8,128)(2,1)} %bitcast.156, bf16[4,4,96,2048]{3,2,1,0:T(8,128)(2,1)} %bitcast.148, bf16[4,4,96,1536]{3,2,1,0:T(8,128)(2,1)} %bitcast.153, bf16[4,4,16,512]{3,2,1,0:T(8,128)(2,1)} %bitcast.159), custom_call_target="tpu_custom_call" | custom-call | bytes 90177536 | tf_op jit(solution)/shard_map/reduce_shares/pallas_call | solution.py:570
  863.9 2.3 fusion.11
  870.8 6.1 join_units.1
  878.4 8.6 collective-permute-done.22
  (252 shorter events, 91.8 us)
Async XLA Ops:
  7.2 7.6 copy-start.44
  7.2 305.0 %all-gather.6.cloned.1.call-start = ((), (), s32[]{:S(2)}) async-start(), calls=%async_computation.5 | async-start | bytes 4300800 | tf_op jit(solution)/shard_map/all_gather | solution.py:845
  10.2 74.4 %copy-start.2 = (bf16[1,512,1536]{2,1,0:T(8,128)(2,1)S(1)}, bf16[1,512,1536]{2,1,0:T(8,128)(2,1)}, u32[]{:S(2)}) copy-start(bf16[1,512,1536]{2,1,0:T(8,128)(2,1)} %param.15) | copy-start | bytes 4718596
  10.2 316.6 %all-gather.4.cloned.1.call-start = ((), (), s32[]{:S(2)}) async-start(), calls=%async_computation.2 | async-start | bytes 8847360 | tf_op jit(solution)/shard_map/all_gather | solution.py:845
  19.4 124.6 %copy-start.4 = (f32[512,128]{1,0:T(8,128)}, f32[512,128]{1,0:T(8,128)S(1)}, u32[]{:S(2)}) copy-start(f32[512,128]{1,0:T(8,128)S(1)} %get-tuple-element.121.cos_ref) | copy-start | bytes 786436
  19.4 124.6 %copy-start.6 = (f32[512,128]{1,0:T(8,128)}, f32[512,128]{1,0:T(8,128)S(1)}, u32[]{:S(2)}) copy-start(f32[512,128]{1,0:T(8,128)S(1)} %get-tuple-element.122.sin_ref) | copy-start | bytes 786436
  147.0 36.0 %collective-permute-start = (bf16[1,512,512]{2,1,0:T(8,128)(2,1)}, bf16[1,512,512]{2,1,0:T(8,128)(2,1)}, u32[]{:S(2)}, u32[]{:S(2)}) collective-permute-start(bf16[1,512,512]{2,1,0:T(8,128)(2,1)} %slice_bitcast_fusion.10), channel_id=1, source_target_pairs={{0,1},{1,0},{2,3},{3,2},{4,5},{5,4},{6,7},{7,6},{8,9},{9,8},{10,11... | collective-permute-start | bytes 1572872 | tf_op jit(solution)/shard_map/ppermute | solution.py:54
  153.8 8.2 copy-start.23
  156.6 6.8 collective-permute-start.6
  158.8 13.4 %collective-permute-start.7 = (bf16[96,2304]{1,0:T(8,128)(2,1)}, bf16[96,2304]{1,0:T(8,128)(2,1)}, u32[]{:S(2)}, u32[]{:S(2)}) collective-permute-start(bf16[96,2304]{1,0:T(8,128)(2,1)} %get-tuple-element.88), channel_id=1, source_target_pairs={{0,4},{2,6},{4,0},{6,2},{8,12},{10,14},{12,8},{14,10},{16,20},{18,... | collective-permute-start | bytes 1327112 | tf_op jit(solution)/shard_map/ppermute | solution.py:861
  159.2 20.4 %collective-permute-start.8 = (bf16[96,2304]{1,0:T(8,128)(2,1)}, bf16[96,2304]{1,0:T(8,128)(2,1)}, u32[]{:S(2)}, u32[]{:S(2)}) collective-permute-start(bf16[96,2304]{1,0:T(8,128)(2,1)} %get-tuple-element.87), channel_id=1, source_target_pairs={{0,6},{2,4},{4,2},{6,0},{8,14},{10,12},{12,10},{14,8},{16,22},{18,... | collective-permute-start | bytes 1327112 | tf_op jit(solution)/shard_map/ppermute | solution.py:861
  160.8 18.9 %copy-start.33 = (bf16[1,96,2304]{2,1,0:T(8,128)(2,1)S(1)}, bf16[1,96,2304]{2,1,0:T(8,128)(2,1)}, u32[]{:S(2)}) copy-start(bf16[1,96,2304]{2,1,0:T(8,128)(2,1)} %get-tuple-element.86) | copy-start | bytes 1327108
  160.8 20.4 %copy-start.50 = (pred[512]{0:T(512)(128)(4,1)}, pred[512]{0:T(512)(128)(4,1)S(1)}, u32[]{:S(2)}) copy-start(pred[512]{0:T(512)(128)(4,1)S(1)} %fusion.25) | copy-start | bytes 1540
  162.0 55.4 %copy-start.42 = (f32[1536]{0:T(1024)}, f32[1536]{0:T(1024)S(1)}, u32[]{:S(2)}) copy-start(f32[1536]{0:T(1024)S(1)} %get-tuple-element.73) | copy-start | bytes 18436
  182.8 351.6 %reduce-scatter.5.cloned.1.call-start = ((), (), s32[]{:S(2)}) async-start(), calls=%async_computation.4 | async-start | bytes 4300800 | tf_op jit(solution)/shard_map/reduce_scatter | solution.py:848
  186.7 31.1 %copy-start.21 = (bf16[1,256,1536]{2,1,0:T(8,128)(2,1)}, bf16[1,256,1536]{2,1,0:T(8,128)(2,1)S(1)}, u32[]{:S(2)}) copy-start(bf16[1,256,1536]{2,1,0:T(8,128)(2,1)S(1)} %get-tuple-element.92) | copy-start | bytes 2359300
  186.7 34.6 %copy-start.19 = (bf16[1,256,1536]{2,1,0:T(8,128)(2,1)}, bf16[1,256,1536]{2,1,0:T(8,128)(2,1)S(1)}, u32[]{:S(2)}) copy-start(bf16[1,256,1536]{2,1,0:T(8,128)(2,1)S(1)} %get-tuple-element.93) | copy-start | bytes 2359300
  186.8 31.0 %collective-permute-start.9 = (bf16[1,256,1536]{2,1,0:T(8,128)(2,1)S(1)}, bf16[1,256,1536]{2,1,0:T(8,128)(2,1)}, u32[]{:S(2)}, u32[]{:S(2)}) collective-permute-start(bf16[1,256,1536]{2,1,0:T(8,128)(2,1)S(1)} %get-tuple-element.92), channel_id=1, source_target_pairs={{0,4},{2,6},{4,0},{6,2},{8,12},{10,14},{12,8},{14,10},{16,20},{18,... | collective-permute-start | bytes 2359304 | tf_op jit(solution)/shard_map/ppermute | solution.py:54
  187.3 34.0 %collective-permute-start.11 = (bf16[1,256,1536]{2,1,0:T(8,128)(2,1)S(1)}, bf16[1,256,1536]{2,1,0:T(8,128)(2,1)}, u32[]{:S(2)}, u32[]{:S(2)}) collective-permute-start(bf16[1,256,1536]{2,1,0:T(8,128)(2,1)S(1)} %get-tuple-element.93), channel_id=1, source_target_pairs={{0,1},{1,0},{2,3},{3,2},{4,5},{5,4},{6,7},{7,6},{8,9},{9,8},{10,11... | collective-permute-start | bytes 2359304 | tf_op jit(solution)/shard_map/ppermute | solution.py:54
  219.2 54.9 %collective-permute-start.10 = (bf16[2,256,1536]{2,1,0:T(8,128)(2,1)S(1)}, bf16[2,256,1536]{2,1,0:T(8,128)(2,1)S(1)}, u32[]{:S(2)}, u32[]{:S(2)}) collective-permute-start(bf16[2,256,1536]{2,1,0:T(8,128)(2,1)S(1)} %pad_maximum_fusion.11), channel_id=1, source_target_pairs={{0,1},{1,0},{2,3},{3,2},{4,5},{5,4},{6,7},{7,6},{8,9},{9,8},{10,11... | collective-permute-start | bytes 4718600 | tf_op jit(solution)/shard_map/ppermute | solution.py:54
  219.7 20.5 %collective-permute-start.1 = (bf16[1,256,1536]{2,1,0:T(8,128)(2,1)S(1)}, bf16[1,256,1536]{2,1,0:T(8,128)(2,1)S(1)}, u32[]{:S(2)}, u32[]{:S(2)}) collective-permute-start(bf16[1,256,1536]{2,1,0:T(8,128)(2,1)S(1)} %get-tuple-element.94), channel_id=1, source_target_pairs={{0,4},{2,6},{4,0},{6,2},{8,12},{10,14},{12,8},{14,10},{16,20},{18,... | collective-permute-start | bytes 2359304 | tf_op jit(solution)/shard_map/ppermute | solution.py:54
  222.6 52.9 %collective-permute-start.12 = (bf16[2,256,1536]{2,1,0:T(8,128)(2,1)S(1)}, bf16[2,256,1536]{2,1,0:T(8,128)(2,1)S(1)}, u32[]{:S(2)}, u32[]{:S(2)}) collective-permute-start(bf16[2,256,1536]{2,1,0:T(8,128)(2,1)S(1)} %pad_maximum_fusion.12), channel_id=1, source_target_pairs={{0,4},{2,6},{4,0},{6,2},{8,12},{10,14},{12,8},{14,10},{16,20},{18,... | collective-permute-start | bytes 4718600 | tf_op jit(solution)/shard_map/ppermute | solution.py:54
  223.2 50.9 %copy-start.22 = (bf16[1,256,1536]{2,1,0:T(8,128)(2,1)S(1)}, bf16[1,256,1536]{2,1,0:T(8,128)(2,1)}, u32[]{:S(2)}) copy-start(bf16[1,256,1536]{2,1,0:T(8,128)(2,1)} %copy-done.21) | copy-start | bytes 2359300
  223.2 50.2 %collective-permute-start.3 = (bf16[1,256,1536]{2,1,0:T(8,128)(2,1)S(1)}, bf16[1,256,1536]{2,1,0:T(8,128)(2,1)S(1)}, u32[]{:S(2)}, u32[]{:S(2)}) collective-permute-start(bf16[1,256,1536]{2,1,0:T(8,128)(2,1)S(1)} %get-tuple-element.95), channel_id=1, source_target_pairs={{0,1},{1,0},{2,3},{3,2},{4,5},{5,4},{6,7},{7,6},{8,9},{9,8},{10,11... | collective-permute-start | bytes 2359304 | tf_op jit(solution)/shard_map/ppermute | solution.py:54
  240.3 66.0 %collective-permute-start.2 = (bf16[2,256,1536]{2,1,0:T(8,128)(2,1)S(1)}, bf16[2,256,1536]{2,1,0:T(8,128)(2,1)S(1)}, u32[]{:S(2)}, u32[]{:S(2)}) collective-permute-start(bf16[2,256,1536]{2,1,0:T(8,128)(2,1)S(1)} %pad_maximum_fusion.9), channel_id=1, source_target_pairs={{0,1},{1,0},{2,3},{3,2},{4,5},{5,4},{6,7},{7,6},{8,9},{9,8},{10,11... | collective-permute-start | bytes 4718600 | tf_op jit(solution)/shard_map/ppermute | solution.py:54
  273.5 35.1 %collective-permute-start.4 = (bf16[2,256,1536]{2,1,0:T(8,128)(2,1)S(1)}, bf16[2,256,1536]{2,1,0:T(8,128)(2,1)S(1)}, u32[]{:S(2)}, u32[]{:S(2)}) collective-permute-start(bf16[2,256,1536]{2,1,0:T(8,128)(2,1)S(1)} %pad_maximum_fusion.10), channel_id=1, source_target_pairs={{0,4},{2,6},{4,0},{6,2},{8,12},{10,14},{12,8},{14,10},{16,20},{18,... | collective-permute-start | bytes 4718600 | tf_op jit(solution)/shard_map/ppermute | solution.py:54
  280.2 36.0 %collective-permute-start.13 = (bf16[2048,1536]{1,0:T(8,128)(2,1)}, bf16[2048,1536]{1,0:T(8,128)(2,1)}, u32[]{:S(2)}, u32[]{:S(2)}) collective-permute-start(bf16[2048,1536]{1,0:T(8,128)(2,1)} %bitcast.30), channel_id=1, source_target_pairs={{0,2},{2,0},{4,6},{6,4},{8,10},{10,8},{12,14},{14,12},{16,18},{18,... | collective-permute-start | bytes 18874376 | tf_op jit(solution)/shard_map/ppermute | solution.py:54
  312.2 14.5 %collective-permute-start.5 = (bf16[2048,1536]{1,0:T(8,128)(2,1)}, bf16[2048,1536]{1,0:T(8,128)(2,1)}, u32[]{:S(2)}, u32[]{:S(2)}) collective-permute-start(bf16[2048,1536]{1,0:T(8,128)(2,1)} %bitcast.14), channel_id=1, source_target_pairs={{0,2},{2,0},{4,6},{6,4},{8,10},{10,8},{12,14},{14,12},{16,18},{18,... | collective-permute-start | bytes 18874376 | tf_op jit(solution)/shard_map/ppermute | solution.py:54
  401.9 36.3 %copy-start.52 = (bf16[4096,1152]{1,0:T(8,128)(2,1)S(1)}, bf16[4096,1152]{1,0:T(8,128)(2,1)}, u32[]{:S(2)}) copy-start(bf16[4096,1152]{1,0:T(8,128)(2,1)} %get-tuple-element.53) | copy-start | bytes 28311556
  458.4 262.4 %reduce-scatter.3.cloned.1.call-start = ((), (), s32[]{:S(2)}) async-start(), calls=%async_computation.3 | async-start | bytes 8847360 | tf_op jit(solution)/shard_map/reduce_scatter | solution.py:848
  464.3 44.0 %collective-permute-start.14 = (bf16[2048,1536]{1,0:T(8,128)(2,1)}, bf16[2048,1536]{1,0:T(8,128)(2,1)}, u32[]{:S(2)}, u32[]{:S(2)}) collective-permute-start(bf16[2048,1536]{1,0:T(8,128)(2,1)} %slice.293), channel_id=1, source_target_pairs={{0,2},{2,0},{4,6},{6,4},{8,10},{10,8},{12,14},{14,12},{16,18},{18,... | collective-permute-start | bytes 18874376 | tf_op jit(solution)/shard_map/ppermute | solution.py:54
  534.4 22.2 %collective-permute-start.25 = (bf16[1,280,1536]{2,1,0:T(8,128)(2,1)}, bf16[1,280,1536]{2,1,0:T(8,128)(2,1)S(1)}, u32[]{:S(2)}, u32[]{:S(2)}) collective-permute-start(bf16[1,280,1536]{2,1,0:T(8,128)(2,1)} %reduce-scatter.5.cloned.1.call-done), channel_id=1, source_target_pairs={{0,1},{1,0},{2,3},{3,2},{4,5},{5,4},{6,7},{7,6},{8,9},{9,8},{10,11... | collective-permute-start | bytes 2580488 | tf_op jit(solution)/shard_map/ppermute | solution.py:54
  539.1 49.7 %collective-permute-start.15 = (bf16[2,256,1536]{2,1,0:T(8,128)(2,1)S(1)}, bf16[2,256,1536]{2,1,0:T(8,128)(2,1)S(1)}, u32[]{:S(2)}, u32[]{:S(2)}) collective-permute-start(bf16[2,256,1536]{2,1,0:T(8,128)(2,1)S(1)} %bitcast.158), channel_id=1, source_target_pairs={{0,1},{1,0},{2,3},{3,2},{4,5},{5,4},{6,7},{7,6},{8,9},{9,8},{10,11... | collective-permute-start | bytes 4718600 | tf_op jit(solution)/shard_map/ppermute | solution.py:54
  539.7 49.5 %collective-permute-start.16 = (bf16[2,256,1536]{2,1,0:T(8,128)(2,1)S(1)}, bf16[2,256,1536]{2,1,0:T(8,128)(2,1)S(1)}, u32[]{:S(2)}, u32[]{:S(2)}) collective-permute-start(bf16[2,256,1536]{2,1,0:T(8,128)(2,1)S(1)} %bitcast.157), channel_id=1, source_target_pairs={{0,4},{2,6},{4,0},{6,2},{8,12},{10,14},{12,8},{14,10},{16,20},{18,... | collective-permute-start | bytes 4718600 | tf_op jit(solution)/shard_map/ppermute | solution.py:54
  590.6 28.5 %collective-permute-start.17 = (bf16[256,1536]{1,0:T(8,128)(2,1)S(1)}, bf16[256,1536]{1,0:T(8,128)(2,1)}, u32[]{:S(2)}, u32[]{:S(2)}) collective-permute-start(bf16[256,1536]{1,0:T(8,128)(2,1)S(1)} %slice_bitcast_fusion.2), channel_id=1, source_target_pairs={{0,4},{2,6},{4,0},{6,2},{8,12},{10,14},{12,8},{14,10},{16,20},{18,... | collective-permute-start | bytes 2359304 | tf_op jit(solution)/shard_map/ppermute | solution.py:54
  592.1 28.6 %collective-permute-start.18 = (bf16[256,1536]{1,0:T(8,128)(2,1)}, bf16[256,1536]{1,0:T(8,128)(2,1)}, u32[]{:S(2)}, u32[]{:S(2)}) collective-permute-start(bf16[256,1536]{1,0:T(8,128)(2,1)} %slice_bitcast_fusion), channel_id=1, source_target_pairs={{0,1},{1,0},{2,3},{3,2},{4,5},{5,4},{6,7},{7,6},{8,9},{9,8},{10,11... | collective-permute-start | bytes 2359304 | tf_op jit(solution)/shard_map/ppermute | solution.py:54
  619.1 78.0 %collective-permute-start.19 = (bf16[2048,1536]{1,0:T(8,128)(2,1)}, bf16[2048,1536]{1,0:T(8,128)(2,1)}, u32[]{:S(2)}, u32[]{:S(2)}) collective-permute-start(bf16[2048,1536]{1,0:T(8,128)(2,1)} %slice.250), channel_id=1, source_target_pairs={{0,2},{2,0},{4,6},{6,4},{8,10},{10,8},{12,14},{14,12},{16,18},{18,... | collective-permute-start | bytes 18874376 | tf_op jit(solution)/shard_map/ppermute | solution.py:54
  664.3 8.0 copy-start.30
  664.4 14.3 %collective-permute-start.24 = (bf16[512,512]{1,0:T(8,128)(2,1)S(1)}, bf16[512,512]{1,0:T(8,128)(2,1)}, u32[]{:S(2)}, u32[]{:S(2)}) collective-permute-start(bf16[512,512]{1,0:T(8,128)(2,1)S(1)} %pad_maximum_fusion.14), channel_id=1, source_target_pairs={{0,1},{1,0},{2,3},{3,2},{4,5},{5,4},{6,7},{7,6},{8,9},{9,8},{10,11... | collective-permute-start | bytes 1572872 | tf_op jit(solution)/shard_map/ppermute | solution.py:54
  672.4 13.3 %copy-start.7 = (f32[512,128]{1,0:T(8,128)S(1)}, f32[512,128]{1,0:T(8,128)}, u32[]{:S(2)}) copy-start(f32[512,128]{1,0:T(8,128)} %copy-done.6) | copy-start | bytes 786436
  711.8 150.3 %collective-permute-start.21 = (bf16[2,256,1536]{2,1,0:T(8,128)(2,1)}, bf16[2,256,1536]{2,1,0:T(8,128)(2,1)}, u32[]{:S(2)}, u32[]{:S(2)}) collective-permute-start(bf16[2,256,1536]{2,1,0:T(8,128)(2,1)} %bitcast.42), channel_id=1, source_target_pairs={{0,4},{2,6},{4,0},{6,2},{8,12},{10,14},{12,8},{14,10},{16,20},{18,... | collective-permute-start | bytes 4718600 | tf_op jit(solution)/shard_map/ppermute | solution.py:54
  718.2 145.7 %collective-permute-start.20 = (bf16[2,256,1536]{2,1,0:T(8,128)(2,1)}, bf16[2,256,1536]{2,1,0:T(8,128)(2,1)}, u32[]{:S(2)}, u32[]{:S(2)}) collective-permute-start(bf16[2,256,1536]{2,1,0:T(8,128)(2,1)} %bitcast.40), channel_id=1, source_target_pairs={{0,1},{1,0},{2,3},{3,2},{4,5},{5,4},{6,7},{7,6},{8,9},{9,8},{10,11... | collective-permute-start | bytes 4718600 | tf_op jit(solution)/shard_map/ppermute | solution.py:54
  720.8 141.3 %copy-start.26 = (bf16[512,1536]{1,0:T(8,128)(2,1)S(1)}, bf16[512,1536]{1,0:T(8,128)(2,1)}, u32[]{:S(2)}) copy-start(bf16[512,1536]{1,0:T(8,128)(2,1)} %get-tuple-element.75) | copy-start | bytes 4718596
  866.3 10.6 %copy-start.40 = (f32[96,2048]{1,0:T(8,128)S(1)}, f32[96,2048]{1,0:T(8,128)}, u32[]{:S(2)}) copy-start(f32[96,2048]{1,0:T(8,128)} %get-tuple-element.63) | copy-start | bytes 2359300
  867.2 19.8 %collective-permute-start.22 = (bf16[256,1536]{1,0:T(8,128)(2,1)}, bf16[256,1536]{1,0:T(8,128)(2,1)}, u32[]{:S(2)}, u32[]{:S(2)}) collective-permute-start(bf16[256,1536]{1,0:T(8,128)(2,1)} %slice_bitcast_fusion.7), channel_id=1, source_target_pairs={{0,4},{2,6},{4,0},{6,2},{8,12},{10,14},{12,8},{14,10},{16,20},{18,... | collective-permute-start | bytes 2359304 | tf_op jit(solution)/shard_map/ppermute | solution.py:54
  867.8 20.5 %collective-permute-start.23 = (bf16[256,1536]{1,0:T(8,128)(2,1)S(1)}, bf16[256,1536]{1,0:T(8,128)(2,1)}, u32[]{:S(2)}, u32[]{:S(2)}) collective-permute-start(bf16[256,1536]{1,0:T(8,128)(2,1)S(1)} %slice_bitcast_fusion.6), channel_id=1, source_target_pairs={{0,1},{1,0},{2,3},{3,2},{4,5},{5,4},{6,7},{7,6},{8,9},{9,8},{10,11... | collective-permute-start | bytes 2359304 | tf_op jit(solution)/shard_map/ppermute | solution.py:54
  876.9 11.5 %copy-start.28 = (bf16[2,256,1536]{2,1,0:T(8,128)(2,1)S(1)}, bf16[2,256,1536]{2,1,0:T(8,128)(2,1)}, u32[]{:S(2)}) copy-start(bf16[2,256,1536]{2,1,0:T(8,128)(2,1)} %copy-done.27) | copy-start | bytes 4718596
  878.4 11.5 %copy-start.15 = (f32[512,1536]{1,0:T(8,128)S(1)}, f32[512,1536]{1,0:T(8,128)}, u32[]{:S(2)}) copy-start(f32[512,1536]{1,0:T(8,128)} %copy-done.13) | copy-start | bytes 9437188
  (37 other events, 126.8 us)
Sparse Core Ops, SparseCore 0:
  10.3 100.4 all-gather.5
  182.9 139.5 all-gather.3
  458.5 75.8 reduce-scatter.4
  536.5 123.6 reduce-scatter.2

commit v4 on v3

--- a/solution.py
+++ b/solution.py
@@ -544,6 +544,8 @@
         arrive(copies)
 
     running = [steps(k) for k in range(count)] + [exchange()]
+    for _ in range(2):
+        next(running[0])
     while running:
         for one in list(running):
             if next(one, "done") == "done":
@@ -927,13 +929,14 @@
         return jnp.concatenate(got, axis=0)
 
     stages = list(range(1, len(slow_a)))[::-1]
-    grad_all = spread(after(upstream_low, pairs))
+    grad_all = spread(upstream_low)
     rows_all = spread(normed_two_low)
     both = product(rows_all, units_w)
     hidden, units_grad = hidden_units(both, grad_all, down_w)
+    down_grad = product_left(hidden, grad_all).astype(low)
+    units_grad, down_grad = lax.optimization_barrier((units_grad, down_grad))
+    down_grad = down_grad[:ff_here]
     partial = product_right(units_grad, units_w).astype(low)
-    down_grad = product_left(after(hidden, partial), grad_all).astype(low)
-    down_grad = down_grad[:ff_here]
     down_line = line_reduce(down_grad.reshape(outer, ff_own, width))
     back = hop_core(partial)
     rows_late, grad_late = lax.optimization_barrier((rows_all, units_grad, back, down_grad))[:2]
@@ -1004,8 +1007,11 @@
     def by_owner(partial):
         return partial.reshape(outer, INNER, -1, partial.shape[-1])
 
-    heads_out, out_w_out, small_out, units_got = reduce_shares(
-        units_line.reshape(INNER, share, 2 * ff_pad), by_owner(head_w_grad), by_owner(out_w_grad), by_owner(small_grad)
+    out_w_out, heads_out, small_out, units_got = reduce_shares(
+        units_line.reshape(INNER, share, 2 * ff_pad),
+        by_owner(out_w_grad),
+        by_owner(head_w_grad),
+        by_owner(small_grad),
     )
     small_out = small_out[0]
     gate_out, up_out = join_units(info, units_got, outer, ff_own)

time: 907 us -> 903 us (level); the launches traced: 899 us -> 885 us
  waiting for transfers between devices: 168 us -> 148 us
    reduce_scatter x2, waiting for transfers between devices: 17.1 us -> 0.01 us  [line_reduce(): lax.psum_scatter(value, 'wt', scatter_dimension=0, axis_index_groups=line...]
  transfers between devices with their start and end apart: 30 -> 30, of which waited for: 11 -> 10; matrix products, arithmetic and copies ran while one was open for 24% -> 28% of each run, Pallas kernels for 36% -> 37%
where the time goes in v4:
time: 903 us; the launch traced here: 885 us
  Pallas kernels  364 us (40%)
  matrix products  181 us (20%)
  waiting for transfers between devices  148 us (16%)
  other arithmetic  90.9 us (10%)
  local copies, waits for them, and re-layouts  59.3 us (7%)
  starting transfers between devices  25.8 us (3%)
  between operations  15.7 us (2%)
    pallas_call x1, Pallas kernels, reduce_shares(): pl.pallas_call(functools.partial(reduce_kernel, outer, seq_count, count),...  143 us
    ppermute x23, waiting for transfers between devices, swap(): return lax.ppermute(value, axis, [(i, i ^ bit) for i in range(count)])  134 us
    dot_general x4, matrix products, product_left(): lax.dot_general(left, right, (((0,), (0,)), ((), ())), preferred_element_...  69.9 us
    pallas_call x1, Pallas kernels, gather_line(): pl.pallas_call(functools.partial(line_kernel, outer, seq_count), in_specs...  64.4 us
    dot_general x3, matrix products, product(): return jnp.dot(left, right, preferred_element_type=full)  63.4 us
    pallas_call x1, Pallas kernels, gather_project(): pl.pallas_call(functools.partial(gather_kernel, outer, seq_count), in_spe...  56.5 us
    dot_general x3, matrix products, product_right(): lax.dot_general(left, right, (((1,), (1,)), ((), ())), preferred_element_...  47.3 us
    pallas_call x1, Pallas kernels, hidden_units(): pl.pallas_call(hidden_kernel, grid=(total // block,), in_specs=[pl.BlockS...  35.8 us
  transfers between devices with their start and end apart: 30, of which 10 were waited for; matrix products, arithmetic and copies ran while one was open for 28% of the time, Pallas kernels for 37%

profile of v4, /device:TPU:0, one launch (start us, length us, event | category | flops | bytes accessed | tf_op | source)
XLA Modules:
  0.0 884.9 jit_solution(11331159974971290175)
XLA Ops:
  20.2 64.4 %gather_line.1 = (bf16[4,96,1024]{2,1,0:T(8,128)(2,1)}, bf16[4,96,768]{2,1,0:T(8,128)(2,1)}, bf16[4,16,128]{2,1,0:T(8,128)(2,1)}) custom-call(bf16[96,2048]{1,0:T(8,128)(2,1)} %pad_maximum_fusion.15.p_ref, bf16[96,1536]{1,0:T(8,128)(2,1)} %convert_element_type.193.wo_ref, bf16[16,128]{1,0:T(8,128)(2,1)} %pad.43.s_ref), custom_call_target="tpu_custom_call" | custom-call | bytes 22020096 | tf_op jit(solution)/shard_map/gather_line/pallas_call | solution.py:194
  87.5 56.5 %gather_project.1 = (bf16[512,1536]{1,0:T(8,128)(2,1)S(1)}, bf16[512,2048]{1,0:T(8,128)(2,1)}, f32[8,2048]{1,0:T(8,128)S(1)}, bf16[4,4,96,2048]{3,2,1,0:T(8,128)(2,1)}, bf16[4,4,96,1536]{3,2,1,0:T(8,128)(2,1)}) custom-call(bf16[512,1536]{1,0:T(8,128)(2,1)S(1)} %bitcast.144, bf16[4,96,1024]{2,1,0:T(8,128)(2,1)S(1)} %copy-done.8, ...), custom_call_target="tpu_custom_call" | custom-call | flops 25769803776 | bytes 22020096 | tf_op jit(solution)/shard_map/gather_project/pallas_call | solution.py:380
  148.9 5.0 split_units.1
  153.9 2.8 fusion.32
  156.6 2.2 collective-permute-start.6
  165.7 6.5 collective-permute-done.7
  172.2 7.5 collective-permute-done.8
  183.2 2.3 pad_maximum_fusion.13
  185.4 22.7 %attend_forward.1 = bf16[512,1536]{1,0:T(8,128)(2,1)} custom-call(s32[1,1024]{1,0:T(1,128)} %compare_select_fusion.kpos_ref, bf16[512,2048]{1,0:T(8,128)(2,1)} %get-tuple-element.44.q_ref, bf16[1024,512]{1,0:T(8,128)(2,1)} %bitcast.160, bf16[1024,512]{1,0:T(8,128)(2,1)} %bitcast.161), custom_call_target="tpu_custom_call" | custom-call | flops 9663676416 | bytes 4194304 | tf_op jit(solution)/shard_map/attend_forward/pallas_call | solution.py:720
  208.1 5.1 multiply_reduce_fusion.2
  221.8 16.4 %collective-permute-done.1 = bf16[1,256,1536]{2,1,0:T(8,128)(2,1)S(1)} collective-permute-done((bf16[1,256,1536]{2,1,0:T(8,128)(2,1)S(1)}, bf16[1,256,1536]{2,1,0:T(8,128)(2,1)S(1)}, u32[]{:S(2)}, u32[]{:S(2)}) %collective-permute-start.1) | collective-permute-done | bytes 786464 | tf_op jit(solution)/shard_map/ppermute | solution.py:54
  238.4 30.8 %collective-permute-done.3 = bf16[1,256,1536]{2,1,0:T(8,128)(2,1)S(1)} collective-permute-done((bf16[1,256,1536]{2,1,0:T(8,128)(2,1)S(1)}, bf16[1,256,1536]{2,1,0:T(8,128)(2,1)S(1)}, u32[]{:S(2)}, u32[]{:S(2)}) %collective-permute-start.3) | collective-permute-done | bytes 786464 | tf_op jit(solution)/shard_map/ppermute | solution.py:54
  269.4 2.5 collective-permute-start.4
  275.2 3.2 pad_maximum_fusion.3
  278.4 24.5 %collective-permute-done.2 = bf16[2,256,1536]{2,1,0:T(8,128)(2,1)S(1)} collective-permute-done((bf16[2,256,1536]{2,1,0:T(8,128)(2,1)S(1)}, bf16[2,256,1536]{2,1,0:T(8,128)(2,1)S(1)}, u32[]{:S(2)}, u32[]{:S(2)}) %collective-permute-start.2) | collective-permute-done | bytes 1572896 | tf_op jit(solution)/shard_map/ppermute | solution.py:54
  303.2 3.1 collective-permute-done.4
  306.6 3.3 pad_maximum_fusion.2
  310.9 4.0 pad.44.down_ref
  314.9 10.5 %pad_maximum_fusion.1.grad_ref = bf16[4096,1536]{1,0:T(8,128)(2,1)} fusion(bf16[2048,1536]{1,0:T(8,128)(2,1)} %collective-permute-done.13, bf16[2048,1536]{1,0:T(8,128)(2,1)} %bitcast.30), kind=kLoop, calls=%fused_computation.3 | loop fusion | flops 25165824 | bytes 25165824 | tf_op jit(solution)/shard_map/concatenate | solution.py:916
  325.4 39.3 %fusion.29.both_ref = f32[4096,2304]{1,0:T(8,128)} fusion(bf16[1536,2304]{1,0:T(8,128)(2,1)} %bitcast.165, bf16[2048,1536]{1,0:T(8,128)(2,1)} %collective-permute-done.5, bf16[2048,1536]{1,0:T(8,128)(2,1)} %bitcast.14), kind=kOutput, calls=%fused_computation.141 | convolution fusion | flops 29016195072 | bytes 57409536 | tf_op jit(solution)/shard_map/dot_general | solution.py:27
  364.7 35.8 %hidden_units.1 = (bf16[4096,1152]{1,0:T(8,128)(2,1)}, bf16[4096,2304]{1,0:T(8,128)(2,1)}) custom-call(f32[4096,2304]{1,0:T(8,128)} %fusion.29.both_ref, bf16[4096,1536]{1,0:T(8,128)(2,1)} %pad_maximum_fusion.1.grad_ref, bf16[1152,1536]{1,0:T(8,128)(2,1)} %pad.44.down_ref), custom_call_target="tpu_custom_call" | custom-call | flops 14495514624 | bytes 82182144 | tf_op jit(solution)/shard_map/hidden_units/pallas_call | solution.py:665
  400.5 20.3 %convolution_convert_fusion.5 = bf16[1152,1536]{1,0:T(8,128)(2,1)S(1)} fusion(bf16[4096,1152]{1,0:T(8,128)(2,1)} %get-tuple-element.53, bf16[2048,1536]{1,0:T(8,128)(2,1)} %collective-permute-done.13, bf16[2048,1536]{1,0:T(8,128)(2,1)} %bitcast.30), kind=kOutput, calls=%fused_computation.9 | convolution fusion | flops 14522449920 | bytes 25559040 | tf_op jit(solution)/shard_map/dot_general | solution.py:31
  422.9 34.9 %convolution_convert_fusion.1 = bf16[4096,1536]{1,0:T(8,128)(2,1)S(1)} fusion(bf16[4096,2304]{1,0:T(8,128)(2,1)} %get-tuple-element.52, bf16[1536,2304]{1,0:T(8,128)(2,1)} %bitcast.166), kind=kOutput, calls=%fused_computation.1 | convolution fusion | flops 28997320704 | bytes 38535168 | tf_op jit(solution)/shard_map/dot_general | solution.py:35
  457.9 3.0 slice.295
  460.9 3.7 copy-done.17
  465.5 6.2 pad_maximum_fusion
  471.7 36.4 %convolution_convert_fusion.2 = bf16[1536,2304]{1,0:T(8,128)(2,1)} fusion(bf16[4096,1536]{1,0:T(8,128)(2,1)S(1)} %pad_maximum_fusion, bf16[4096,2304]{1,0:T(8,128)(2,1)} %get-tuple-element.52), kind=kOutput, calls=%fused_computation.6 | convolution fusion | flops 28994568192 | bytes 38535168 | tf_op jit(solution)/shard_map/dot_general | solution.py:31
  508.2 9.0 %add_convert_fusion.1 = bf16[2048,1536]{1,0:T(8,128)(2,1)} fusion(bf16[2048,1536]{1,0:T(8,128)(2,1)} %collective-permute-done.14, bf16[4096,1536]{1,0:T(8,128)(2,1)} %copy-done.17), kind=kLoop, calls=%fused_computation.5 | loop fusion | flops 12582912 | bytes 18874368 | tf_op jit(solution)/shard_map/convert_element_type | solution.py:920
  518.8 3.2 fusion.31
  524.2 15.3 %collective-permute-done.25 = bf16[1,280,1536]{2,1,0:T(8,128)(2,1)S(1)} collective-permute-done((bf16[1,280,1536]{2,1,0:T(8,128)(2,1)}, bf16[1,280,1536]{2,1,0:T(8,128)(2,1)S(1)}, u32[]{:S(2)}, u32[]{:S(2)}) %collective-permute-start.25) | collective-permute-done | bytes 860192 | tf_op jit(solution)/shard_map/ppermute | solution.py:54
  539.8 2.3 bitcast_convert_fusion
  542.1 30.5 %collective-permute-done.15 = bf16[2,256,1536]{2,1,0:T(8,128)(2,1)S(1)} collective-permute-done((bf16[2,256,1536]{2,1,0:T(8,128)(2,1)S(1)}, bf16[2,256,1536]{2,1,0:T(8,128)(2,1)S(1)}, u32[]{:S(2)}, u32[]{:S(2)}) %collective-permute-start.15) | collective-permute-done | bytes 1572896 | tf_op jit(solution)/shard_map/ppermute | solution.py:54
  576.5 19.0 %convolution_convert_fusion = bf16[4096,1536]{1,0:T(8,128)(2,1)S(1)} fusion(bf16[4096,1152]{1,0:T(8,128)(2,1)} %get-tuple-element.53, bf16[1120,1536]{1,0:T(8,128)(2,1)S(1)} %copy-done.28), kind=kOutput, calls=%fused_computation | convolution fusion | flops 14501806080 | bytes 25460736 | tf_op jit(solution)/shard_map/dot_general | solution.py:27
  595.6 3.3 slice.250
  598.8 3.2 copy-done.16
  609.7 3.7 convolution_convert_fusion.6.g_ref
  613.4 31.2 %attend_backward.1 = (bf16[512,1536]{1,0:T(8,128)(2,1)}, f32[1024,256]{1,0:T(8,128)}, f32[1024,256]{1,0:T(8,128)}) custom-call(s32[1,1024]{1,0:T(1,128)} %compare_select_fusion.kpos_ref, f32[512,128]{1,0:T(8,128)} %copy-done.4, f32[512,128]{1,0:T(8,128)} %copy-done.6, bf16[512,2048]{1,0:T(8,128)(2,1)} %get-tuple-element.44.q_ref, ...), custom_call_target="tpu_custom_call" | custom-call | flops 24159191040 | bytes 9437184 | tf_op jit(solution)/shard_map/attend_backward/pallas_call | solution.py:788
  648.5 7.3 convolution_convert_fusion.4
  655.8 5.8 collective-permute-done.24
  664.6 2.1 reshape.299
  670.4 8.7 fusion.7
  680.0 8.9 %add_convert_fusion = bf16[2048,1536]{1,0:T(8,128)(2,1)} fusion(bf16[2048,1536]{1,0:T(8,128)(2,1)} %collective-permute-done.19, bf16[4096,1536]{1,0:T(8,128)(2,1)} %copy-done.16), kind=kLoop, calls=%fused_computation.4 | loop fusion | flops 12582912 | bytes 18874368 | tf_op jit(solution)/shard_map/convert_element_type | solution.py:920
  689.0 5.8 fusion.30
  696.0 5.9 convolution_convert_fusion.3
  704.8 142.6 %reduce_shares.1 = (f32[96,1536]{1,0:T(8,128)}, f32[96,2048]{1,0:T(8,128)}, f32[16,512]{1,0:T(8,128)}, bf16[2,4,96,2304]{3,2,1,0:T(8,128)(2,1)}) custom-call(bf16[4,96,2304]{2,1,0:T(8,128)(2,1)} %bitcast.156, bf16[4,4,96,1536]{3,2,1,0:T(8,128)(2,1)} %bitcast.153, bf16[4,4,96,2048]{3,2,1,0:T(8,128)(2,1)} %bitcast.148, bf16[4,4,16,512]{3,2,1,0:T(8,128)(2,1)} %bitcast.159), custom_call_target="tpu_custom_call" | custom-call | bytes 90177536 | tf_op jit(solution)/shard_map/reduce_shares/pallas_call | solution.py:572
  850.7 2.3 fusion.11
  857.4 6.1 join_units.1
  865.0 7.7 collective-permute-done.22
  (242 shorter events, 92.3 us)
Async XLA Ops:
  7.2 7.6 copy-start.40
  7.2 303.7 %all-gather.6.cloned.1.call-start = ((), (), s32[]{:S(2)}) async-start(), calls=%async_computation.5 | async-start | bytes 4300800 | tf_op jit(solution)/shard_map/all_gather | solution.py:847
  10.2 74.5 %copy-start.2 = (bf16[1,512,1536]{2,1,0:T(8,128)(2,1)S(1)}, bf16[1,512,1536]{2,1,0:T(8,128)(2,1)}, u32[]{:S(2)}) copy-start(bf16[1,512,1536]{2,1,0:T(8,128)(2,1)} %param.15) | copy-start | bytes 4718596
  10.2 315.2 %all-gather.4.cloned.1.call-start = ((), (), s32[]{:S(2)}) async-start(), calls=%async_computation.2 | async-start | bytes 8847360 | tf_op jit(solution)/shard_map/all_gather | solution.py:847
  19.4 124.6 %copy-start.4 = (f32[512,128]{1,0:T(8,128)}, f32[512,128]{1,0:T(8,128)S(1)}, u32[]{:S(2)}) copy-start(f32[512,128]{1,0:T(8,128)S(1)} %get-tuple-element.121.cos_ref) | copy-start | bytes 786436
  19.4 124.6 %copy-start.6 = (f32[512,128]{1,0:T(8,128)}, f32[512,128]{1,0:T(8,128)S(1)}, u32[]{:S(2)}) copy-start(f32[512,128]{1,0:T(8,128)S(1)} %get-tuple-element.122.sin_ref) | copy-start | bytes 786436
  147.0 36.1 %collective-permute-start = (bf16[1,512,512]{2,1,0:T(8,128)(2,1)}, bf16[1,512,512]{2,1,0:T(8,128)(2,1)}, u32[]{:S(2)}, u32[]{:S(2)}) collective-permute-start(bf16[1,512,512]{2,1,0:T(8,128)(2,1)} %slice_bitcast_fusion.10), channel_id=1, source_target_pairs={{0,1},{1,0},{2,3},{3,2},{4,5},{5,4},{6,7},{7,6},{8,9},{9,8},{10,11... | collective-permute-start | bytes 1572872 | tf_op jit(solution)/shard_map/ppermute | solution.py:54
  153.9 6.9 copy-start.20
  156.6 7.6 collective-permute-start.6
  158.8 13.4 %collective-permute-start.7 = (bf16[96,2304]{1,0:T(8,128)(2,1)}, bf16[96,2304]{1,0:T(8,128)(2,1)}, u32[]{:S(2)}, u32[]{:S(2)}) collective-permute-start(bf16[96,2304]{1,0:T(8,128)(2,1)} %get-tuple-element.88), channel_id=1, source_target_pairs={{0,4},{2,6},{4,0},{6,2},{8,12},{10,14},{12,8},{14,10},{16,20},{18,... | collective-permute-start | bytes 1327112 | tf_op jit(solution)/shard_map/ppermute | solution.py:863
  159.3 20.4 %collective-permute-start.8 = (bf16[96,2304]{1,0:T(8,128)(2,1)}, bf16[96,2304]{1,0:T(8,128)(2,1)}, u32[]{:S(2)}, u32[]{:S(2)}) collective-permute-start(bf16[96,2304]{1,0:T(8,128)(2,1)} %get-tuple-element.87), channel_id=1, source_target_pairs={{0,6},{2,4},{4,2},{6,0},{8,14},{10,12},{12,10},{14,8},{16,22},{18,... | collective-permute-start | bytes 1327112 | tf_op jit(solution)/shard_map/ppermute | solution.py:863
  162.3 51.9 %collective-permute-start.9 = (bf16[1,256,1536]{2,1,0:T(8,128)(2,1)}, bf16[1,256,1536]{2,1,0:T(8,128)(2,1)}, u32[]{:S(2)}, u32[]{:S(2)}) collective-permute-start(bf16[1,256,1536]{2,1,0:T(8,128)(2,1)} %get-tuple-element.92), channel_id=1, source_target_pairs={{0,4},{2,6},{4,0},{6,2},{8,12},{10,14},{12,8},{14,10},{16,20},{18,... | collective-permute-start | bytes 2359304 | tf_op jit(solution)/shard_map/ppermute | solution.py:54
  164.2 49.7 %copy-start.38 = (f32[1536]{0:T(1024)}, f32[1536]{0:T(1024)S(1)}, u32[]{:S(2)}) copy-start(f32[1536]{0:T(1024)S(1)} %get-tuple-element.73) | copy-start | bytes 18436
  164.2 54.3 %collective-permute-start.11 = (bf16[1,256,1536]{2,1,0:T(8,128)(2,1)}, bf16[1,256,1536]{2,1,0:T(8,128)(2,1)}, u32[]{:S(2)}, u32[]{:S(2)}) collective-permute-start(bf16[1,256,1536]{2,1,0:T(8,128)(2,1)} %get-tuple-element.93), channel_id=1, source_target_pairs={{0,1},{1,0},{2,3},{3,2},{4,5},{5,4},{6,7},{7,6},{8,9},{9,8},{10,11... | collective-permute-start | bytes 2359304 | tf_op jit(solution)/shard_map/ppermute | solution.py:54
  182.9 334.3 %reduce-scatter.5.cloned.1.call-start = ((), (), s32[]{:S(2)}) async-start(), calls=%async_computation.4 | async-start | bytes 4300800 | tf_op jit(solution)/shard_map/reduce_scatter | solution.py:850
  215.9 55.9 %collective-permute-start.10 = (bf16[2,256,1536]{2,1,0:T(8,128)(2,1)S(1)}, bf16[2,256,1536]{2,1,0:T(8,128)(2,1)S(1)}, u32[]{:S(2)}, u32[]{:S(2)}) collective-permute-start(bf16[2,256,1536]{2,1,0:T(8,128)(2,1)S(1)} %pad_maximum_fusion.11), channel_id=1, source_target_pairs={{0,1},{1,0},{2,3},{3,2},{4,5},{5,4},{6,7},{7,6},{8,9},{9,8},{10,11... | collective-permute-start | bytes 4718600 | tf_op jit(solution)/shard_map/ppermute | solution.py:54
  217.7 20.5 %collective-permute-start.1 = (bf16[1,256,1536]{2,1,0:T(8,128)(2,1)S(1)}, bf16[1,256,1536]{2,1,0:T(8,128)(2,1)S(1)}, u32[]{:S(2)}, u32[]{:S(2)}) collective-permute-start(bf16[1,256,1536]{2,1,0:T(8,128)(2,1)S(1)} %get-tuple-element.94), channel_id=1, source_target_pairs={{0,4},{2,6},{4,0},{6,2},{8,12},{10,14},{12,8},{14,10},{16,20},{18,... | collective-permute-start | bytes 2359304 | tf_op jit(solution)/shard_map/ppermute | solution.py:54
  220.0 53.5 %collective-permute-start.12 = (bf16[2,256,1536]{2,1,0:T(8,128)(2,1)S(1)}, bf16[2,256,1536]{2,1,0:T(8,128)(2,1)S(1)}, u32[]{:S(2)}, u32[]{:S(2)}) collective-permute-start(bf16[2,256,1536]{2,1,0:T(8,128)(2,1)S(1)} %pad_maximum_fusion.12), channel_id=1, source_target_pairs={{0,4},{2,6},{4,0},{6,2},{8,12},{10,14},{12,8},{14,10},{16,20},{18,... | collective-permute-start | bytes 4718600 | tf_op jit(solution)/shard_map/ppermute | solution.py:54
  221.4 47.8 %collective-permute-start.3 = (bf16[1,256,1536]{2,1,0:T(8,128)(2,1)S(1)}, bf16[1,256,1536]{2,1,0:T(8,128)(2,1)S(1)}, u32[]{:S(2)}, u32[]{:S(2)}) collective-permute-start(bf16[1,256,1536]{2,1,0:T(8,128)(2,1)S(1)} %get-tuple-element.95), channel_id=1, source_target_pairs={{0,1},{1,0},{2,3},{3,2},{4,5},{5,4},{6,7},{7,6},{8,9},{9,8},{10,11... | collective-permute-start | bytes 2359304 | tf_op jit(solution)/shard_map/ppermute | solution.py:54
  238.3 64.6 %collective-permute-start.2 = (bf16[2,256,1536]{2,1,0:T(8,128)(2,1)S(1)}, bf16[2,256,1536]{2,1,0:T(8,128)(2,1)S(1)}, u32[]{:S(2)}, u32[]{:S(2)}) collective-permute-start(bf16[2,256,1536]{2,1,0:T(8,128)(2,1)S(1)} %pad_maximum_fusion.9), channel_id=1, source_target_pairs={{0,1},{1,0},{2,3},{3,2},{4,5},{5,4},{6,7},{7,6},{8,9},{9,8},{10,11... | collective-permute-start | bytes 4718600 | tf_op jit(solution)/shard_map/ppermute | solution.py:54
  269.4 37.0 %collective-permute-start.4 = (bf16[2,256,1536]{2,1,0:T(8,128)(2,1)S(1)}, bf16[2,256,1536]{2,1,0:T(8,128)(2,1)S(1)}, u32[]{:S(2)}, u32[]{:S(2)}) collective-permute-start(bf16[2,256,1536]{2,1,0:T(8,128)(2,1)S(1)} %pad_maximum_fusion.10), channel_id=1, source_target_pairs={{0,4},{2,6},{4,0},{6,2},{8,12},{10,14},{12,8},{14,10},{16,20},{18,... | collective-permute-start | bytes 4718600 | tf_op jit(solution)/shard_map/ppermute | solution.py:54
  278.4 36.5 %collective-permute-start.13 = (bf16[2048,1536]{1,0:T(8,128)(2,1)}, bf16[2048,1536]{1,0:T(8,128)(2,1)}, u32[]{:S(2)}, u32[]{:S(2)}) collective-permute-start(bf16[2048,1536]{1,0:T(8,128)(2,1)} %bitcast.30), channel_id=1, source_target_pairs={{0,2},{2,0},{4,6},{6,4},{8,10},{10,8},{12,14},{14,12},{16,18},{18,... | collective-permute-start | bytes 18874376 | tf_op jit(solution)/shard_map/ppermute | solution.py:54
  309.9 15.4 %collective-permute-start.5 = (bf16[2048,1536]{1,0:T(8,128)(2,1)}, bf16[2048,1536]{1,0:T(8,128)(2,1)}, u32[]{:S(2)}, u32[]{:S(2)}) collective-permute-start(bf16[2048,1536]{1,0:T(8,128)(2,1)} %bitcast.14), channel_id=1, source_target_pairs={{0,2},{2,0},{4,6},{6,4},{8,10},{10,8},{12,14},{14,12},{16,18},{18,... | collective-permute-start | bytes 18874376 | tf_op jit(solution)/shard_map/ppermute | solution.py:54
  422.9 281.9 %reduce-scatter.3.cloned.1.call-start = ((), (), s32[]{:S(2)}) async-start(), calls=%async_computation.3 | async-start | bytes 8847360 | tf_op jit(solution)/shard_map/reduce_scatter | solution.py:850
  464.6 43.6 %collective-permute-start.14 = (bf16[2048,1536]{1,0:T(8,128)(2,1)}, bf16[2048,1536]{1,0:T(8,128)(2,1)}, u32[]{:S(2)}, u32[]{:S(2)}) collective-permute-start(bf16[2048,1536]{1,0:T(8,128)(2,1)} %slice.295), channel_id=1, source_target_pairs={{0,2},{2,0},{4,6},{6,4},{8,10},{10,8},{12,14},{14,12},{16,18},{18,... | collective-permute-start | bytes 18874376 | tf_op jit(solution)/shard_map/ppermute | solution.py:54
  517.2 6.9 copy-start.35
  517.2 22.2 %collective-permute-start.25 = (bf16[1,280,1536]{2,1,0:T(8,128)(2,1)}, bf16[1,280,1536]{2,1,0:T(8,128)(2,1)S(1)}, u32[]{:S(2)}, u32[]{:S(2)}) collective-permute-start(bf16[1,280,1536]{2,1,0:T(8,128)(2,1)} %reduce-scatter.5.cloned.1.call-done), channel_id=1, source_target_pairs={{0,1},{1,0},{2,3},{3,2},{4,5},{5,4},{6,7},{7,6},{8,9},{9,8},{10,11... | collective-permute-start | bytes 2580488 | tf_op jit(solution)/shard_map/ppermute | solution.py:54
  522.1 50.6 %collective-permute-start.15 = (bf16[2,256,1536]{2,1,0:T(8,128)(2,1)S(1)}, bf16[2,256,1536]{2,1,0:T(8,128)(2,1)S(1)}, u32[]{:S(2)}, u32[]{:S(2)}) collective-permute-start(bf16[2,256,1536]{2,1,0:T(8,128)(2,1)S(1)} %bitcast.158), channel_id=1, source_target_pairs={{0,1},{1,0},{2,3},{3,2},{4,5},{5,4},{6,7},{7,6},{8,9},{9,8},{10,11... | collective-permute-start | bytes 4718600 | tf_op jit(solution)/shard_map/ppermute | solution.py:54
  522.6 50.5 %collective-permute-start.16 = (bf16[2,256,1536]{2,1,0:T(8,128)(2,1)S(1)}, bf16[2,256,1536]{2,1,0:T(8,128)(2,1)S(1)}, u32[]{:S(2)}, u32[]{:S(2)}) collective-permute-start(bf16[2,256,1536]{2,1,0:T(8,128)(2,1)S(1)} %bitcast.157), channel_id=1, source_target_pairs={{0,4},{2,6},{4,0},{6,2},{8,12},{10,14},{12,8},{14,10},{16,20},{18,... | collective-permute-start | bytes 4718600 | tf_op jit(solution)/shard_map/ppermute | solution.py:54
  574.5 27.6 %collective-permute-start.17 = (bf16[256,1536]{1,0:T(8,128)(2,1)S(1)}, bf16[256,1536]{1,0:T(8,128)(2,1)}, u32[]{:S(2)}, u32[]{:S(2)}) collective-permute-start(bf16[256,1536]{1,0:T(8,128)(2,1)S(1)} %slice_bitcast_fusion.2), channel_id=1, source_target_pairs={{0,4},{2,6},{4,0},{6,2},{8,12},{10,14},{12,8},{14,10},{16,20},{18,... | collective-permute-start | bytes 2359304 | tf_op jit(solution)/shard_map/ppermute | solution.py:54
  575.6 28.1 %collective-permute-start.18 = (bf16[256,1536]{1,0:T(8,128)(2,1)}, bf16[256,1536]{1,0:T(8,128)(2,1)}, u32[]{:S(2)}, u32[]{:S(2)}) collective-permute-start(bf16[256,1536]{1,0:T(8,128)(2,1)} %slice_bitcast_fusion), channel_id=1, source_target_pairs={{0,1},{1,0},{2,3},{3,2},{4,5},{5,4},{6,7},{7,6},{8,9},{9,8},{10,11... | collective-permute-start | bytes 2359304 | tf_op jit(solution)/shard_map/ppermute | solution.py:54
  602.1 77.9 %collective-permute-start.19 = (bf16[2048,1536]{1,0:T(8,128)(2,1)}, bf16[2048,1536]{1,0:T(8,128)(2,1)}, u32[]{:S(2)}, u32[]{:S(2)}) collective-permute-start(bf16[2048,1536]{1,0:T(8,128)(2,1)} %slice.250), channel_id=1, source_target_pairs={{0,2},{2,0},{4,6},{6,4},{8,10},{10,8},{12,14},{14,12},{16,18},{18,... | collective-permute-start | bytes 18874376 | tf_op jit(solution)/shard_map/ppermute | solution.py:54
  647.4 8.4 copy-start.27
  647.4 14.2 %collective-permute-start.24 = (bf16[512,512]{1,0:T(8,128)(2,1)S(1)}, bf16[512,512]{1,0:T(8,128)(2,1)}, u32[]{:S(2)}, u32[]{:S(2)}) collective-permute-start(bf16[512,512]{1,0:T(8,128)(2,1)S(1)} %pad_maximum_fusion.14), channel_id=1, source_target_pairs={{0,1},{1,0},{2,3},{3,2},{4,5},{5,4},{6,7},{7,6},{8,9},{9,8},{10,11... | collective-permute-start | bytes 1572872 | tf_op jit(solution)/shard_map/ppermute | solution.py:54
  655.8 12.8 %copy-start.7 = (f32[512,128]{1,0:T(8,128)S(1)}, f32[512,128]{1,0:T(8,128)}, u32[]{:S(2)}) copy-start(f32[512,128]{1,0:T(8,128)} %copy-done.6) | copy-start | bytes 786436
  688.9 7.0 copy-start.12
  688.9 7.0 copy-start.31
  688.9 7.0 copy-start.34
  694.8 154.1 %collective-permute-start.21 = (bf16[2,256,1536]{2,1,0:T(8,128)(2,1)}, bf16[2,256,1536]{2,1,0:T(8,128)(2,1)}, u32[]{:S(2)}, u32[]{:S(2)}) collective-permute-start(bf16[2,256,1536]{2,1,0:T(8,128)(2,1)} %bitcast.42), channel_id=1, source_target_pairs={{0,4},{2,6},{4,0},{6,2},{8,12},{10,14},{12,8},{14,10},{16,20},{18,... | collective-permute-start | bytes 4718600 | tf_op jit(solution)/shard_map/ppermute | solution.py:54
  695.9 6.8 copy-start.19
  695.9 6.8 copy-start.29
  701.9 148.8 %collective-permute-start.20 = (bf16[2,256,1536]{2,1,0:T(8,128)(2,1)}, bf16[2,256,1536]{2,1,0:T(8,128)(2,1)}, u32[]{:S(2)}, u32[]{:S(2)}) collective-permute-start(bf16[2,256,1536]{2,1,0:T(8,128)(2,1)} %bitcast.40), channel_id=1, source_target_pairs={{0,1},{1,0},{2,3},{3,2},{4,5},{5,4},{6,7},{7,6},{8,9},{9,8},{10,11... | collective-permute-start | bytes 4718600 | tf_op jit(solution)/shard_map/ppermute | solution.py:54
  704.8 144.0 %copy-start.23 = (bf16[512,1536]{1,0:T(8,128)(2,1)S(1)}, bf16[512,1536]{1,0:T(8,128)(2,1)}, u32[]{:S(2)}) copy-start(bf16[512,1536]{1,0:T(8,128)(2,1)} %get-tuple-element.75) | copy-start | bytes 4718596
  853.0 10.4 %copy-start.36 = (f32[96,2048]{1,0:T(8,128)S(1)}, f32[96,2048]{1,0:T(8,128)}, u32[]{:S(2)}) copy-start(f32[96,2048]{1,0:T(8,128)} %get-tuple-element.63) | copy-start | bytes 2359300
  854.0 18.8 %collective-permute-start.22 = (bf16[256,1536]{1,0:T(8,128)(2,1)}, bf16[256,1536]{1,0:T(8,128)(2,1)}, u32[]{:S(2)}, u32[]{:S(2)}) collective-permute-start(bf16[256,1536]{1,0:T(8,128)(2,1)} %slice_bitcast_fusion.9), channel_id=1, source_target_pairs={{0,4},{2,6},{4,0},{6,2},{8,12},{10,14},{12,8},{14,10},{16,20},{18,... | collective-permute-start | bytes 2359304 | tf_op jit(solution)/shard_map/ppermute | solution.py:54
  855.1 19.1 %collective-permute-start.23 = (bf16[256,1536]{1,0:T(8,128)(2,1)S(1)}, bf16[256,1536]{1,0:T(8,128)(2,1)}, u32[]{:S(2)}, u32[]{:S(2)}) collective-permute-start(bf16[256,1536]{1,0:T(8,128)(2,1)S(1)} %slice_bitcast_fusion.8), channel_id=1, source_target_pairs={{0,1},{1,0},{2,3},{3,2},{4,5},{5,4},{6,7},{7,6},{8,9},{9,8},{10,11... | collective-permute-start | bytes 2359304 | tf_op jit(solution)/shard_map/ppermute | solution.py:54
  863.5 10.7 %copy-start.25 = (bf16[2,256,1536]{2,1,0:T(8,128)(2,1)S(1)}, bf16[2,256,1536]{2,1,0:T(8,128)(2,1)}, u32[]{:S(2)}) copy-start(bf16[2,256,1536]{2,1,0:T(8,128)(2,1)} %copy-done.24) | copy-start | bytes 4718596
  865.0 10.6 %copy-start.15 = (f32[512,1536]{1,0:T(8,128)S(1)}, f32[512,1536]{1,0:T(8,128)}, u32[]{:S(2)}) copy-start(f32[512,1536]{1,0:T(8,128)} %copy-done.13) | copy-start | bytes 9437188
  (32 other events, 95.5 us)
Sparse Core Ops, SparseCore 0:
  10.3 100.4 all-gather.5
  183.0 140.8 all-gather.3
  423.0 75.6 reduce-scatter.4
  508.3 134.5 reduce-scatter.2

commit v5 on v4

--- a/solution.py
+++ b/solution.py
@@ -411,10 +411,7 @@
     return sorted(set(a for a, _ in subsets(hops[:-1])))
 
 
-def reduce_kernel(outer, seq_count, count, u_ref, *refs):
-    refs = list(refs)
-    units_ref = refs.pop(2 * count)
-    own_sem = refs.pop()
+def reduce_kernel(outer, seq_count, count, *refs):
     given, results = refs[:count], refs[count : 2 * count]
     slow = len(plane_hops(seq_count)[0]) - 1
     held = refs[2 * count : 3 * count]
@@ -427,14 +424,8 @@
     hops = plane_hops(seq_count)
     nears = near_inner(seq_count)
     peers = [(flip_all(line, d) * INNER + inner, seq) for d in range(1, outer)]
-    peers += [
-        (wt - inner + flip_all(inner, a), flip_all(seq, b))
-        for b in range(seq_count)
-        for a in range(INNER)
-        if a or b
-    ]
-    keep = pltpu.make_async_copy(u_ref.at[inner], units_ref.at[0, 0], own_sem.at[0])
-    keep.start()
+    peers += [(wt - inner + flip(inner, bit), seq) for bit in inner_bits()]
+    peers += [(wt, flip_all(seq, d)) for d in range(1, seq_count)]
     meet(peers)
     out = Sender(send_sems, recv_sems)
 
@@ -525,25 +516,7 @@
         arrive(copies)
         results[k][...] = joined[k][...].astype(full)
 
-    def exchange():
-        copies = []
-        for b in range(seq_count):
-            copies += [
-                out.start(
-                    u_ref.at[flip_all(inner, a)],
-                    units_ref.at[b, a],
-                    (wt - inner + flip_all(inner, a), flip_all(seq, b)),
-                )
-                for a in range(INNER)
-                if a or b
-            ]
-            if b == 0:
-                for _ in range(slow + 1):
-                    yield
-        yield
-        arrive(copies)
-
-    running = [steps(k) for k in range(count)] + [exchange()]
+    running = [steps(k) for k in range(count)]
     for _ in range(2):
         next(running[0])
     while running:
@@ -552,10 +525,9 @@
                 running.remove(one)
     for copy in out.copies:
         copy.wait_send()
-    keep.wait()
-
-
-def reduce_shares(units, *partials):
+
+
+def reduce_shares(*partials):
     outer = lax.axis_size("wt") // INNER
     seq_count = lax.axis_size("seq")
     count = len(partials)
@@ -567,25 +539,23 @@
     ]
     shapes = [p.shape[2:] for p in partials]
     copies = count * (nears + 2 * (2**slow - 1) + outer - 1 + seq_count - 1)
-    copies += INNER * seq_count - 1
     sent = sum(2 * p.size for p in partials)
     return pl.pallas_call(
         functools.partial(reduce_kernel, outer, seq_count, count),
-        in_specs=[vmem] * (count + 1),
-        out_specs=[vmem] * (count + 1),
-        out_shape=[jax.ShapeDtypeStruct(shape, full) for shape in shapes]
-        + [jax.ShapeDtypeStruct((seq_count,) + units.shape, low)],
+        in_specs=[vmem] * count,
+        out_specs=[vmem] * count,
+        out_shape=[jax.ShapeDtypeStruct(shape, full) for shape in shapes],
         scratch_shapes=near
         + [pltpu.VMEM((outer, r, c // seq_count), low) for r, c in shapes]
         + [pltpu.VMEM(shape, low) for shape in shapes]
         + near * (1 + slow)
-        + [pltpu.SemaphoreType.DMA((n,)) for n in (copies, copies, 1)],
+        + [pltpu.SemaphoreType.DMA((n,)) for n in (copies, copies)],
         compiler_params=pltpu.CompilerParams(
             collective_id=2, has_side_effects=True, vmem_limit_bytes=60 << 20
         ),
         cost_estimate=pl.CostEstimate(flops=0, bytes_accessed=8 * sent, transcendentals=0),
         name="reduce_shares",
-    )(units, *partials)
+    )(*partials)
 
 
 def split_kernel(outer, seq_count, own, info_ref, gate_ref, up_ref, o_ref):
@@ -913,7 +883,8 @@
         part_a = gather_hops(block[: rows // 2], slow_a)
         part_b = gather_hops(block[rows // 2 :], slow_b)
         near = jnp.stack([part_a, part_b]).reshape(near_rows, width)
-        return jnp.concatenate([near, swap(near, core)], axis=0)
+        far = swap(near, core)
+        return jnp.concatenate([near, far], axis=0)
 
     def hop_core(partial):
         other = swap(partial[near_rows:], core)
@@ -964,6 +935,22 @@
     layer_out = jnp.where(keep, resid + forth, 0.0).astype(low)
     layer_out = layer_out.reshape(slot_count, rows, width)
 
+    blocks = units_line.reshape(INNER, share, 2 * ff_pad)
+
+    def plane_swap(distance, seq_distance):
+        block = to_place(blocks, inner_here ^ distance)
+        if not distance and not seq_distance:
+            return block
+        pairs = [
+            (w * seq_count + q, (w ^ distance) * seq_count + (q ^ seq_distance))
+            for w in range(wt_count)
+            for q in range(seq_count)
+        ]
+        return lax.ppermute(block, ("wt", "seq"), pairs)
+
+    units_got = [
+        jnp.stack([plane_swap(a, b) for a in range(INNER)]) for b in range(seq_count)
+    ]
     down_out = seq_gather(down_line)
     down_out = down_out.reshape(seq_count * ff_own, width).astype(full)
     pair_part = jnp.concatenate([key_part, value_part], axis=1)
@@ -1007,14 +994,13 @@
     def by_owner(partial):
         return partial.reshape(outer, INNER, -1, partial.shape[-1])
 
-    out_w_out, heads_out, small_out, units_got = reduce_shares(
-        units_line.reshape(INNER, share, 2 * ff_pad),
+    out_w_out, heads_out, small_out = reduce_shares(
         by_owner(out_w_grad),
         by_owner(head_w_grad),
         by_owner(small_grad),
     )
     small_out = small_out[0]
-    gate_out, up_out = join_units(info, units_got, outer, ff_own)
+    gate_out, up_out = join_units(info, jnp.stack(units_got), outer, ff_own)
     return (
         layer_out,
         input_grad,

time: 903 us -> 953 us (1.055); the launches traced: 885 us -> 945 us
  waiting for transfers between devices: 148 us -> 238 us
  Pallas kernels: 364 us -> 323 us
    ppermute x0 -> x7, waiting for transfers between devices: none -> 54.8 us  [plane_swap(): return lax.ppermute(block, ('wt', 'seq'), pairs)]
    pallas_call x1, Pallas kernels: 143 us -> 101 us  [reduce_shares(): pl.pallas_call(functools.partial(reduce_kernel, outer, seq_count, count),...]
    ppermute x23, waiting for transfers between devices: 134 us -> 169 us  [swap(): return lax.ppermute(value, axis, [(i, i ^ bit) for i in range(count)])]
  transfers between devices with their start and end apart: 30 -> 37, of which waited for: 10 -> 15; matrix products, arithmetic and copies ran while one was open for 28% -> 27% of each run, Pallas kernels for 37% -> 30%
where the time goes in v5:
time: 953 us; the launch traced here: 945 us
  Pallas kernels  323 us (34%)
  waiting for transfers between devices  238 us (25%)
  matrix products  182 us (19%)
  other arithmetic  94.3 us (10%)
  local copies, waits for them, and re-layouts  59.2 us (6%)
  starting transfers between devices  33.3 us (3%)
  between operations  15.8 us (2%)
    ppermute x23, waiting for transfers between devices, swap(): return lax.ppermute(value, axis, [(i, i ^ bit) for i in range(count)])  169 us
    pallas_call x1, Pallas kernels, reduce_shares(): pl.pallas_call(functools.partial(reduce_kernel, outer, seq_count, count),...  101 us
    dot_general x4, matrix products, product_left(): lax.dot_general(left, right, (((0,), (0,)), ((), ())), preferred_element_...  71.2 us
    pallas_call x1, Pallas kernels, gather_line(): pl.pallas_call(functools.partial(line_kernel, outer, seq_count), in_specs...  64.4 us
    dot_general x3, matrix products, product(): return jnp.dot(left, right, preferred_element_type=full)  63.4 us
    pallas_call x1, Pallas kernels, gather_project(): pl.pallas_call(functools.partial(gather_kernel, outer, seq_count), in_spe...  56.5 us
    ppermute x7, waiting for transfers between devices, plane_swap(): return lax.ppermute(block, ('wt', 'seq'), pairs)  54.8 us
    dot_general x3, matrix products, product_right(): lax.dot_general(left, right, (((1,), (1,)), ((), ())), preferred_element_...  47.5 us
  transfers between devices with their start and end apart: 37, of which 15 were waited for; matrix products, arithmetic and copies ran while one was open for 27% of the time, Pallas kernels for 30%

profile of v5, /device:TPU:0, one launch (start us, length us, event | category | flops | bytes accessed | tf_op | source)
XLA Modules:
  0.0 945.3 jit_solution(721857503225866086)
XLA Ops:
  20.2 64.4 %gather_line.1 = (bf16[4,96,1024]{2,1,0:T(8,128)(2,1)}, bf16[4,96,768]{2,1,0:T(8,128)(2,1)}, bf16[4,16,128]{2,1,0:T(8,128)(2,1)}) custom-call(bf16[96,2048]{1,0:T(8,128)(2,1)} %pad_maximum_fusion.16.p_ref, bf16[96,1536]{1,0:T(8,128)(2,1)} %convert_element_type.193.wo_ref, bf16[16,128]{1,0:T(8,128)(2,1)} %pad.43.s_ref), custom_call_target="tpu_custom_call" | custom-call | bytes 22020096 | tf_op jit(solution)/shard_map/gather_line/pallas_call | solution.py:194
  87.5 56.5 %gather_project.1 = (bf16[512,1536]{1,0:T(8,128)(2,1)S(1)}, bf16[512,2048]{1,0:T(8,128)(2,1)}, f32[8,2048]{1,0:T(8,128)S(1)}, bf16[4,4,96,2048]{3,2,1,0:T(8,128)(2,1)}, bf16[4,4,96,1536]{3,2,1,0:T(8,128)(2,1)}) custom-call(bf16[512,1536]{1,0:T(8,128)(2,1)S(1)} %bitcast.162, bf16[4,96,1024]{2,1,0:T(8,128)(2,1)S(1)} %copy-done.8, ...), custom_call_target="tpu_custom_call" | custom-call | flops 25769803776 | bytes 22020096 | tf_op jit(solution)/shard_map/gather_project/pallas_call | solution.py:380
  148.8 5.0 split_units.1
  153.8 2.8 fusion.32
  165.6 6.5 collective-permute-done.7
  172.1 7.5 collective-permute-done.8
  185.3 22.7 %attend_forward.1 = bf16[512,1536]{1,0:T(8,128)(2,1)} custom-call(s32[1,1024]{1,0:T(1,128)} %compare_select_fusion.kpos_ref, bf16[512,2048]{1,0:T(8,128)(2,1)} %get-tuple-element.43.q_ref, bf16[1024,512]{1,0:T(8,128)(2,1)} %bitcast.179, bf16[1024,512]{1,0:T(8,128)(2,1)} %bitcast.180), custom_call_target="tpu_custom_call" | custom-call | flops 9663676416 | bytes 4194304 | tf_op jit(solution)/shard_map/attend_forward/pallas_call | solution.py:690
  208.0 5.1 multiply_reduce_fusion.2
  221.7 16.4 %collective-permute-done.1 = bf16[1,256,1536]{2,1,0:T(8,128)(2,1)S(1)} collective-permute-done((bf16[1,256,1536]{2,1,0:T(8,128)(2,1)S(1)}, bf16[1,256,1536]{2,1,0:T(8,128)(2,1)S(1)}, u32[]{:S(2)}, u32[]{:S(2)}) %collective-permute-start.1) | collective-permute-done | bytes 786464 | tf_op jit(solution)/shard_map/ppermute | solution.py:54
  238.3 30.8 %collective-permute-done.3 = bf16[1,256,1536]{2,1,0:T(8,128)(2,1)S(1)} collective-permute-done((bf16[1,256,1536]{2,1,0:T(8,128)(2,1)S(1)}, bf16[1,256,1536]{2,1,0:T(8,128)(2,1)S(1)}, u32[]{:S(2)}, u32[]{:S(2)}) %collective-permute-start.3) | collective-permute-done | bytes 786464 | tf_op jit(solution)/shard_map/ppermute | solution.py:54
  275.1 3.2 pad_maximum_fusion.3
  278.3 24.5 %collective-permute-done.2 = bf16[2,256,1536]{2,1,0:T(8,128)(2,1)S(1)} collective-permute-done((bf16[2,256,1536]{2,1,0:T(8,128)(2,1)S(1)}, bf16[2,256,1536]{2,1,0:T(8,128)(2,1)S(1)}, u32[]{:S(2)}, u32[]{:S(2)}) %collective-permute-start.2) | collective-permute-done | bytes 1572896 | tf_op jit(solution)/shard_map/ppermute | solution.py:54
  303.1 3.1 collective-permute-done.4
  306.5 3.3 pad_maximum_fusion.2
  310.8 4.0 pad.44.down_ref
  314.8 10.4 %pad_maximum_fusion.1.grad_ref = bf16[4096,1536]{1,0:T(8,128)(2,1)} fusion(bf16[2048,1536]{1,0:T(8,128)(2,1)} %collective-permute-done.13, bf16[2048,1536]{1,0:T(8,128)(2,1)} %bitcast.30), kind=kLoop, calls=%fused_computation.3 | loop fusion | flops 25165824 | bytes 25165824 | tf_op jit(solution)/shard_map/concatenate | solution.py:887
  325.2 39.3 %fusion.29.both_ref = f32[4096,2304]{1,0:T(8,128)} fusion(bf16[1536,2304]{1,0:T(8,128)(2,1)} %bitcast.191, bf16[2048,1536]{1,0:T(8,128)(2,1)} %collective-permute-done.5, bf16[2048,1536]{1,0:T(8,128)(2,1)} %bitcast.14), kind=kOutput, calls=%fused_computation.148 | convolution fusion | flops 29016195072 | bytes 57409536 | tf_op jit(solution)/shard_map/dot_general | solution.py:27
  364.6 35.8 %hidden_units.1 = (bf16[4096,1152]{1,0:T(8,128)(2,1)}, bf16[4096,2304]{1,0:T(8,128)(2,1)}) custom-call(f32[4096,2304]{1,0:T(8,128)} %fusion.29.both_ref, bf16[4096,1536]{1,0:T(8,128)(2,1)} %pad_maximum_fusion.1.grad_ref, bf16[1152,1536]{1,0:T(8,128)(2,1)} %pad.44.down_ref), custom_call_target="tpu_custom_call" | custom-call | flops 14495514624 | bytes 82182144 | tf_op jit(solution)/shard_map/hidden_units/pallas_call | solution.py:635
  400.4 20.3 %convolution_convert_fusion.5 = bf16[1152,1536]{1,0:T(8,128)(2,1)S(1)} fusion(bf16[4096,1152]{1,0:T(8,128)(2,1)} %get-tuple-element.52, bf16[2048,1536]{1,0:T(8,128)(2,1)} %collective-permute-done.13, bf16[2048,1536]{1,0:T(8,128)(2,1)} %bitcast.30), kind=kOutput, calls=%fused_computation.9 | convolution fusion | flops 14522449920 | bytes 25559040 | tf_op jit(solution)/shard_map/dot_general | solution.py:31
  422.8 34.9 %convolution_convert_fusion.1 = bf16[4096,1536]{1,0:T(8,128)(2,1)S(1)} fusion(bf16[4096,2304]{1,0:T(8,128)(2,1)} %get-tuple-element.51, bf16[1536,2304]{1,0:T(8,128)(2,1)} %bitcast.192), kind=kOutput, calls=%fused_computation.1 | convolution fusion | flops 28997320704 | bytes 38535168 | tf_op jit(solution)/shard_map/dot_general | solution.py:35
  457.7 3.0 slice.295
  460.7 3.7 copy-done.17
  465.5 6.2 pad_maximum_fusion
  471.7 36.5 %convolution_convert_fusion.2 = bf16[1536,2304]{1,0:T(8,128)(2,1)} fusion(bf16[4096,1536]{1,0:T(8,128)(2,1)S(1)} %pad_maximum_fusion, bf16[4096,2304]{1,0:T(8,128)(2,1)} %get-tuple-element.51), kind=kOutput, calls=%fused_computation.6 | convolution fusion | flops 28994568192 | bytes 38535168 | tf_op jit(solution)/shard_map/dot_general | solution.py:31
  508.2 9.0 add_convert_fusion.1
  518.8 3.2 fusion.31
  524.1 15.3 %collective-permute-done.32 = bf16[1,280,1536]{2,1,0:T(8,128)(2,1)S(1)} collective-permute-done((bf16[1,280,1536]{2,1,0:T(8,128)(2,1)}, bf16[1,280,1536]{2,1,0:T(8,128)(2,1)S(1)}, u32[]{:S(2)}, u32[]{:S(2)}) %collective-permute-start.32) | collective-permute-done | bytes 860192 | tf_op jit(solution)/shard_map/ppermute | solution.py:54
  542.1 30.4 %collective-permute-done.15 = bf16[2,256,1536]{2,1,0:T(8,128)(2,1)S(1)} collective-permute-done((bf16[2,256,1536]{2,1,0:T(8,128)(2,1)S(1)}, bf16[2,256,1536]{2,1,0:T(8,128)(2,1)S(1)}, u32[]{:S(2)}, u32[]{:S(2)}) %collective-permute-start.15) | collective-permute-done | bytes 1572896 | tf_op jit(solution)/shard_map/ppermute | solution.py:54
  576.6 19.0 %convolution_convert_fusion = bf16[4096,1536]{1,0:T(8,128)(2,1)S(1)} fusion(bf16[4096,1152]{1,0:T(8,128)(2,1)} %get-tuple-element.52, bf16[1120,1536]{1,0:T(8,128)(2,1)S(1)} %copy-done.27), kind=kOutput, calls=%fused_computation | convolution fusion | flops 14501806080 | bytes 25460736 | tf_op jit(solution)/shard_map/dot_general | solution.py:27
  595.6 3.3 slice.250
  598.9 3.2 copy-done.16
  609.7 3.7 convolution_convert_fusion.6.g_ref
  613.4 31.2 %attend_backward.1 = (bf16[512,1536]{1,0:T(8,128)(2,1)}, f32[1024,256]{1,0:T(8,128)}, f32[1024,256]{1,0:T(8,128)}) custom-call(s32[1,1024]{1,0:T(1,128)} %compare_select_fusion.kpos_ref, f32[512,128]{1,0:T(8,128)} %copy-done.4, f32[512,128]{1,0:T(8,128)} %copy-done.6, bf16[512,2048]{1,0:T(8,128)(2,1)} %get-tuple-element.43.q_ref, ...), custom_call_target="tpu_custom_call" | custom-call | flops 24159191040 | bytes 9437184 | tf_op jit(solution)/shard_map/attend_backward/pallas_call | solution.py:758
  648.4 7.3 convolution_convert_fusion.4
  655.8 5.9 collective-permute-done.24
  670.4 8.8 fusion.7
  680.2 7.1 convolution_convert_fusion.3
  687.3 100.8 %reduce_shares.1 = (f32[96,1536]{1,0:T(8,128)}, f32[96,2048]{1,0:T(8,128)}, f32[16,512]{1,0:T(8,128)}) custom-call(bf16[4,4,96,1536]{3,2,1,0:T(8,128)(2,1)} %bitcast.171, bf16[4,4,96,2048]{3,2,1,0:T(8,128)(2,1)} %bitcast.170, bf16[4,4,16,512]{3,2,1,0:T(8,128)(2,1)} %bitcast.178), custom_call_target="tpu_custom_call" | custom-call | bytes 90177536 | tf_op jit(solution)/shard_map/reduce_shares/pallas_call | solution.py:543
  788.1 4.8 fusion.15
  792.9 8.9 add_convert_fusion
  801.8 5.1 fusion.30
  815.1 38.8 %collective-permute-done.26 = bf16[96,2304]{1,0:T(8,128)(2,1)S(1)} collective-permute-done((bf16[96,2304]{1,0:T(8,128)(2,1)S(1)}, bf16[96,2304]{1,0:T(8,128)(2,1)S(1)}, u32[]{:S(2)}, u32[]{:S(2)}) %collective-permute-start.26) | collective-permute-done | bytes 442400 | tf_op jit(solution)/shard_map/ppermute | solution.py:949
  855.4 6.5 collective-permute-done.27
  867.6 5.7 collective-permute-done.30
  873.3 3.8 collective-permute-done.31
  879.2 33.5 %collective-permute-done.20 = bf16[2,256,1536]{2,1,0:T(8,128)(2,1)S(1)} collective-permute-done((bf16[2,256,1536]{2,1,0:T(8,128)(2,1)}, bf16[2,256,1536]{2,1,0:T(8,128)(2,1)S(1)}, u32[]{:S(2)}, u32[]{:S(2)}) %collective-permute-start.20) | collective-permute-done | bytes 1572896 | tf_op jit(solution)/shard_map/ppermute | solution.py:54
  917.7 6.2 join_units.1
  923.9 9.0 collective-permute-done.22
  (250 shorter events, 112.8 us)
Async XLA Ops:
  7.2 303.6 %all-gather.6.cloned.1.call-start = ((), (), s32[]{:S(2)}) async-start(), calls=%async_computation.5 | async-start | bytes 4300800 | tf_op jit(solution)/shard_map/all_gather | solution.py:817
  10.2 74.4 %copy-start.2 = (bf16[1,512,1536]{2,1,0:T(8,128)(2,1)S(1)}, bf16[1,512,1536]{2,1,0:T(8,128)(2,1)}, u32[]{:S(2)}) copy-start(bf16[1,512,1536]{2,1,0:T(8,128)(2,1)} %param.15) | copy-start | bytes 4718596
  10.2 315.1 %all-gather.4.cloned.1.call-start = ((), (), s32[]{:S(2)}) async-start(), calls=%async_computation.2 | async-start | bytes 8847360 | tf_op jit(solution)/shard_map/all_gather | solution.py:817
  19.4 124.7 %copy-start.4 = (f32[512,128]{1,0:T(8,128)}, f32[512,128]{1,0:T(8,128)S(1)}, u32[]{:S(2)}) copy-start(f32[512,128]{1,0:T(8,128)S(1)} %get-tuple-element.123.cos_ref) | copy-start | bytes 786436
  19.4 124.7 %copy-start.6 = (f32[512,128]{1,0:T(8,128)}, f32[512,128]{1,0:T(8,128)S(1)}, u32[]{:S(2)}) copy-start(f32[512,128]{1,0:T(8,128)S(1)} %get-tuple-element.124.sin_ref) | copy-start | bytes 786436
  147.1 36.0 %collective-permute-start = (bf16[1,512,512]{2,1,0:T(8,128)(2,1)}, bf16[1,512,512]{2,1,0:T(8,128)(2,1)}, u32[]{:S(2)}, u32[]{:S(2)}) collective-permute-start(bf16[1,512,512]{2,1,0:T(8,128)(2,1)} %slice_bitcast_fusion.10), channel_id=1, source_target_pairs={{0,1},{1,0},{2,3},{3,2},{4,5},{5,4},{6,7},{7,6},{8,9},{9,8},{10,11... | collective-permute-start | bytes 1572872 | tf_op jit(solution)/shard_map/ppermute | solution.py:54
  156.5 7.6 collective-permute-start.6
  158.7 13.4 %collective-permute-start.7 = (bf16[96,2304]{1,0:T(8,128)(2,1)}, bf16[96,2304]{1,0:T(8,128)(2,1)}, u32[]{:S(2)}, u32[]{:S(2)}) collective-permute-start(bf16[96,2304]{1,0:T(8,128)(2,1)} %get-tuple-element.90), channel_id=1, source_target_pairs={{0,4},{2,6},{4,0},{6,2},{8,12},{10,14},{12,8},{14,10},{16,20},{18,... | collective-permute-start | bytes 1327112 | tf_op jit(solution)/shard_map/ppermute | solution.py:833
  159.2 20.4 %collective-permute-start.8 = (bf16[96,2304]{1,0:T(8,128)(2,1)}, bf16[96,2304]{1,0:T(8,128)(2,1)}, u32[]{:S(2)}, u32[]{:S(2)}) collective-permute-start(bf16[96,2304]{1,0:T(8,128)(2,1)} %get-tuple-element.89), channel_id=1, source_target_pairs={{0,6},{2,4},{4,2},{6,0},{8,14},{10,12},{12,10},{14,8},{16,22},{18,... | collective-permute-start | bytes 1327112 | tf_op jit(solution)/shard_map/ppermute | solution.py:833
  162.2 51.9 %collective-permute-start.9 = (bf16[1,256,1536]{2,1,0:T(8,128)(2,1)}, bf16[1,256,1536]{2,1,0:T(8,128)(2,1)}, u32[]{:S(2)}, u32[]{:S(2)}) collective-permute-start(bf16[1,256,1536]{2,1,0:T(8,128)(2,1)} %get-tuple-element.94), channel_id=1, source_target_pairs={{0,4},{2,6},{4,0},{6,2},{8,12},{10,14},{12,8},{14,10},{16,20},{18,... | collective-permute-start | bytes 2359304 | tf_op jit(solution)/shard_map/ppermute | solution.py:54
  164.1 49.7 %copy-start.33 = (f32[1536]{0:T(1024)}, f32[1536]{0:T(1024)S(1)}, u32[]{:S(2)}) copy-start(f32[1536]{0:T(1024)S(1)} %get-tuple-element.71) | copy-start | bytes 18436
  164.1 54.3 %collective-permute-start.11 = (bf16[1,256,1536]{2,1,0:T(8,128)(2,1)}, bf16[1,256,1536]{2,1,0:T(8,128)(2,1)}, u32[]{:S(2)}, u32[]{:S(2)}) collective-permute-start(bf16[1,256,1536]{2,1,0:T(8,128)(2,1)} %get-tuple-element.95), channel_id=1, source_target_pairs={{0,1},{1,0},{2,3},{3,2},{4,5},{5,4},{6,7},{7,6},{8,9},{9,8},{10,11... | collective-permute-start | bytes 2359304 | tf_op jit(solution)/shard_map/ppermute | solution.py:54
  182.8 334.4 %reduce-scatter.5.cloned.1.call-start = ((), (), s32[]{:S(2)}) async-start(), calls=%async_computation.4 | async-start | bytes 4300800 | tf_op jit(solution)/shard_map/reduce_scatter | solution.py:820
  215.8 55.9 %collective-permute-start.10 = (bf16[2,256,1536]{2,1,0:T(8,128)(2,1)S(1)}, bf16[2,256,1536]{2,1,0:T(8,128)(2,1)S(1)}, u32[]{:S(2)}, u32[]{:S(2)}) collective-permute-start(bf16[2,256,1536]{2,1,0:T(8,128)(2,1)S(1)} %pad_maximum_fusion.12), channel_id=1, source_target_pairs={{0,1},{1,0},{2,3},{3,2},{4,5},{5,4},{6,7},{7,6},{8,9},{9,8},{10,11... | collective-permute-start | bytes 4718600 | tf_op jit(solution)/shard_map/ppermute | solution.py:54
  217.6 20.5 %collective-permute-start.1 = (bf16[1,256,1536]{2,1,0:T(8,128)(2,1)S(1)}, bf16[1,256,1536]{2,1,0:T(8,128)(2,1)S(1)}, u32[]{:S(2)}, u32[]{:S(2)}) collective-permute-start(bf16[1,256,1536]{2,1,0:T(8,128)(2,1)S(1)} %get-tuple-element.96), channel_id=1, source_target_pairs={{0,4},{2,6},{4,0},{6,2},{8,12},{10,14},{12,8},{14,10},{16,20},{18,... | collective-permute-start | bytes 2359304 | tf_op jit(solution)/shard_map/ppermute | solution.py:54
  219.9 53.5 %collective-permute-start.12 = (bf16[2,256,1536]{2,1,0:T(8,128)(2,1)S(1)}, bf16[2,256,1536]{2,1,0:T(8,128)(2,1)S(1)}, u32[]{:S(2)}, u32[]{:S(2)}) collective-permute-start(bf16[2,256,1536]{2,1,0:T(8,128)(2,1)S(1)} %pad_maximum_fusion.13), channel_id=1, source_target_pairs={{0,4},{2,6},{4,0},{6,2},{8,12},{10,14},{12,8},{14,10},{16,20},{18,... | collective-permute-start | bytes 4718600 | tf_op jit(solution)/shard_map/ppermute | solution.py:54
  221.3 47.9 %collective-permute-start.3 = (bf16[1,256,1536]{2,1,0:T(8,128)(2,1)S(1)}, bf16[1,256,1536]{2,1,0:T(8,128)(2,1)S(1)}, u32[]{:S(2)}, u32[]{:S(2)}) collective-permute-start(bf16[1,256,1536]{2,1,0:T(8,128)(2,1)S(1)} %get-tuple-element.97), channel_id=1, source_target_pairs={{0,1},{1,0},{2,3},{3,2},{4,5},{5,4},{6,7},{7,6},{8,9},{9,8},{10,11... | collective-permute-start | bytes 2359304 | tf_op jit(solution)/shard_map/ppermute | solution.py:54
  238.2 64.6 %collective-permute-start.2 = (bf16[2,256,1536]{2,1,0:T(8,128)(2,1)S(1)}, bf16[2,256,1536]{2,1,0:T(8,128)(2,1)S(1)}, u32[]{:S(2)}, u32[]{:S(2)}) collective-permute-start(bf16[2,256,1536]{2,1,0:T(8,128)(2,1)S(1)} %pad_maximum_fusion.10), channel_id=1, source_target_pairs={{0,1},{1,0},{2,3},{3,2},{4,5},{5,4},{6,7},{7,6},{8,9},{9,8},{10,11... | collective-permute-start | bytes 4718600 | tf_op jit(solution)/shard_map/ppermute | solution.py:54
  269.3 36.9 %collective-permute-start.4 = (bf16[2,256,1536]{2,1,0:T(8,128)(2,1)S(1)}, bf16[2,256,1536]{2,1,0:T(8,128)(2,1)S(1)}, u32[]{:S(2)}, u32[]{:S(2)}) collective-permute-start(bf16[2,256,1536]{2,1,0:T(8,128)(2,1)S(1)} %pad_maximum_fusion.11), channel_id=1, source_target_pairs={{0,4},{2,6},{4,0},{6,2},{8,12},{10,14},{12,8},{14,10},{16,20},{18,... | collective-permute-start | bytes 4718600 | tf_op jit(solution)/shard_map/ppermute | solution.py:54
  278.3 36.5 %collective-permute-start.13 = (bf16[2048,1536]{1,0:T(8,128)(2,1)}, bf16[2048,1536]{1,0:T(8,128)(2,1)}, u32[]{:S(2)}, u32[]{:S(2)}) collective-permute-start(bf16[2048,1536]{1,0:T(8,128)(2,1)} %bitcast.30), channel_id=1, source_target_pairs={{0,2},{2,0},{4,6},{6,4},{8,10},{10,8},{12,14},{14,12},{16,18},{18,... | collective-permute-start | bytes 18874376 | tf_op jit(solution)/shard_map/ppermute | solution.py:54
  309.8 15.4 %collective-permute-start.5 = (bf16[2048,1536]{1,0:T(8,128)(2,1)}, bf16[2048,1536]{1,0:T(8,128)(2,1)}, u32[]{:S(2)}, u32[]{:S(2)}) collective-permute-start(bf16[2048,1536]{1,0:T(8,128)(2,1)} %bitcast.14), channel_id=1, source_target_pairs={{0,2},{2,0},{4,6},{6,4},{8,10},{10,8},{12,14},{14,12},{16,18},{18,... | collective-permute-start | bytes 18874376 | tf_op jit(solution)/shard_map/ppermute | solution.py:54
  422.7 385.2 %reduce-scatter.3.cloned.1.call-start = ((), (), s32[]{:S(2)}) async-start(), calls=%async_computation.3 | async-start | bytes 8847360 | tf_op jit(solution)/shard_map/reduce_scatter | solution.py:820
  464.4 43.8 %collective-permute-start.14 = (bf16[2048,1536]{1,0:T(8,128)(2,1)}, bf16[2048,1536]{1,0:T(8,128)(2,1)}, u32[]{:S(2)}, u32[]{:S(2)}) collective-permute-start(bf16[2048,1536]{1,0:T(8,128)(2,1)} %slice.295), channel_id=1, source_target_pairs={{0,2},{2,0},{4,6},{6,4},{8,10},{10,8},{12,14},{14,12},{16,18},{18,... | collective-permute-start | bytes 18874376 | tf_op jit(solution)/shard_map/ppermute | solution.py:54
  517.2 22.2 %collective-permute-start.32 = (bf16[1,280,1536]{2,1,0:T(8,128)(2,1)}, bf16[1,280,1536]{2,1,0:T(8,128)(2,1)S(1)}, u32[]{:S(2)}, u32[]{:S(2)}) collective-permute-start(bf16[1,280,1536]{2,1,0:T(8,128)(2,1)} %reduce-scatter.5.cloned.1.call-done), channel_id=1, source_target_pairs={{0,1},{1,0},{2,3},{3,2},{4,5},{5,4},{6,7},{7,6},{8,9},{9,8},{10,11... | collective-permute-start | bytes 2580488 | tf_op jit(solution)/shard_map/ppermute | solution.py:54
  522.0 50.5 %collective-permute-start.15 = (bf16[2,256,1536]{2,1,0:T(8,128)(2,1)S(1)}, bf16[2,256,1536]{2,1,0:T(8,128)(2,1)S(1)}, u32[]{:S(2)}, u32[]{:S(2)}) collective-permute-start(bf16[2,256,1536]{2,1,0:T(8,128)(2,1)S(1)} %bitcast.177), channel_id=1, source_target_pairs={{0,1},{1,0},{2,3},{3,2},{4,5},{5,4},{6,7},{7,6},{8,9},{9,8},{10,11... | collective-permute-start | bytes 4718600 | tf_op jit(solution)/shard_map/ppermute | solution.py:54
  522.5 50.5 %collective-permute-start.16 = (bf16[2,256,1536]{2,1,0:T(8,128)(2,1)S(1)}, bf16[2,256,1536]{2,1,0:T(8,128)(2,1)S(1)}, u32[]{:S(2)}, u32[]{:S(2)}) collective-permute-start(bf16[2,256,1536]{2,1,0:T(8,128)(2,1)S(1)} %bitcast.176), channel_id=1, source_target_pairs={{0,4},{2,6},{4,0},{6,2},{8,12},{10,14},{12,8},{14,10},{16,20},{18,... | collective-permute-start | bytes 4718600 | tf_op jit(solution)/shard_map/ppermute | solution.py:54
  574.4 27.7 %collective-permute-start.17 = (bf16[256,1536]{1,0:T(8,128)(2,1)S(1)}, bf16[256,1536]{1,0:T(8,128)(2,1)}, u32[]{:S(2)}, u32[]{:S(2)}) collective-permute-start(bf16[256,1536]{1,0:T(8,128)(2,1)S(1)} %slice_bitcast_fusion.2), channel_id=1, source_target_pairs={{0,4},{2,6},{4,0},{6,2},{8,12},{10,14},{12,8},{14,10},{16,20},{18,... | collective-permute-start | bytes 2359304 | tf_op jit(solution)/shard_map/ppermute | solution.py:54
  575.5 28.2 %collective-permute-start.18 = (bf16[256,1536]{1,0:T(8,128)(2,1)}, bf16[256,1536]{1,0:T(8,128)(2,1)}, u32[]{:S(2)}, u32[]{:S(2)}) collective-permute-start(bf16[256,1536]{1,0:T(8,128)(2,1)} %slice_bitcast_fusion), channel_id=1, source_target_pairs={{0,1},{1,0},{2,3},{3,2},{4,5},{5,4},{6,7},{7,6},{8,9},{9,8},{10,11... | collective-permute-start | bytes 2359304 | tf_op jit(solution)/shard_map/ppermute | solution.py:54
  602.1 190.8 %collective-permute-start.19 = (bf16[2048,1536]{1,0:T(8,128)(2,1)}, bf16[2048,1536]{1,0:T(8,128)(2,1)}, u32[]{:S(2)}, u32[]{:S(2)}) collective-permute-start(bf16[2048,1536]{1,0:T(8,128)(2,1)} %slice.250), channel_id=1, source_target_pairs={{0,2},{2,0},{4,6},{6,4},{8,10},{10,8},{12,14},{14,12},{16,18},{18,... | collective-permute-start | bytes 18874376 | tf_op jit(solution)/shard_map/ppermute | solution.py:54
  647.4 14.2 %collective-permute-start.24 = (bf16[512,512]{1,0:T(8,128)(2,1)S(1)}, bf16[512,512]{1,0:T(8,128)(2,1)}, u32[]{:S(2)}, u32[]{:S(2)}) collective-permute-start(bf16[512,512]{1,0:T(8,128)(2,1)S(1)} %pad_maximum_fusion.15), channel_id=1, source_target_pairs={{0,1},{1,0},{2,3},{3,2},{4,5},{5,4},{6,7},{7,6},{8,9},{9,8},{10,11... | collective-permute-start | bytes 1572872 | tf_op jit(solution)/shard_map/ppermute | solution.py:54
  655.8 12.9 %copy-start.7 = (f32[512,128]{1,0:T(8,128)S(1)}, f32[512,128]{1,0:T(8,128)}, u32[]{:S(2)}) copy-start(f32[512,128]{1,0:T(8,128)} %copy-done.6) | copy-start | bytes 786436
  670.4 9.8 %copy-start.12 = (bf16[512,1536]{1,0:T(8,128)(2,1)S(1)}, bf16[512,1536]{1,0:T(8,128)(2,1)}, u32[]{:S(2)}) copy-start(bf16[512,1536]{1,0:T(8,128)(2,1)} %copy-done.11) | copy-start | bytes 4718596
  687.3 100.8 %copy-start.40 = (f32[512]{0:T(512)S(1)}, f32[512]{0:T(512)}, u32[]{:S(2)}) copy-start(f32[512]{0:T(512)} %get-tuple-element.112) | copy-start | bytes 6148
  807.0 70.4 %collective-permute-start.21 = (bf16[2,256,1536]{2,1,0:T(8,128)(2,1)}, bf16[2,256,1536]{2,1,0:T(8,128)(2,1)}, u32[]{:S(2)}, u32[]{:S(2)}) collective-permute-start(bf16[2,256,1536]{2,1,0:T(8,128)(2,1)} %bitcast.42), channel_id=1, source_target_pairs={{0,4},{2,6},{4,0},{6,2},{8,12},{10,14},{12,8},{14,10},{16,20},{18,... | collective-permute-start | bytes 4718600 | tf_op jit(solution)/shard_map/ppermute | solution.py:54
  809.4 5.1 collective-permute-start.25
  809.5 44.4 %collective-permute-start.26 = (bf16[96,2304]{1,0:T(8,128)(2,1)S(1)}, bf16[96,2304]{1,0:T(8,128)(2,1)S(1)}, u32[]{:S(2)}, u32[]{:S(2)}) collective-permute-start(bf16[96,2304]{1,0:T(8,128)(2,1)S(1)} %get-tuple-element.82), channel_id=1, source_target_pairs={{0,4},{1,5},{2,6},{3,7},{4,0},{5,1},{6,2},{7,3},{8,12},{9,13},{10,... | collective-permute-start | bytes 1327112 | tf_op jit(solution)/shard_map/ppermute | solution.py:949
  810.7 51.2 %collective-permute-start.27 = (bf16[96,2304]{1,0:T(8,128)(2,1)S(1)}, bf16[96,2304]{1,0:T(8,128)(2,1)S(1)}, u32[]{:S(2)}, u32[]{:S(2)}) collective-permute-start(bf16[96,2304]{1,0:T(8,128)(2,1)S(1)} %get-tuple-element.81), channel_id=1, source_target_pairs={{0,6},{1,7},{2,4},{3,5},{4,2},{5,3},{6,0},{7,1},{8,14},{9,15},{10,... | collective-permute-start | bytes 1327112 | tf_op jit(solution)/shard_map/ppermute | solution.py:949
  811.3 52.9 %collective-permute-start.28 = (bf16[96,2304]{1,0:T(8,128)(2,1)S(1)}, bf16[96,2304]{1,0:T(8,128)(2,1)S(1)}, u32[]{:S(2)}, u32[]{:S(2)}) collective-permute-start(bf16[96,2304]{1,0:T(8,128)(2,1)S(1)} %bitcast.175), channel_id=1, source_target_pairs={{0,1},{1,0},{2,3},{3,2},{4,5},{5,4},{6,7},{7,6},{8,9},{9,8},{10,11... | collective-permute-start | bytes 1327112 | tf_op jit(solution)/shard_map/ppermute | solution.py:949
  814.5 53.1 %collective-permute-start.29 = (bf16[96,2304]{1,0:T(8,128)(2,1)S(1)}, bf16[96,2304]{1,0:T(8,128)(2,1)S(1)}, u32[]{:S(2)}, u32[]{:S(2)}) collective-permute-start(bf16[96,2304]{1,0:T(8,128)(2,1)S(1)} %get-tuple-element.83), channel_id=1, source_target_pairs={{0,3},{1,2},{2,1},{3,0},{4,7},{5,6},{6,5},{7,4},{8,11},{9,10},{10,... | collective-permute-start | bytes 1327112 | tf_op jit(solution)/shard_map/ppermute | solution.py:949
  853.9 19.4 %collective-permute-start.30 = (bf16[96,2304]{1,0:T(8,128)(2,1)S(1)}, bf16[96,2304]{1,0:T(8,128)(2,1)S(1)}, u32[]{:S(2)}, u32[]{:S(2)}) collective-permute-start(bf16[96,2304]{1,0:T(8,128)(2,1)S(1)} %get-tuple-element.82), channel_id=1, source_target_pairs={{0,5},{1,4},{2,7},{3,6},{4,1},{5,0},{6,3},{7,2},{8,13},{9,12},{10,... | collective-permute-start | bytes 1327112 | tf_op jit(solution)/shard_map/ppermute | solution.py:949
  861.8 15.3 %collective-permute-start.31 = (bf16[96,2304]{1,0:T(8,128)(2,1)S(1)}, bf16[96,2304]{1,0:T(8,128)(2,1)S(1)}, u32[]{:S(2)}, u32[]{:S(2)}) collective-permute-start(bf16[96,2304]{1,0:T(8,128)(2,1)S(1)} %get-tuple-element.81), channel_id=1, source_target_pairs={{0,7},{1,6},{2,5},{3,4},{4,3},{5,2},{6,1},{7,0},{8,15},{9,14},{10,... | collective-permute-start | bytes 1327112 | tf_op jit(solution)/shard_map/ppermute | solution.py:949
  864.3 48.5 %collective-permute-start.20 = (bf16[2,256,1536]{2,1,0:T(8,128)(2,1)}, bf16[2,256,1536]{2,1,0:T(8,128)(2,1)S(1)}, u32[]{:S(2)}, u32[]{:S(2)}) collective-permute-start(bf16[2,256,1536]{2,1,0:T(8,128)(2,1)} %bitcast.40), channel_id=1, source_target_pairs={{0,1},{1,0},{2,3},{3,2},{4,5},{5,4},{6,7},{7,6},{8,9},{9,8},{10,11... | collective-permute-start | bytes 4718600 | tf_op jit(solution)/shard_map/ppermute | solution.py:54
  867.4 10.0 %copy-start.21 = (bf16[512,1536]{1,0:T(8,128)(2,1)S(1)}, bf16[512,1536]{1,0:T(8,128)(2,1)}, u32[]{:S(2)}) copy-start(bf16[512,1536]{1,0:T(8,128)(2,1)} %get-tuple-element.73) | copy-start | bytes 4718596
  879.2 35.3 %copy-start.22 = (bf16[2,256,1536]{2,1,0:T(8,128)(2,1)}, bf16[2,256,1536]{2,1,0:T(8,128)(2,1)S(1)}, u32[]{:S(2)}) copy-start(bf16[2,256,1536]{2,1,0:T(8,128)(2,1)S(1)} %fusion.10) | copy-start | bytes 4718596
  913.2 19.6 %collective-permute-start.22 = (bf16[256,1536]{1,0:T(8,128)(2,1)S(1)}, bf16[256,1536]{1,0:T(8,128)(2,1)}, u32[]{:S(2)}, u32[]{:S(2)}) collective-permute-start(bf16[256,1536]{1,0:T(8,128)(2,1)S(1)} %slice_bitcast_fusion.9), channel_id=1, source_target_pairs={{0,4},{2,6},{4,0},{6,2},{8,12},{10,14},{12,8},{14,10},{16,20},{18,... | collective-permute-start | bytes 2359304 | tf_op jit(solution)/shard_map/ppermute | solution.py:54
  914.6 19.6 %collective-permute-start.23 = (bf16[256,1536]{1,0:T(8,128)(2,1)S(1)}, bf16[256,1536]{1,0:T(8,128)(2,1)}, u32[]{:S(2)}, u32[]{:S(2)}) collective-permute-start(bf16[256,1536]{1,0:T(8,128)(2,1)S(1)} %slice_bitcast_fusion.8), channel_id=1, source_target_pairs={{0,1},{1,0},{2,3},{3,2},{4,5},{5,4},{6,7},{7,6},{8,9},{9,8},{10,11... | collective-permute-start | bytes 2359304 | tf_op jit(solution)/shard_map/ppermute | solution.py:54
  917.7 15.2 %copy-start.24 = (bf16[2,256,1536]{2,1,0:T(8,128)(2,1)S(1)}, bf16[2,256,1536]{2,1,0:T(8,128)(2,1)}, u32[]{:S(2)}) copy-start(bf16[2,256,1536]{2,1,0:T(8,128)(2,1)} %copy-done.23) | copy-start | bytes 4718596
  923.8 12.1 %copy-start.15 = (f32[512,1536]{1,0:T(8,128)S(1)}, f32[512,1536]{1,0:T(8,128)}, u32[]{:S(2)}) copy-start(f32[512,1536]{1,0:T(8,128)} %copy-done.13) | copy-start | bytes 9437188
  (34 other events, 118.3 us)
Sparse Core Ops, SparseCore 0:
  10.3 100.4 all-gather.5
  183.0 140.7 all-gather.3
  422.8 75.7 reduce-scatter.4
  508.3 134.5 reduce-scatter.2

commit v6 on v5

--- a/solution.py
+++ b/solution.py
@@ -152,7 +152,7 @@
     return (2 * (2**slow - 1), len(set(a for a, _ in subsets(hops_a[:-1]))))
 
 
-def line_kernel(outer, seq_count, p_ref, wo_ref, s_ref, head_ref, out_ref, small_ref, *sems):
+def line_kernel(outer, seq_count, p_ref, s_ref, head_ref, small_ref, *sems):
     send_sems, recv_sems, local_sems = sems
     wt, seq = lax.axis_index("wt"), lax.axis_index("seq")
     line, inner = wt // INNER, wt % INNER
@@ -164,7 +164,6 @@
     pairs = [
         (s_ref, small_ref),
         (p_ref.at[:, own_columns(p_ref.shape[1])], head_ref),
-        (wo_ref.at[:, own_columns(wo_ref.shape[1])], out_ref),
     ]
     own = [
         pltpu.make_async_copy(source, target.at[0], local_sems.at[k])
@@ -184,31 +183,30 @@
         copy.wait()
 
 
-def gather_line(packed, w_out, small):
+def gather_line(packed, small):
     outer = lax.axis_size("wt") // INNER
     seq_count = lax.axis_size("seq")
     share, head_width = packed.shape
     vmem = pl.BlockSpec(memory_space=pltpu.VMEM)
-    copies = 3 * (outer - 1)
-    sent = 2 * outer * share * (head_width + w_out.shape[1])
+    copies = 2 * (outer - 1)
+    sent = 2 * outer * share * head_width
     return pl.pallas_call(
         functools.partial(line_kernel, outer, seq_count),
-        in_specs=[vmem] * 3,
-        out_specs=[vmem] * 3,
+        in_specs=[vmem] * 2,
+        out_specs=[vmem] * 2,
         out_shape=[
             jax.ShapeDtypeStruct((outer, share, head_width // seq_count), low),
-            jax.ShapeDtypeStruct((outer, share, w_out.shape[1] // seq_count), low),
             jax.ShapeDtypeStruct((outer,) + small.shape, low),
         ],
         scratch_shapes=[
             pltpu.SemaphoreType.DMA((copies,)),
             pltpu.SemaphoreType.DMA((copies,)),
-            pltpu.SemaphoreType.DMA((3,)),
+            pltpu.SemaphoreType.DMA((2,)),
         ],
         compiler_params=pltpu.CompilerParams(collective_id=3, has_side_effects=True),
         cost_estimate=pl.CostEstimate(flops=0, bytes_accessed=8 * sent, transcendentals=0),
         name="gather_line",
-    )(packed, w_out, small)
+    )(packed, small)
 
 
 def gather_kernel(
@@ -222,23 +220,28 @@
     line, inner = wt // INNER, wt % INNER
     hops = plane_hops(seq_count)
     slow = len(hops[0]) - 1
+    line_peers = [(flip_all(line, d) * INNER + inner, seq) for d in range(1, outer)]
     peers = [(wt - inner + flip(inner, bit), seq) for bit in inner_bits()]
-    peers += [(wt, flip(seq, bit)) for _, bit in bits_of("seq", seq_count)]
+    peers += [(wt, flip(seq, bit)) for _, bit in bits_of("seq", seq_count)] + line_peers
 
     def own_columns(total):
         wide = total // seq_count
         return pl.ds(pl.multiple_of(seq * wide, 128), wide)
 
-    fill = []
+    mine = own_columns(o_scr.shape[3])
+    fill = [
+        pltpu.make_async_copy(
+            wo_ref.at[:, mine], o_scr.at[line, inner, :, mine], local_sems.at[2 * outer]
+        )
+    ]
     for d in range(outer):
         at = flip_all(line, d)
         pairs = [
             (s_ref.at[d], s_scr.at[at, inner]),
             (p_ref.at[d], w_scr.at[at, inner, :, own_columns(head_width)]),
-            (wo_ref.at[d], o_scr.at[at, inner, :, own_columns(o_scr.shape[3])]),
         ]
         fill += [
-            pltpu.make_async_copy(source, target, local_sems.at[3 * d + k])
+            pltpu.make_async_copy(source, target, local_sems.at[2 * d + k])
             for k, (source, target) in enumerate(pairs)
         ]
     for copy in fill:
@@ -280,6 +283,10 @@
             if copy is not None:
                 copy.wait_recv()
 
+    out_line = [
+        out.start(wo_ref.at[:, mine], o_scr.at[line, inner, :, mine], peer)
+        for peer in line_peers
+    ]
     for copy in fill:
         copy.wait()
     waiting = [[] for _ in range(outer)]
@@ -298,6 +305,7 @@
                 place = s_scr.at[:, flip_all(inner, a)]
                 small_wait.append(out.start(place, place, hop_peer(("wt", bit))))
     arrive(small_wait)
+    arrive(out_line)
     out_wait = start_stage(o_scr, slice(None), 0)
 
     count = outer * INNER
@@ -369,11 +377,11 @@
     seq_count = lax.axis_size("seq")
     rows, width = tokens.shape
     share, head_width = packed.shape[1], packed.shape[2] * seq_count
-    out_width = w_out.shape[2] * seq_count
+    out_width = w_out.shape[1]
     slow_copies, last_copies = plane_copies(seq_count)
     each = slow_copies + last_copies
     small_copies = 2 ** len(inner_bits()) - 1
-    copies = (outer + 1) * each + small_copies
+    copies = (outer + 1) * each + small_copies + outer - 1
     vmem = pl.BlockSpec(memory_space=pltpu.VMEM)
     anywhere = pl.BlockSpec(memory_space=pl.ANY)
     sent = 2 * outer * INNER * share * (head_width + out_width)
@@ -394,7 +402,7 @@
             pltpu.VMEM((outer, INNER) + small.shape[1:], low),
             pltpu.SemaphoreType.DMA((copies,)),
             pltpu.SemaphoreType.DMA((copies,)),
-            pltpu.SemaphoreType.DMA((3 * outer,)),
+            pltpu.SemaphoreType.DMA((2 * outer + 1,)),
         ],
         compiler_params=pltpu.CompilerParams(
             collective_id=1, has_side_effects=True, vmem_limit_bytes=48 << 20
@@ -614,31 +622,44 @@
     )(info, units)
 
 
-def hidden_kernel(both_ref, grad_ref, down_ref, hidden_ref, units_ref):
+def hidden_kernel(near_ref, far_ref, grad_ref, down_ref, hidden_ref, units_ref):
     wide = hidden_ref.shape[1]
     hidden_grad = lax.dot_general(
         grad_ref[...], down_ref[...], (((1,), (1,)), ((), ())), preferred_element_type=full
     )
-    gate, upper = both_ref[:, :wide], both_ref[:, wide:]
-    sigma = 1.0 / (1.0 + jnp.exp(-gate))
-    taken = gate * sigma
-    hidden_ref[...] = (taken * upper).astype(low)
-    slope = sigma * (1.0 + gate * (1.0 - sigma))
-    units_ref[:, :wide] = (hidden_grad * upper * slope).astype(low)
-    units_ref[:, wide:] = (hidden_grad * taken).astype(low)
-
-
-def hidden_units(both, grad, down_w):
+    step, half = pl.program_id(0), pl.num_programs(0) // 2
+
+    def finish(both_ref):
+        gate, upper = both_ref[:, :wide], both_ref[:, wide:]
+        sigma = 1.0 / (1.0 + jnp.exp(-gate))
+        taken = gate * sigma
+        hidden_ref[...] = (taken * upper).astype(low)
+        slope = sigma * (1.0 + gate * (1.0 - sigma))
+        units_ref[:, :wide] = (hidden_grad * upper * slope).astype(low)
+        units_ref[:, wide:] = (hidden_grad * taken).astype(low)
+
+    @pl.when(step < half)
+    def _():
+        finish(near_ref)
+
+    @pl.when(step >= half)
+    def _():
+        finish(far_ref)
+
+
+def hidden_units(near, far, grad, down_w):
     total, width = grad.shape
     wide = down_w.shape[0]
-    block = min(512, total)
+    block = min(512, total // 2)
+    half = total // block // 2
     return pl.pallas_call(
         hidden_kernel,
         grid=(total // block,),
         in_specs=[
-            pl.BlockSpec((block, 2 * wide), lambda i: (i, 0)),
+            pl.BlockSpec((block, 2 * wide), lambda i: (jnp.minimum(i, half - 1), 0)),
+            pl.BlockSpec((block, 2 * wide), lambda i: (jnp.maximum(i - half, 0), 0)),
             pl.BlockSpec((block, width), lambda i: (i, 0)),
-            pl.BlockSpec((wide, width), lambda i: (0, 0)),
+            pl.BlockSpec((wide, width), lambda i: (0, 0), pipeline_mode=pl.Buffered(1)),
         ],
         out_specs=[
             pl.BlockSpec((block, wide), lambda i: (i, 0)),
@@ -648,14 +669,14 @@
             jax.ShapeDtypeStruct((total, wide), low),
             jax.ShapeDtypeStruct((total, 2 * wide), low),
         ],
-        compiler_params=pltpu.CompilerParams(vmem_limit_bytes=56 << 20),
+        compiler_params=pltpu.CompilerParams(vmem_limit_bytes=60 << 20),
         cost_estimate=pl.CostEstimate(
             flops=2 * total * width * wide,
             bytes_accessed=2 * total * (width + 7 * wide) + 2 * wide * width,
             transcendentals=total * wide,
         ),
         name="hidden_units",
-    )(both, grad, down_w)
+    )(near, far, grad, down_w)
 
 
 def after(value, *others):
@@ -853,9 +874,11 @@
     small = jnp.stack([line_of(v) for v in (attn_gain, b_query, b_key, b_value, ffn_gain)])
     small = jnp.pad(small.astype(low), ((0, 11), (0, 0)))
     packed = jnp.concatenate([w_query, w_key, w_value], axis=1).astype(low)
+    head_line, small_line = gather_line(packed, small)
+    project_inputs = (head_line, w_out.astype(low), small_line)
     normed_low, qkv, vectors, head_all, out_all = gather_project(
         tokens.reshape(rows, width),
-        *gather_line(packed, w_out.astype(low), small), cosine, sine,
+        *project_inputs, cosine, sine,
     )
     head_w = head_all.reshape(width, head_width)
     out_w = out_all.reshape(query_width, width)
@@ -884,7 +907,7 @@
         part_b = gather_hops(block[rows // 2 :], slow_b)
         near = jnp.stack([part_a, part_b]).reshape(near_rows, width)
         far = swap(near, core)
-        return jnp.concatenate([near, far], axis=0)
+        return (near, far, jnp.concatenate([near, far], axis=0))
 
     def hop_core(partial):
         other = swap(partial[near_rows:], core)
@@ -900,10 +923,11 @@
         return jnp.concatenate(got, axis=0)
 
     stages = list(range(1, len(slow_a)))[::-1]
-    grad_all = spread(upstream_low)
-    rows_all = spread(normed_two_low)
-    both = product(rows_all, units_w)
-    hidden, units_grad = hidden_units(both, grad_all, down_w)
+    grad_all = spread(upstream_low)[2]
+    rows_near, rows_far, rows_all = spread(normed_two_low)
+    both_near = product(rows_near, units_w)
+    both_far = product(rows_far, units_w)
+    hidden, units_grad = hidden_units(both_near, both_far, grad_all, down_w)
     down_grad = product_left(hidden, grad_all).astype(low)
     units_grad, down_grad = lax.optimization_barrier((units_grad, down_grad))
     down_grad = down_grad[:ff_here]

time: 953 us -> 911 us (0.956)
  Pallas kernels: 323 us -> 302 us
  waiting for transfers between devices: 238 us -> 220 us
    pallas_call x1, Pallas kernels: 64.4 us -> 32.6 us  [gather_line(): pl.pallas_call(functools.partial(line_kernel, outer, seq_count), in_specs...]
    pallas_call x1, Pallas kernels: 56.5 us -> 71.7 us  [gather_project(): pl.pallas_call(functools.partial(gather_kernel, outer, seq_count), in_spe...]
    ppermute x3, waiting for transfers between devices: 14 us -> 0.01 us  [inner_swap(): return lax.ppermute(value, 'wt', [(i, i ^ distance) for i in range(count)])]
    dot_general x3 -> x4, matrix products: 63.4 us -> 65.1 us  [product(): return jnp.dot(left, right, preferred_element_type=full)]
  transfers between devices with their start and end apart: 37 -> 37, of which waited for: 15 -> 17; matrix products, arithmetic and copies ran while one was open for 27% -> 30% of each run, Pallas kernels for 30% -> 29%
where the time goes in v6:
time: 911 us; the launch traced here: 904 us
  Pallas kernels  302 us (33%)
  waiting for transfers between devices  220 us (24%)
  matrix products  183 us (20%)
  other arithmetic  93.4 us (10%)
  local copies, waits for them, and re-layouts  56.6 us (6%)
  starting transfers between devices  33.1 us (4%)
  between operations  15.6 us (2%)
    ppermute x23, waiting for transfers between devices, swap(): return lax.ppermute(value, axis, [(i, i ^ bit) for i in range(count)])  165 us
    pallas_call x1, Pallas kernels, reduce_shares(): pl.pallas_call(functools.partial(reduce_kernel, outer, seq_count, count),...  95.1 us
    pallas_call x1, Pallas kernels, gather_project(): pl.pallas_call(functools.partial(gather_kernel, outer, seq_count), in_spe...  71.7 us
    dot_general x4, matrix products, product_left(): lax.dot_general(left, right, (((0,), (0,)), ((), ())), preferred_element_...  71.1 us
    dot_general x4, matrix products, product(): return jnp.dot(left, right, preferred_element_type=full)  65.1 us
    ppermute x7, waiting for transfers between devices, plane_swap(): return lax.ppermute(block, ('wt', 'seq'), pairs)  54.8 us
    dot_general x3, matrix products, product_right(): lax.dot_general(left, right, (((1,), (1,)), ((), ())), preferred_element_...  47.2 us
    pallas_call x1, Pallas kernels, hidden_units(): pl.pallas_call(hidden_kernel, grid=(total // block,), in_specs=[pl.BlockS...  37.3 us
  transfers between devices with their start and end apart: 37, of which 17 were waited for; matrix products, arithmetic and copies ran while one was open for 30% of the time, Pallas kernels for 29%

profile of v6, /device:TPU:0, one launch (start us, length us, event | category | flops | bytes accessed | tf_op | source)
XLA Modules:
  0.0 903.8 jit_solution(630037631807696154)
XLA Ops:
  7.8 5.3 split_units.1
  26.5 32.6 %gather_line.1 = (bf16[4,96,1024]{2,1,0:T(8,128)(2,1)}, bf16[4,16,128]{2,1,0:T(8,128)(2,1)}) custom-call(bf16[96,2048]{1,0:T(8,128)(2,1)} %pad_maximum_fusion.16.p_ref, bf16[16,128]{1,0:T(8,128)(2,1)} %pad.43.s_ref), custom_call_target="tpu_custom_call" | custom-call | bytes 12582912 | tf_op jit(solution)/shard_map/gather_line/pallas_call | solution.py:193
  61.4 71.7 %gather_project.1 = (bf16[512,1536]{1,0:T(8,128)(2,1)S(1)}, bf16[512,2048]{1,0:T(8,128)(2,1)}, f32[8,2048]{1,0:T(8,128)S(1)}, bf16[4,4,96,2048]{3,2,1,0:T(8,128)(2,1)}, bf16[4,4,96,1536]{3,2,1,0:T(8,128)(2,1)}) custom-call(bf16[512,1536]{1,0:T(8,128)(2,1)S(1)} %bitcast.165, bf16[4,96,1024]{2,1,0:T(8,128)(2,1)S(1)} %copy-done.8, ...), custom_call_target="tpu_custom_call" | custom-call | flops 25769803776 | bytes 22020096 | tf_op jit(solution)/shard_map/gather_project/pallas_call | solution.py:388
  145.5 3.8 collective-permute-done
  151.6 6.7 collective-permute-done.9
  161.2 5.0 collective-permute-done.11
  169.8 22.7 %attend_forward.1 = bf16[512,1536]{1,0:T(8,128)(2,1)} custom-call(s32[1,1024]{1,0:T(1,128)} %compare_select_fusion.kpos_ref, bf16[512,2048]{1,0:T(8,128)(2,1)} %get-tuple-element.41.q_ref, bf16[1024,512]{1,0:T(8,128)(2,1)} %bitcast.182, bf16[1024,512]{1,0:T(8,128)(2,1)} %bitcast.183), custom_call_target="tpu_custom_call" | custom-call | flops 9663676416 | bytes 4194304 | tf_op jit(solution)/shard_map/attend_forward/pallas_call | solution.py:711
  192.6 5.1 multiply_reduce_fusion.2
  202.1 3.1 collective-permute-done.12
  207.3 3.2 pad_maximum_fusion.3
  214.5 17.4 %collective-permute-done.1 = bf16[1,256,1536]{2,1,0:T(8,128)(2,1)S(1)} collective-permute-done((bf16[1,256,1536]{2,1,0:T(8,128)(2,1)S(1)}, bf16[1,256,1536]{2,1,0:T(8,128)(2,1)S(1)}, u32[]{:S(2)}, u32[]{:S(2)}) %collective-permute-start.1) | collective-permute-done | bytes 786464 | tf_op jit(solution)/shard_map/ppermute | solution.py:54
  234.4 33.3 %collective-permute-done.2 = bf16[2,256,1536]{2,1,0:T(8,128)(2,1)S(1)} collective-permute-done((bf16[2,256,1536]{2,1,0:T(8,128)(2,1)S(1)}, bf16[2,256,1536]{2,1,0:T(8,128)(2,1)S(1)}, u32[]{:S(2)}, u32[]{:S(2)}) %collective-permute-start.2) | collective-permute-done | bytes 1572896 | tf_op jit(solution)/shard_map/ppermute | solution.py:54
  268.9 3.3 pad_maximum_fusion.2
  272.2 4.0 pad.44.down_ref
  276.2 10.5 %pad_maximum_fusion.grad_ref = bf16[4096,1536]{1,0:T(8,128)(2,1)} fusion(bf16[2048,1536]{1,0:T(8,128)(2,1)} %collective-permute-done.13, bf16[2048,1536]{1,0:T(8,128)(2,1)} %bitcast.30), kind=kLoop, calls=%fused_computation.2 | loop fusion | flops 25165824 | bytes 25165824 | tf_op jit(solution)/shard_map/concatenate | solution.py:910
  286.6 21.6 %fusion.36.near_ref = f32[2048,2304]{1,0:T(8,128)} fusion(bf16[2048,1536]{1,0:T(8,128)(2,1)} %bitcast.14, bf16[1536,2304]{1,0:T(8,128)(2,1)} %bitcast.194), kind=kOutput, calls=%fused_computation.155 | convolution fusion | flops 14495514624 | bytes 32243712 | tf_op jit(solution)/shard_map/dot_general | solution.py:27
  308.3 19.2 %fusion.37.far_ref = f32[2048,2304]{1,0:T(8,128)} fusion(bf16[2048,1536]{1,0:T(8,128)(2,1)} %collective-permute-done.8, bf16[1536,2304]{1,0:T(8,128)(2,1)S(1)} %bitcast.196), kind=kOutput, calls=%fused_computation.156 | convolution fusion | flops 14495514624 | bytes 32243712 | tf_op jit(solution)/shard_map/dot_general | solution.py:27
  327.5 37.3 %hidden_units.1 = (bf16[4096,1152]{1,0:T(8,128)(2,1)}, bf16[4096,2304]{1,0:T(8,128)(2,1)}) custom-call(f32[2048,2304]{1,0:T(8,128)} %fusion.36.near_ref, f32[2048,2304]{1,0:T(8,128)} %fusion.37.far_ref, bf16[4096,1536]{1,0:T(8,128)(2,1)} %pad_maximum_fusion.grad_ref, bf16[1152,1536]{1,0:T(8,128)(2,1)} %pad.44.down_ref), custom_call_target="tpu_custom_call" | custom-call | flops 14495514624 | bytes 82182144 | tf_op jit(solution)/shard_map/hidden_units/pallas_call | solution.py:655
  364.7 20.3 %convolution_convert_fusion.5 = bf16[1152,1536]{1,0:T(8,128)(2,1)S(1)} fusion(bf16[4096,1152]{1,0:T(8,128)(2,1)} %get-tuple-element.50, bf16[2048,1536]{1,0:T(8,128)(2,1)} %collective-permute-done.13, bf16[2048,1536]{1,0:T(8,128)(2,1)} %bitcast.30), kind=kOutput, calls=%fused_computation.9 | convolution fusion | flops 14522449920 | bytes 25559040 | tf_op jit(solution)/shard_map/dot_general | solution.py:31
  387.1 34.6 %convolution_convert_fusion.1 = bf16[4096,1536]{1,0:T(8,128)(2,1)S(1)} fusion(bf16[4096,2304]{1,0:T(8,128)(2,1)} %get-tuple-element.49, bf16[1536,2304]{1,0:T(8,128)(2,1)} %bitcast.195), kind=kOutput, calls=%fused_computation.1 | convolution fusion | flops 28997320704 | bytes 38535168 | tf_op jit(solution)/shard_map/dot_general | solution.py:35
  421.8 3.0 slice.295
  424.8 3.7 copy-done.16
  430.0 6.2 pad_maximum_fusion.1
  436.2 36.6 %convolution_convert_fusion.2 = bf16[1536,2304]{1,0:T(8,128)(2,1)} fusion(bf16[4096,1536]{1,0:T(8,128)(2,1)S(1)} %pad_maximum_fusion.1, bf16[4096,2304]{1,0:T(8,128)(2,1)} %get-tuple-element.49), kind=kOutput, calls=%fused_computation.6 | convolution fusion | flops 28994568192 | bytes 38535168 | tf_op jit(solution)/shard_map/dot_general | solution.py:31
  472.8 9.2 %add_convert_fusion.1 = bf16[2048,1536]{1,0:T(8,128)(2,1)} fusion(bf16[2048,1536]{1,0:T(8,128)(2,1)} %collective-permute-done.14, bf16[4096,1536]{1,0:T(8,128)(2,1)} %copy-done.16), kind=kLoop, calls=%fused_computation.5 | loop fusion | flops 12582912 | bytes 18874368 | tf_op jit(solution)/shard_map/convert_element_type | solution.py:914
  483.1 4.4 fusion.30
  489.4 14.8 %collective-permute-done.32 = bf16[1,280,1536]{2,1,0:T(8,128)(2,1)S(1)} collective-permute-done((bf16[1,280,1536]{2,1,0:T(8,128)(2,1)}, bf16[1,280,1536]{2,1,0:T(8,128)(2,1)S(1)}, u32[]{:S(2)}, u32[]{:S(2)}) %collective-permute-start.32) | collective-permute-done | bytes 860192 | tf_op jit(solution)/shard_map/ppermute | solution.py:54
  506.9 30.1 %collective-permute-done.15 = bf16[2,256,1536]{2,1,0:T(8,128)(2,1)S(1)} collective-permute-done((bf16[2,256,1536]{2,1,0:T(8,128)(2,1)S(1)}, bf16[2,256,1536]{2,1,0:T(8,128)(2,1)S(1)}, u32[]{:S(2)}, u32[]{:S(2)}) %collective-permute-start.15) | collective-permute-done | bytes 1572896 | tf_op jit(solution)/shard_map/ppermute | solution.py:54
  540.9 19.1 %convolution_convert_fusion = bf16[4096,1536]{1,0:T(8,128)(2,1)S(1)} fusion(bf16[4096,1152]{1,0:T(8,128)(2,1)} %get-tuple-element.50, bf16[1120,1536]{1,0:T(8,128)(2,1)S(1)} %copy-done.26), kind=kOutput, calls=%fused_computation | convolution fusion | flops 14501806080 | bytes 25460736 | tf_op jit(solution)/shard_map/dot_general | solution.py:27
  560.0 3.4 slice.250
  563.4 3.1 copy-done.15
  574.1 3.7 convolution_convert_fusion.6.g_ref
  577.8 31.1 %attend_backward.1 = (bf16[512,1536]{1,0:T(8,128)(2,1)}, f32[1024,256]{1,0:T(8,128)}, f32[1024,256]{1,0:T(8,128)}) custom-call(s32[1,1024]{1,0:T(1,128)} %compare_select_fusion.kpos_ref, f32[512,128]{1,0:T(8,128)} %copy-done.4, f32[512,128]{1,0:T(8,128)} %copy-done.6, bf16[512,2048]{1,0:T(8,128)(2,1)} %get-tuple-element.41.q_ref, ...), custom_call_target="tpu_custom_call" | custom-call | flops 24159191040 | bytes 9437184 | tf_op jit(solution)/shard_map/attend_backward/pallas_call | solution.py:779
  612.8 7.2 convolution_convert_fusion.4
  619.9 6.1 collective-permute-done.24
  634.7 8.8 fusion.7
  644.6 7.0 convolution_convert_fusion.3
  651.6 95.1 %reduce_shares.1 = (f32[96,1536]{1,0:T(8,128)}, f32[96,2048]{1,0:T(8,128)}, f32[16,512]{1,0:T(8,128)}) custom-call(bf16[4,4,96,1536]{3,2,1,0:T(8,128)(2,1)} %bitcast.174, bf16[4,4,96,2048]{3,2,1,0:T(8,128)(2,1)} %bitcast.173, bf16[4,4,16,512]{3,2,1,0:T(8,128)(2,1)} %bitcast.181), custom_call_target="tpu_custom_call" | custom-call | bytes 90177536 | tf_op jit(solution)/shard_map/reduce_shares/pallas_call | solution.py:551
  746.7 4.8 fusion.15
  751.6 9.0 %add_convert_fusion = bf16[2048,1536]{1,0:T(8,128)(2,1)} fusion(bf16[2048,1536]{1,0:T(8,128)(2,1)} %collective-permute-done.19, bf16[4096,1536]{1,0:T(8,128)(2,1)} %copy-done.15), kind=kLoop, calls=%fused_computation.4 | loop fusion | flops 12582912 | bytes 18874368 | tf_op jit(solution)/shard_map/convert_element_type | solution.py:914
  760.6 5.1 fusion.29
  773.9 38.8 %collective-permute-done.26 = bf16[96,2304]{1,0:T(8,128)(2,1)S(1)} collective-permute-done((bf16[96,2304]{1,0:T(8,128)(2,1)S(1)}, bf16[96,2304]{1,0:T(8,128)(2,1)S(1)}, u32[]{:S(2)}, u32[]{:S(2)}) %collective-permute-start.26) | collective-permute-done | bytes 442400 | tf_op jit(solution)/shard_map/ppermute | solution.py:973
  814.2 6.5 collective-permute-done.27
  826.4 5.7 collective-permute-done.30
  832.1 3.8 collective-permute-done.31
  838.0 33.5 %collective-permute-done.20 = bf16[2,256,1536]{2,1,0:T(8,128)(2,1)S(1)} collective-permute-done((bf16[2,256,1536]{2,1,0:T(8,128)(2,1)}, bf16[2,256,1536]{2,1,0:T(8,128)(2,1)S(1)}, u32[]{:S(2)}, u32[]{:S(2)}) %collective-permute-start.20) | collective-permute-done | bytes 1572896 | tf_op jit(solution)/shard_map/ppermute | solution.py:54
  876.6 6.2 join_units.1
  882.8 8.8 collective-permute-done.22
  (259 shorter events, 112.6 us)
Async XLA Ops:
  7.2 265.0 %all-gather.6.cloned.1.call-start = ((), (), s32[]{:S(2)}) async-start(), calls=%async_computation.5 | async-start | bytes 4300800 | tf_op jit(solution)/shard_map/all_gather | solution.py:838
  15.9 124.8 %collective-permute-start.5 = (bf16[96,2304]{1,0:T(8,128)(2,1)}, bf16[96,2304]{1,0:T(8,128)(2,1)}, u32[]{:S(2)}, u32[]{:S(2)}) collective-permute-start(bf16[96,2304]{1,0:T(8,128)(2,1)} %get-tuple-element.89), channel_id=1, source_target_pairs={{0,2},{2,0},{4,6},{6,4},{8,10},{10,8},{12,14},{14,12},{16,18},{18,... | collective-permute-start | bytes 1327112 | tf_op jit(solution)/shard_map/ppermute | solution.py:854
  16.4 125.7 %collective-permute-start.6 = (bf16[96,2304]{1,0:T(8,128)(2,1)}, bf16[96,2304]{1,0:T(8,128)(2,1)}, u32[]{:S(2)}, u32[]{:S(2)}) collective-permute-start(bf16[96,2304]{1,0:T(8,128)(2,1)} %get-tuple-element.88), channel_id=1, source_target_pairs={{0,4},{2,6},{4,0},{6,2},{8,12},{10,14},{12,8},{14,10},{16,20},{18,... | collective-permute-start | bytes 1327112 | tf_op jit(solution)/shard_map/ppermute | solution.py:854
  18.8 123.2 %collective-permute-start.7 = (bf16[96,2304]{1,0:T(8,128)(2,1)}, bf16[96,2304]{1,0:T(8,128)(2,1)}, u32[]{:S(2)}, u32[]{:S(2)}) collective-permute-start(bf16[96,2304]{1,0:T(8,128)(2,1)} %get-tuple-element.87), channel_id=1, source_target_pairs={{0,6},{2,4},{4,2},{6,0},{8,14},{10,12},{12,10},{14,8},{16,22},{18,... | collective-permute-start | bytes 1327112 | tf_op jit(solution)/shard_map/ppermute | solution.py:854
  20.0 39.4 %copy-start.2 = (bf16[1,512,1536]{2,1,0:T(8,128)(2,1)S(1)}, bf16[1,512,1536]{2,1,0:T(8,128)(2,1)}, u32[]{:S(2)}) copy-start(bf16[1,512,1536]{2,1,0:T(8,128)(2,1)} %param.15) | copy-start | bytes 4718596
  20.0 266.6 %all-gather.4.cloned.1.call-start = ((), (), s32[]{:S(2)}) async-start(), calls=%async_computation.2 | async-start | bytes 8847360 | tf_op jit(solution)/shard_map/all_gather | solution.py:838
  59.3 73.7 %copy-start.4 = (f32[512,128]{1,0:T(8,128)}, f32[512,128]{1,0:T(8,128)S(1)}, u32[]{:S(2)}) copy-start(f32[512,128]{1,0:T(8,128)S(1)} %get-tuple-element.121.cos_ref) | copy-start | bytes 786436
  59.3 73.7 %copy-start.6 = (f32[512,128]{1,0:T(8,128)}, f32[512,128]{1,0:T(8,128)S(1)}, u32[]{:S(2)}) copy-start(f32[512,128]{1,0:T(8,128)S(1)} %get-tuple-element.122.sin_ref) | copy-start | bytes 786436
  61.4 76.0 %copy-start.18 = (bf16[1,512,1536]{2,1,0:T(8,128)(2,1)S(1)}, bf16[1,512,1536]{2,1,0:T(8,128)(2,1)}, u32[]{:S(2)}) copy-start(bf16[1,512,1536]{2,1,0:T(8,128)(2,1)} %param.29) | copy-start | bytes 4718596
  135.3 14.0 %collective-permute-start = (bf16[1,512,512]{2,1,0:T(8,128)(2,1)}, bf16[1,512,512]{2,1,0:T(8,128)(2,1)}, u32[]{:S(2)}, u32[]{:S(2)}) collective-permute-start(bf16[1,512,512]{2,1,0:T(8,128)(2,1)} %slice_bitcast_fusion.10), channel_id=1, source_target_pairs={{0,1},{1,0},{2,3},{3,2},{4,5},{5,4},{6,7},{7,6},{8,9},{9,8},{10,11... | collective-permute-start | bytes 1572872 | tf_op jit(solution)/shard_map/ppermute | solution.py:54
  138.8 19.5 %collective-permute-start.9 = (bf16[1,256,1536]{2,1,0:T(8,128)(2,1)}, bf16[1,256,1536]{2,1,0:T(8,128)(2,1)}, u32[]{:S(2)}, u32[]{:S(2)}) collective-permute-start(bf16[1,256,1536]{2,1,0:T(8,128)(2,1)} %get-tuple-element.92), channel_id=1, source_target_pairs={{0,4},{2,6},{4,0},{6,2},{8,12},{10,14},{12,8},{14,10},{16,20},{18,... | collective-permute-start | bytes 2359304 | tf_op jit(solution)/shard_map/ppermute | solution.py:54
  140.7 71.2 %copy-start.32 = (f32[1536]{0:T(1024)}, f32[1536]{0:T(1024)S(1)}, u32[]{:S(2)}) copy-start(f32[1536]{0:T(1024)S(1)} %get-tuple-element.69) | copy-start | bytes 18436
  140.7 25.5 %collective-permute-start.11 = (bf16[1,256,1536]{2,1,0:T(8,128)(2,1)}, bf16[1,256,1536]{2,1,0:T(8,128)(2,1)}, u32[]{:S(2)}, u32[]{:S(2)}) collective-permute-start(bf16[1,256,1536]{2,1,0:T(8,128)(2,1)} %get-tuple-element.93), channel_id=1, source_target_pairs={{0,1},{1,0},{2,3},{3,2},{4,5},{5,4},{6,7},{7,6},{8,9},{9,8},{10,11... | collective-permute-start | bytes 2359304 | tf_op jit(solution)/shard_map/ppermute | solution.py:54
  145.3 336.7 %reduce-scatter.5.cloned.1.call-start = ((), (), s32[]{:S(2)}) async-start(), calls=%async_computation.4 | async-start | bytes 4300800 | tf_op jit(solution)/shard_map/reduce_scatter | solution.py:841
  160.0 39.9 %collective-permute-start.10 = (bf16[2,256,1536]{2,1,0:T(8,128)(2,1)S(1)}, bf16[2,256,1536]{2,1,0:T(8,128)(2,1)}, u32[]{:S(2)}, u32[]{:S(2)}) collective-permute-start(bf16[2,256,1536]{2,1,0:T(8,128)(2,1)S(1)} %pad_maximum_fusion.12), channel_id=1, source_target_pairs={{0,1},{1,0},{2,3},{3,2},{4,5},{5,4},{6,7},{7,6},{8,9},{9,8},{10,11... | collective-permute-start | bytes 4718600 | tf_op jit(solution)/shard_map/ppermute | solution.py:54
  168.9 36.3 %collective-permute-start.12 = (bf16[2,256,1536]{2,1,0:T(8,128)(2,1)}, bf16[2,256,1536]{2,1,0:T(8,128)(2,1)}, u32[]{:S(2)}, u32[]{:S(2)}) collective-permute-start(bf16[2,256,1536]{2,1,0:T(8,128)(2,1)} %pad_maximum_fusion.13), channel_id=1, source_target_pairs={{0,4},{2,6},{4,0},{6,2},{8,12},{10,14},{12,8},{14,10},{16,20},{18,... | collective-permute-start | bytes 4718600 | tf_op jit(solution)/shard_map/ppermute | solution.py:54
  197.7 14.2 %copy-start.12 = (f32[512,1536]{1,0:T(8,128)}, f32[512,1536]{1,0:T(8,128)S(1)}, u32[]{:S(2)}) copy-start(f32[512,1536]{1,0:T(8,128)S(1)} %get-tuple-element.115) | copy-start | bytes 9437188
  198.3 13.6 %copy-start.35 = (f32[512]{0:T(512)}, f32[512]{0:T(512)S(1)}, u32[]{:S(2)}) copy-start(f32[512]{0:T(512)S(1)} %get-tuple-element.113) | copy-start | bytes 6148
  210.5 65.6 %collective-permute-start.13 = (bf16[2048,1536]{1,0:T(8,128)(2,1)}, bf16[2048,1536]{1,0:T(8,128)(2,1)}, u32[]{:S(2)}, u32[]{:S(2)}) collective-permute-start(bf16[2048,1536]{1,0:T(8,128)(2,1)} %bitcast.30), channel_id=1, source_target_pairs={{0,2},{2,0},{4,6},{6,4},{8,10},{10,8},{12,14},{14,12},{16,18},{18,... | collective-permute-start | bytes 18874376 | tf_op jit(solution)/shard_map/ppermute | solution.py:54
  212.4 19.5 %collective-permute-start.1 = (bf16[1,256,1536]{2,1,0:T(8,128)(2,1)S(1)}, bf16[1,256,1536]{2,1,0:T(8,128)(2,1)S(1)}, u32[]{:S(2)}, u32[]{:S(2)}) collective-permute-start(bf16[1,256,1536]{2,1,0:T(8,128)(2,1)S(1)} %get-tuple-element.94), channel_id=1, source_target_pairs={{0,4},{2,6},{4,0},{6,2},{8,12},{10,14},{12,8},{14,10},{16,20},{18,... | collective-permute-start | bytes 2359304 | tf_op jit(solution)/shard_map/ppermute | solution.py:54
  213.4 19.7 %collective-permute-start.3 = (bf16[1,256,1536]{2,1,0:T(8,128)(2,1)S(1)}, bf16[1,256,1536]{2,1,0:T(8,128)(2,1)S(1)}, u32[]{:S(2)}, u32[]{:S(2)}) collective-permute-start(bf16[1,256,1536]{2,1,0:T(8,128)(2,1)S(1)} %get-tuple-element.95), channel_id=1, source_target_pairs={{0,1},{1,0},{2,3},{3,2},{4,5},{5,4},{6,7},{7,6},{8,9},{9,8},{10,11... | collective-permute-start | bytes 2359304 | tf_op jit(solution)/shard_map/ppermute | solution.py:54
  232.0 35.6 %collective-permute-start.2 = (bf16[2,256,1536]{2,1,0:T(8,128)(2,1)S(1)}, bf16[2,256,1536]{2,1,0:T(8,128)(2,1)S(1)}, u32[]{:S(2)}, u32[]{:S(2)}) collective-permute-start(bf16[2,256,1536]{2,1,0:T(8,128)(2,1)S(1)} %pad_maximum_fusion.10), channel_id=1, source_target_pairs={{0,1},{1,0},{2,3},{3,2},{4,5},{5,4},{6,7},{7,6},{8,9},{9,8},{10,11... | collective-permute-start | bytes 4718600 | tf_op jit(solution)/shard_map/ppermute | solution.py:54
  233.2 35.3 %collective-permute-start.4 = (bf16[2,256,1536]{2,1,0:T(8,128)(2,1)S(1)}, bf16[2,256,1536]{2,1,0:T(8,128)(2,1)S(1)}, u32[]{:S(2)}, u32[]{:S(2)}) collective-permute-start(bf16[2,256,1536]{2,1,0:T(8,128)(2,1)S(1)} %pad_maximum_fusion.11), channel_id=1, source_target_pairs={{0,4},{2,6},{4,0},{6,2},{8,12},{10,14},{12,8},{14,10},{16,20},{18,... | collective-permute-start | bytes 4718600 | tf_op jit(solution)/shard_map/ppermute | solution.py:54
  272.2 36.1 %collective-permute-start.8 = (bf16[2048,1536]{1,0:T(8,128)(2,1)}, bf16[2048,1536]{1,0:T(8,128)(2,1)}, u32[]{:S(2)}, u32[]{:S(2)}) collective-permute-start(bf16[2048,1536]{1,0:T(8,128)(2,1)} %bitcast.14), channel_id=1, source_target_pairs={{0,2},{2,0},{4,6},{6,4},{8,10},{10,8},{12,14},{14,12},{16,18},{18,... | collective-permute-start | bytes 18874376 | tf_op jit(solution)/shard_map/ppermute | solution.py:54
  286.6 21.6 %copy-start.42 = (bf16[4,384,2304]{2,1,0:T(8,128)(2,1)S(1)}, bf16[4,384,2304]{2,1,0:T(8,128)(2,1)}, u32[]{:S(2)}) copy-start(bf16[4,384,2304]{2,1,0:T(8,128)(2,1)} %all-gather.4.cloned.1.call-done) | copy-start | bytes 21233668
  387.1 379.6 %reduce-scatter.3.cloned.1.call-start = ((), (), s32[]{:S(2)}) async-start(), calls=%async_computation.3 | async-start | bytes 8847360 | tf_op jit(solution)/shard_map/reduce_scatter | solution.py:841
  428.5 44.3 %collective-permute-start.14 = (bf16[2048,1536]{1,0:T(8,128)(2,1)}, bf16[2048,1536]{1,0:T(8,128)(2,1)}, u32[]{:S(2)}, u32[]{:S(2)}) collective-permute-start(bf16[2048,1536]{1,0:T(8,128)(2,1)} %slice.295), channel_id=1, source_target_pairs={{0,2},{2,0},{4,6},{6,4},{8,10},{10,8},{12,14},{14,12},{16,18},{18,... | collective-permute-start | bytes 18874376 | tf_op jit(solution)/shard_map/ppermute | solution.py:54
  482.0 22.2 %collective-permute-start.32 = (bf16[1,280,1536]{2,1,0:T(8,128)(2,1)}, bf16[1,280,1536]{2,1,0:T(8,128)(2,1)S(1)}, u32[]{:S(2)}, u32[]{:S(2)}) collective-permute-start(bf16[1,280,1536]{2,1,0:T(8,128)(2,1)} %reduce-scatter.5.cloned.1.call-done), channel_id=1, source_target_pairs={{0,1},{1,0},{2,3},{3,2},{4,5},{5,4},{6,7},{7,6},{8,9},{9,8},{10,11... | collective-permute-start | bytes 2580488 | tf_op jit(solution)/shard_map/ppermute | solution.py:54
  487.4 49.5 %collective-permute-start.15 = (bf16[2,256,1536]{2,1,0:T(8,128)(2,1)S(1)}, bf16[2,256,1536]{2,1,0:T(8,128)(2,1)S(1)}, u32[]{:S(2)}, u32[]{:S(2)}) collective-permute-start(bf16[2,256,1536]{2,1,0:T(8,128)(2,1)S(1)} %bitcast.180), channel_id=1, source_target_pairs={{0,1},{1,0},{2,3},{3,2},{4,5},{5,4},{6,7},{7,6},{8,9},{9,8},{10,11... | collective-permute-start | bytes 4718600 | tf_op jit(solution)/shard_map/ppermute | solution.py:54
  488.6 48.8 %collective-permute-start.16 = (bf16[2,256,1536]{2,1,0:T(8,128)(2,1)S(1)}, bf16[2,256,1536]{2,1,0:T(8,128)(2,1)S(1)}, u32[]{:S(2)}, u32[]{:S(2)}) collective-permute-start(bf16[2,256,1536]{2,1,0:T(8,128)(2,1)S(1)} %bitcast.179), channel_id=1, source_target_pairs={{0,4},{2,6},{4,0},{6,2},{8,12},{10,14},{12,8},{14,10},{16,20},{18,... | collective-permute-start | bytes 4718600 | tf_op jit(solution)/shard_map/ppermute | solution.py:54
  538.8 27.7 %collective-permute-start.17 = (bf16[256,1536]{1,0:T(8,128)(2,1)S(1)}, bf16[256,1536]{1,0:T(8,128)(2,1)}, u32[]{:S(2)}, u32[]{:S(2)}) collective-permute-start(bf16[256,1536]{1,0:T(8,128)(2,1)S(1)} %slice_bitcast_fusion.2), channel_id=1, source_target_pairs={{0,4},{2,6},{4,0},{6,2},{8,12},{10,14},{12,8},{14,10},{16,20},{18,... | collective-permute-start | bytes 2359304 | tf_op jit(solution)/shard_map/ppermute | solution.py:54
  539.8 28.2 %collective-permute-start.18 = (bf16[256,1536]{1,0:T(8,128)(2,1)}, bf16[256,1536]{1,0:T(8,128)(2,1)}, u32[]{:S(2)}, u32[]{:S(2)}) collective-permute-start(bf16[256,1536]{1,0:T(8,128)(2,1)} %slice_bitcast_fusion), channel_id=1, source_target_pairs={{0,1},{1,0},{2,3},{3,2},{4,5},{5,4},{6,7},{7,6},{8,9},{9,8},{10,11... | collective-permute-start | bytes 2359304 | tf_op jit(solution)/shard_map/ppermute | solution.py:54
  566.5 185.1 %collective-permute-start.19 = (bf16[2048,1536]{1,0:T(8,128)(2,1)}, bf16[2048,1536]{1,0:T(8,128)(2,1)}, u32[]{:S(2)}, u32[]{:S(2)}) collective-permute-start(bf16[2048,1536]{1,0:T(8,128)(2,1)} %slice.250), channel_id=1, source_target_pairs={{0,2},{2,0},{4,6},{6,4},{8,10},{10,8},{12,14},{14,12},{16,18},{18,... | collective-permute-start | bytes 18874376 | tf_op jit(solution)/shard_map/ppermute | solution.py:54
  611.7 14.3 %collective-permute-start.24 = (bf16[512,512]{1,0:T(8,128)(2,1)S(1)}, bf16[512,512]{1,0:T(8,128)(2,1)}, u32[]{:S(2)}, u32[]{:S(2)}) collective-permute-start(bf16[512,512]{1,0:T(8,128)(2,1)S(1)} %pad_maximum_fusion.15), channel_id=1, source_target_pairs={{0,1},{1,0},{2,3},{3,2},{4,5},{5,4},{6,7},{7,6},{8,9},{9,8},{10,11... | collective-permute-start | bytes 1572872 | tf_op jit(solution)/shard_map/ppermute | solution.py:54
  651.6 95.1 %copy-start.39 = (f32[512]{0:T(512)S(1)}, f32[512]{0:T(512)}, u32[]{:S(2)}) copy-start(f32[512]{0:T(512)} %get-tuple-element.110) | copy-start | bytes 6148
  765.7 70.4 %collective-permute-start.21 = (bf16[2,256,1536]{2,1,0:T(8,128)(2,1)}, bf16[2,256,1536]{2,1,0:T(8,128)(2,1)}, u32[]{:S(2)}, u32[]{:S(2)}) collective-permute-start(bf16[2,256,1536]{2,1,0:T(8,128)(2,1)} %bitcast.42), channel_id=1, source_target_pairs={{0,4},{2,6},{4,0},{6,2},{8,12},{10,14},{12,8},{14,10},{16,20},{18,... | collective-permute-start | bytes 4718600 | tf_op jit(solution)/shard_map/ppermute | solution.py:54
  768.2 5.1 collective-permute-start.25
  768.3 44.4 %collective-permute-start.26 = (bf16[96,2304]{1,0:T(8,128)(2,1)S(1)}, bf16[96,2304]{1,0:T(8,128)(2,1)S(1)}, u32[]{:S(2)}, u32[]{:S(2)}) collective-permute-start(bf16[96,2304]{1,0:T(8,128)(2,1)S(1)} %get-tuple-element.80), channel_id=1, source_target_pairs={{0,4},{1,5},{2,6},{3,7},{4,0},{5,1},{6,2},{7,3},{8,12},{9,13},{10,... | collective-permute-start | bytes 1327112 | tf_op jit(solution)/shard_map/ppermute | solution.py:973
  769.4 51.2 %collective-permute-start.27 = (bf16[96,2304]{1,0:T(8,128)(2,1)S(1)}, bf16[96,2304]{1,0:T(8,128)(2,1)S(1)}, u32[]{:S(2)}, u32[]{:S(2)}) collective-permute-start(bf16[96,2304]{1,0:T(8,128)(2,1)S(1)} %get-tuple-element.79), channel_id=1, source_target_pairs={{0,6},{1,7},{2,4},{3,5},{4,2},{5,3},{6,0},{7,1},{8,14},{9,15},{10,... | collective-permute-start | bytes 1327112 | tf_op jit(solution)/shard_map/ppermute | solution.py:973
  770.1 52.9 %collective-permute-start.28 = (bf16[96,2304]{1,0:T(8,128)(2,1)S(1)}, bf16[96,2304]{1,0:T(8,128)(2,1)S(1)}, u32[]{:S(2)}, u32[]{:S(2)}) collective-permute-start(bf16[96,2304]{1,0:T(8,128)(2,1)S(1)} %bitcast.178), channel_id=1, source_target_pairs={{0,1},{1,0},{2,3},{3,2},{4,5},{5,4},{6,7},{7,6},{8,9},{9,8},{10,11... | collective-permute-start | bytes 1327112 | tf_op jit(solution)/shard_map/ppermute | solution.py:973
  773.3 53.1 %collective-permute-start.29 = (bf16[96,2304]{1,0:T(8,128)(2,1)S(1)}, bf16[96,2304]{1,0:T(8,128)(2,1)S(1)}, u32[]{:S(2)}, u32[]{:S(2)}) collective-permute-start(bf16[96,2304]{1,0:T(8,128)(2,1)S(1)} %get-tuple-element.81), channel_id=1, source_target_pairs={{0,3},{1,2},{2,1},{3,0},{4,7},{5,6},{6,5},{7,4},{8,11},{9,10},{10,... | collective-permute-start | bytes 1327112 | tf_op jit(solution)/shard_map/ppermute | solution.py:973
  812.7 19.4 %collective-permute-start.30 = (bf16[96,2304]{1,0:T(8,128)(2,1)S(1)}, bf16[96,2304]{1,0:T(8,128)(2,1)S(1)}, u32[]{:S(2)}, u32[]{:S(2)}) collective-permute-start(bf16[96,2304]{1,0:T(8,128)(2,1)S(1)} %get-tuple-element.80), channel_id=1, source_target_pairs={{0,5},{1,4},{2,7},{3,6},{4,1},{5,0},{6,3},{7,2},{8,13},{9,12},{10,... | collective-permute-start | bytes 1327112 | tf_op jit(solution)/shard_map/ppermute | solution.py:973
  820.6 15.3 %collective-permute-start.31 = (bf16[96,2304]{1,0:T(8,128)(2,1)S(1)}, bf16[96,2304]{1,0:T(8,128)(2,1)S(1)}, u32[]{:S(2)}, u32[]{:S(2)}) collective-permute-start(bf16[96,2304]{1,0:T(8,128)(2,1)S(1)} %get-tuple-element.79), channel_id=1, source_target_pairs={{0,7},{1,6},{2,5},{3,4},{4,3},{5,2},{6,1},{7,0},{8,15},{9,14},{10,... | collective-permute-start | bytes 1327112 | tf_op jit(solution)/shard_map/ppermute | solution.py:973
  823.1 48.5 %collective-permute-start.20 = (bf16[2,256,1536]{2,1,0:T(8,128)(2,1)}, bf16[2,256,1536]{2,1,0:T(8,128)(2,1)S(1)}, u32[]{:S(2)}, u32[]{:S(2)}) collective-permute-start(bf16[2,256,1536]{2,1,0:T(8,128)(2,1)} %bitcast.40), channel_id=1, source_target_pairs={{0,1},{1,0},{2,3},{3,2},{4,5},{5,4},{6,7},{7,6},{8,9},{9,8},{10,11... | collective-permute-start | bytes 4718600 | tf_op jit(solution)/shard_map/ppermute | solution.py:54
  838.0 35.5 %copy-start.21 = (bf16[2,256,1536]{2,1,0:T(8,128)(2,1)}, bf16[2,256,1536]{2,1,0:T(8,128)(2,1)S(1)}, u32[]{:S(2)}) copy-start(bf16[2,256,1536]{2,1,0:T(8,128)(2,1)S(1)} %fusion.10) | copy-start | bytes 4718596
  872.0 19.6 %collective-permute-start.22 = (bf16[256,1536]{1,0:T(8,128)(2,1)S(1)}, bf16[256,1536]{1,0:T(8,128)(2,1)}, u32[]{:S(2)}, u32[]{:S(2)}) collective-permute-start(bf16[256,1536]{1,0:T(8,128)(2,1)S(1)} %slice_bitcast_fusion.9), channel_id=1, source_target_pairs={{0,4},{2,6},{4,0},{6,2},{8,12},{10,14},{12,8},{14,10},{16,20},{18,... | collective-permute-start | bytes 2359304 | tf_op jit(solution)/shard_map/ppermute | solution.py:54
  873.6 19.4 %collective-permute-start.23 = (bf16[256,1536]{1,0:T(8,128)(2,1)S(1)}, bf16[256,1536]{1,0:T(8,128)(2,1)}, u32[]{:S(2)}, u32[]{:S(2)}) collective-permute-start(bf16[256,1536]{1,0:T(8,128)(2,1)S(1)} %slice_bitcast_fusion.8), channel_id=1, source_target_pairs={{0,1},{1,0},{2,3},{3,2},{4,5},{5,4},{6,7},{7,6},{8,9},{9,8},{10,11... | collective-permute-start | bytes 2359304 | tf_op jit(solution)/shard_map/ppermute | solution.py:54
  876.6 15.0 %copy-start.23 = (bf16[2,256,1536]{2,1,0:T(8,128)(2,1)S(1)}, bf16[2,256,1536]{2,1,0:T(8,128)(2,1)}, u32[]{:S(2)}) copy-start(bf16[2,256,1536]{2,1,0:T(8,128)(2,1)} %copy-done.22) | copy-start | bytes 4718596
  (38 other events, 195.1 us)
Sparse Core Ops, SparseCore 0:
  20.1 98.1 all-gather.5
  145.4 132.2 all-gather.3
  387.2 69.9 reduce-scatter.4
  472.9 128.3 reduce-scatter.2
